TPU v7x, 16 devices: a 4x2x1 block of a 4x4x8 slice. The times are simulated.
16 devices in a mesh: dp: 2 (over y, z), sp: 8 (over x, core).
Axes of the slice: x: 4, y: 2, z: 1, core: 2. Of those that a mesh axis runs over, the one named last changes fastest.
The devices are a block of a 4x4x8 slice.
Arguments:
- tok_in: bfloat16 [4096, 6144], P(('dp', 'sp')), parts along dimension 0
- tok_pos: int32 [4096], P(('dp', 'sp')), parts along dimension 0
- w_dq: bfloat16 [6144, 1536], replicated
- g_q: float32 [1536], replicated
- w_uq: bfloat16 [1536, 64, 192], replicated
- w_dkv: bfloat16 [6144, 576], replicated
- g_kv: float32 [512], replicated
- w_uk: bfloat16 [512, 64, 128], replicated
- w_uv: bfloat16 [512, 64, 128], replicated
- w_o: bfloat16 [64, 128, 6144], replicated
Outputs:
- output 1: bfloat16 [4096, 6144], P(('dp', 'sp')), parts along dimension 0
- output 2: bfloat16 [4096, 512], P(('dp', 'sp')), parts along dimension 0
- output 3: bfloat16 [4096, 64], P(('dp', 'sp')), parts along dimension 0
There are 2 independent parts. A program takes and returns all parts, laid end to end along the dimension named above; an argument that names none is the same for every part.
All inputs are finite; a program needn't handle non-finite values.
Results may differ from a plain program's by a relative error of at most 0.00605.
Values are sent between devices in bfloat16 or wider.
A program may use at most 768 MiB of HBM per device.

v0:
```python
import math
import jax
import jax.numpy as jnp
from jax import lax
from jax.sharding import PartitionSpec as P

ROPE_THETA = 10000.0
YARN_FACTOR = 40.0
ORIG_CTX = 4096.0
BETA_FAST = 32.0
BETA_SLOW = 1.0
NORM_EPS = 1e-6


def rope_freqs(rot_dim):
    half_dim = rot_dim // 2
    log_base = 2.0 * math.log(ROPE_THETA)
    low_idx = max(math.floor(rot_dim * math.log(ORIG_CTX / (BETA_FAST * 2.0 * math.pi)) / log_base), 0)
    high_idx = min(math.ceil(rot_dim * math.log(ORIG_CTX / (BETA_SLOW * 2.0 * math.pi)) / log_base), half_dim - 1)
    spread = max(high_idx - low_idx, 0.001)
    freq_list = []
    for freq_idx in range(half_dim):
        base_freq = ROPE_THETA ** (-2.0 * freq_idx / rot_dim)
        ramp_val = min(max((freq_idx - low_idx) / spread, 0.0), 1.0)
        freq_list.append(base_freq / YARN_FACTOR * ramp_val + base_freq * (1.0 - ramp_val))
    return jnp.asarray(freq_list, dtype=jnp.float32)


def rotate_half(act_in, cos_t, sin_t):
    half_dim = act_in.shape[-1] // 2
    first = act_in[..., :half_dim]
    second = act_in[..., half_dim:]
    return jnp.concatenate([first * cos_t - second * sin_t, second * cos_t + first * sin_t], axis=-1)


def rms_norm(act_in, gain):
    mean_sq = jnp.mean(act_in * act_in, axis=-1, keepdims=True)
    return act_in * lax.rsqrt(mean_sq + NORM_EPS) * gain


def solution(mesh):
    groups = mesh.shape['sp']
    tok_spec = P(('dp', 'sp'))
    rows_spec = P(('dp', 'sp'), None)
    replicated = P()

    def local_step(tok_in, tok_pos, w_dq, g_q, w_uq, w_dkv, g_kv, w_uk, w_uv, w_o):
        rows = tok_in.shape[0]
        num_heads = w_uq.shape[1]
        qk_dim = w_uq.shape[2]
        kv_rank = g_kv.shape[0]
        rot_dim = w_dkv.shape[1] - kv_rank
        nope_dim = qk_dim - rot_dim
        v_dim = w_uv.shape[2]
        seq_len = rows * groups
        attn_scale = (0.1 * math.log(YARN_FACTOR) + 1.0) ** 2 / math.sqrt(qk_dim)
        angles = tok_pos.astype(jnp.float32)[:, None] * rope_freqs(rot_dim)[None, :]
        cos_t = jnp.cos(angles)
        sin_t = jnp.sin(angles)
        q_lat = rms_norm(jnp.dot(tok_in, w_dq, preferred_element_type=jnp.float32), g_q).astype(jnp.bfloat16)
        q_full = jnp.einsum('tc,che->the', q_lat, w_uq, preferred_element_type=jnp.float32)
        q_all = jnp.concatenate([q_full[:, :, :nope_dim], rotate_half(q_full[:, :, nope_dim:], cos_t[:, None, :], sin_t[:, None, :])], axis=-1).astype(jnp.bfloat16)
        kv_lat = jnp.dot(tok_in, w_dkv, preferred_element_type=jnp.float32)
        cache_kv = rms_norm(kv_lat[:, :kv_rank], g_kv).astype(jnp.bfloat16)
        cache_pe = rotate_half(kv_lat[:, kv_rank:], cos_t, sin_t).astype(jnp.bfloat16)
        k_nope = jnp.einsum('tc,chn->thn', cache_kv, w_uk, preferred_element_type=jnp.float32).astype(jnp.bfloat16)
        values = jnp.einsum('tc,chv->thv', cache_kv, w_uv, preferred_element_type=jnp.float32).astype(jnp.bfloat16)
        k_all = jnp.concatenate([k_nope, jnp.broadcast_to(cache_pe[:, None, :], (rows, num_heads, rot_dim))], axis=-1)
        q_heads = lax.all_to_all(q_all, 'sp', 1, 0, tiled=True)
        k_heads = lax.all_to_all(k_all, 'sp', 1, 0, tiled=True)
        v_heads = lax.all_to_all(values, 'sp', 1, 0, tiled=True)
        key_idx = jnp.arange(seq_len)

        def block_attention(blk_idx):
            start = blk_idx * rows
            q_blk = lax.dynamic_slice_in_dim(q_heads, start, rows, axis=0)
            logits = jnp.einsum('qhe,khe->hqk', q_blk, k_heads, preferred_element_type=jnp.float32) * attn_scale
            row_idx = start + jnp.arange(rows)
            logits = jnp.where(key_idx[None, None, :] <= row_idx[None, :, None], logits, -jnp.inf)
            attn_prob = jax.nn.softmax(logits, axis=-1).astype(jnp.bfloat16)
            return jnp.einsum('hqk,khv->qhv', attn_prob, v_heads, preferred_element_type=jnp.float32).astype(jnp.bfloat16)

        o_heads = lax.map(block_attention, jnp.arange(groups)).reshape(seq_len, num_heads // groups, v_dim)
        o_local = lax.all_to_all(o_heads, 'sp', 0, 1, tiled=True)
        attn_out = jnp.einsum('thv,hvd->td', o_local, w_o, preferred_element_type=jnp.float32).astype(jnp.bfloat16)
        return attn_out, cache_kv, cache_pe

    return jax.shard_map(local_step, mesh=mesh, in_specs=(rows_spec, tok_spec, replicated, replicated, replicated, replicated, replicated, replicated, replicated, replicated), out_specs=(rows_spec, rows_spec, rows_spec), check_vma=False)
```

profile of v0, /device:TPU:119, one launch (start us, length us, event | category | flops | bytes accessed | tf_op | source)
XLA Modules:
  0.0 515.4 jit_solution(8037569711367536987)
XLA Ops:
  2.5 5.8 %fusion.40 = f32[256,576]{0,1:T(8,128)S(1)} fusion(bf16[256,6144]{1,0:T(8,128)(2,1)S(1)} %copy-done, bf16[6144,576]{0,1:T(8,128)(2,1)} %param.18), kind=kOutput, calls=%fused_computation.49 | convolution fusion | flops 1811939328 | bytes 10813440 | tf_op jit(solution)/shard_map/dot_general | solution.py:63
  9.3 8.1 %fusion.28 = bf16[256,64,128]{2,0,1:T(8,128)(2,1)} fusion(bf16[512,64,128]{2,1,0:T(8,128)(2,1)S(1)} %copy-done.9, bf16[256,512]{0,1:T(8,128)(2,1)S(1)} %multiply_convert_fusion.2), kind=kOutput, calls=%fused_computation.30 | convolution fusion | flops 2149580800 | bytes 12845056 | tf_op jit(solution)/shard_map/tc,chv->thv/dot_general | solution.py:67
  22.4 9.2 %multiply_reduce_fusion = (f32[256]{0:T(256)S(1)}, f32[256,1536]{1,0:T(8,128)S(1)}) fusion(bf16[256,6144]{1,0:T(8,128)(2,1)S(1)} %copy-done, bf16[6144,1536]{1,0:T(8,128)(2,1)} %param.15), kind=kOutput, calls=%fused_computation.34 | convolution fusion | flops 4832624640 | bytes 23593984 | tf_op jit(solution)/shard_map/dot_general | solution.py:60
  31.7 20.9 %fusion.31 = f32[256,12288]{0,1} fusion(bf16[1536,12288]{0,1:T(8,128)(2,1)} %bitcast.64, f32[256,1536]{1,0:T(8,128)S(1)} %get-tuple-element.82, f32[1536]{0:T(1024)S(1)} %copy-done.10, f32[256]{0:T(256)S(1)} %add_rsqrt_fusion.1), kind=kOutput, calls=%fused_computation.35 | convolution fusion | flops 9664856064 | bytes 51911680
  60.5 5.7 %pad_maximum_fusion = bf16[256,64,192]{0,2,1:T(8,128)(2,1)} fusion(bf16[256,64,32]{0,2,1:T(8,128)(2,1)S(1)} %get-tuple-element.76, bf16[256,64,32]{0,2,1:T(8,128)(2,1)S(1)} %get-tuple-element.75, bf16[256,64,128]{0,2,1:T(8,128)(2,1)S(1)} %slice.48), kind=kLoop, calls=%fused_computation.28 | loop fusion | flops 18874368 | bytes 12582912 | tf_op jit(solution)/shard_map/concatenate | solution.py:62
  69.3 7.5 %all-to-all-start = ((bf16[256,64,192]{0,2,1:T(8,128)(2,1)}), bf16[256,64,192]{0,2,1:T(8,128)(2,1)}, u32[]{:S(2)}, u32[]{:S(2)}) async-start(bf16[256,64,192]{0,2,1:T(8,128)(2,1)} %pad_maximum_fusion), calls=%async_computation | async-start | bytes 12582912 | tf_op jit(solution)/shard_map/all_to_all | solution.py:69
  76.9 12.9 %copy.24 = bf16[512,64,128]{0,2,1:T(8,128)(2,1)} copy(bf16[512,64,128]{2,1,0:T(8,128)(2,1)} %param.20) | data formatting | bytes 16777216 | tf_op args[7]
  99.7 46.4 %all-to-all-done = bf16[256,64,192]{0,2,1:T(8,128)(2,1)} async-done(((bf16[256,64,192]{0,2,1:T(8,128)(2,1)}), bf16[256,64,192]{0,2,1:T(8,128)(2,1)}, u32[]{:S(2)}, u32[]{:S(2)}) %all-to-all-start) | async-done | bytes 6291488 | tf_op jit(solution)/shard_map/all_to_all | solution.py:69
  146.2 7.5 %all-to-all-start.1 = ((bf16[256,64,192]{0,2,1:T(8,128)(2,1)}), bf16[256,64,192]{0,2,1:T(8,128)(2,1)}, u32[]{:S(2)}, u32[]{:S(2)}) async-start(bf16[256,64,192]{0,2,1:T(8,128)(2,1)} %pad_maximum_fusion.1), calls=%async_computation.1 | async-start | bytes 12582912 | tf_op jit(solution)/shard_map/all_to_all | solution.py:70
  158.4 6.4 %copy.37 = bf16[8,8,24,8,256]{4,3,0,2,1:T(8,128)(2,1)} copy(bf16[8,8,24,8,256]{4,3,2,1,0:T(8,128)(2,1)} %bitcast.25) | data formatting | bytes 12582912 | tf_op jit(solution)/shard_map/all_to_all | solution.py:69
  164.7 58.3 %all-to-all-done.1 = bf16[256,64,192]{0,2,1:T(8,128)(2,1)} async-done(((bf16[256,64,192]{0,2,1:T(8,128)(2,1)}), bf16[256,64,192]{0,2,1:T(8,128)(2,1)}, u32[]{:S(2)}, u32[]{:S(2)}) %all-to-all-start.1) | async-done | bytes 6291488 | tf_op jit(solution)/shard_map/all_to_all | solution.py:70
  223.0 6.2 %copy.38 = bf16[8,8,24,8,256]{4,3,0,2,1:T(8,128)(2,1)} copy(bf16[8,8,24,8,256]{4,3,2,1,0:T(8,128)(2,1)} %bitcast.27) | data formatting | bytes 12582912 | tf_op jit(solution)/shard_map/all_to_all | solution.py:70
  229.3 190.1 %while.11 = (s32[]{:T(128)}, bf16[8,256,8,128]{3,2,1,0:T(8,128)(2,1)}, s32[8]{0:T(128)S(1)}, bf16[2048,8,192]{0,2,1:T(8,128)(2,1)}, bf16[2048,8,192]{0,2,1:T(8,1...) while((s32[]{:T(128)}, ...), condition=%wide.region_5.6_spmd.clone, body=%wide.region_2.5_spmd.clone.sunk | while | flops 2710309120 | bytes 47467176 | solution.py:83
  231.0 11.5 %fusion.62 = (f32[8,256]{1,0:T(8,128)S(1)}, f32[8,256,2048]{2,1,0:T(8,128)}) fusion(pred[256,2048]{1,0:T(8,128)(4,1)S(1)} %iota_compare_fusion.2, bf16[2048,8,192]{0,2,1:T(8,128)(2,1)} %get-tuple-element.148, bf16[2048,8,192]{0,2,1:T(8,128)(2,1)} %get-tuple-element.147, s32[]{:T(128)S(6)} %select_n.22), kind=kOutput, calls=%fused_computation.48.clone.1 | convolution fusion | flops 1627392000 | bytes 24387588 | tf_op jit(solution)/shard_map/while/body/eval_jaxpr/sub | solution.py:80
  242.5 9.4 %fusion.63 = bf16[1,256,8,128]{3,1,2,0:T(8,128)(2,1)S(1)} fusion(bf16[2048,8,128]{2,0,1:T(8,128)(2,1)} %get-tuple-element.149, f32[8,256,2048]{2,1,0:T(8,128)} %get-tuple-element.122, f32[8,256]{1,0:T(8,128)S(1)} %get-tuple-element.123), kind=kOutput, calls=%fused_computation.12.clone.1 | convolution fusion | flops 1082392576 | bytes 21504000 | tf_op jit(solution)/shard_map/while/body/eval_jaxpr/hqk,khv->qhv/dot_general | solution.py:81
  254.7 11.5 %fusion.62 = (f32[8,256]{1,0:T(8,128)S(1)}, f32[8,256,2048]{2,1,0:T(8,128)}) fusion(pred[256,2048]{1,0:T(8,128)(4,1)S(1)} %iota_compare_fusion.2, bf16[2048,8,192]{0,2,1:T(8,128)(2,1)} %get-tuple-element.148, bf16[2048,8,192]{0,2,1:T(8,128)(2,1)} %get-tuple-element.147, s32[]{:T(128)S(6)} %select_n.22), kind=kOutput, calls=%fused_computation.48.clone.1 | convolution fusion | flops 1627392000 | bytes 24387588 | tf_op jit(solution)/shard_map/while/body/eval_jaxpr/sub | solution.py:80
  266.3 9.4 %fusion.63 = bf16[1,256,8,128]{3,1,2,0:T(8,128)(2,1)S(1)} fusion(bf16[2048,8,128]{2,0,1:T(8,128)(2,1)} %get-tuple-element.149, f32[8,256,2048]{2,1,0:T(8,128)} %get-tuple-element.122, f32[8,256]{1,0:T(8,128)S(1)} %get-tuple-element.123), kind=kOutput, calls=%fused_computation.12.clone.1 | convolution fusion | flops 1082392576 | bytes 21504000 | tf_op jit(solution)/shard_map/while/body/eval_jaxpr/hqk,khv->qhv/dot_general | solution.py:81
  278.5 11.5 %fusion.62 = (f32[8,256]{1,0:T(8,128)S(1)}, f32[8,256,2048]{2,1,0:T(8,128)}) fusion(pred[256,2048]{1,0:T(8,128)(4,1)S(1)} %iota_compare_fusion.2, bf16[2048,8,192]{0,2,1:T(8,128)(2,1)} %get-tuple-element.148, bf16[2048,8,192]{0,2,1:T(8,128)(2,1)} %get-tuple-element.147, s32[]{:T(128)S(6)} %select_n.22), kind=kOutput, calls=%fused_computation.48.clone.1 | convolution fusion | flops 1627392000 | bytes 24387588 | tf_op jit(solution)/shard_map/while/body/eval_jaxpr/sub | solution.py:80
  290.0 9.4 %fusion.63 = bf16[1,256,8,128]{3,1,2,0:T(8,128)(2,1)S(1)} fusion(bf16[2048,8,128]{2,0,1:T(8,128)(2,1)} %get-tuple-element.149, f32[8,256,2048]{2,1,0:T(8,128)} %get-tuple-element.122, f32[8,256]{1,0:T(8,128)S(1)} %get-tuple-element.123), kind=kOutput, calls=%fused_computation.12.clone.1 | convolution fusion | flops 1082392576 | bytes 21504000 | tf_op jit(solution)/shard_map/while/body/eval_jaxpr/hqk,khv->qhv/dot_general | solution.py:81
  302.2 11.5 %fusion.62 = (f32[8,256]{1,0:T(8,128)S(1)}, f32[8,256,2048]{2,1,0:T(8,128)}) fusion(pred[256,2048]{1,0:T(8,128)(4,1)S(1)} %iota_compare_fusion.2, bf16[2048,8,192]{0,2,1:T(8,128)(2,1)} %get-tuple-element.148, bf16[2048,8,192]{0,2,1:T(8,128)(2,1)} %get-tuple-element.147, s32[]{:T(128)S(6)} %select_n.22), kind=kOutput, calls=%fused_computation.48.clone.1 | convolution fusion | flops 1627392000 | bytes 24387588 | tf_op jit(solution)/shard_map/while/body/eval_jaxpr/sub | solution.py:80
  313.8 9.4 %fusion.63 = bf16[1,256,8,128]{3,1,2,0:T(8,128)(2,1)S(1)} fusion(bf16[2048,8,128]{2,0,1:T(8,128)(2,1)} %get-tuple-element.149, f32[8,256,2048]{2,1,0:T(8,128)} %get-tuple-element.122, f32[8,256]{1,0:T(8,128)S(1)} %get-tuple-element.123), kind=kOutput, calls=%fused_computation.12.clone.1 | convolution fusion | flops 1082392576 | bytes 21504000 | tf_op jit(solution)/shard_map/while/body/eval_jaxpr/hqk,khv->qhv/dot_general | solution.py:81
  326.0 11.5 %fusion.62 = (f32[8,256]{1,0:T(8,128)S(1)}, f32[8,256,2048]{2,1,0:T(8,128)}) fusion(pred[256,2048]{1,0:T(8,128)(4,1)S(1)} %iota_compare_fusion.2, bf16[2048,8,192]{0,2,1:T(8,128)(2,1)} %get-tuple-element.148, bf16[2048,8,192]{0,2,1:T(8,128)(2,1)} %get-tuple-element.147, s32[]{:T(128)S(6)} %select_n.22), kind=kOutput, calls=%fused_computation.48.clone.1 | convolution fusion | flops 1627392000 | bytes 24387588 | tf_op jit(solution)/shard_map/while/body/eval_jaxpr/sub | solution.py:80
  337.5 9.4 %fusion.63 = bf16[1,256,8,128]{3,1,2,0:T(8,128)(2,1)S(1)} fusion(bf16[2048,8,128]{2,0,1:T(8,128)(2,1)} %get-tuple-element.149, f32[8,256,2048]{2,1,0:T(8,128)} %get-tuple-element.122, f32[8,256]{1,0:T(8,128)S(1)} %get-tuple-element.123), kind=kOutput, calls=%fused_computation.12.clone.1 | convolution fusion | flops 1082392576 | bytes 21504000 | tf_op jit(solution)/shard_map/while/body/eval_jaxpr/hqk,khv->qhv/dot_general | solution.py:81
  349.8 11.5 %fusion.62 = (f32[8,256]{1,0:T(8,128)S(1)}, f32[8,256,2048]{2,1,0:T(8,128)}) fusion(pred[256,2048]{1,0:T(8,128)(4,1)S(1)} %iota_compare_fusion.2, bf16[2048,8,192]{0,2,1:T(8,128)(2,1)} %get-tuple-element.148, bf16[2048,8,192]{0,2,1:T(8,128)(2,1)} %get-tuple-element.147, s32[]{:T(128)S(6)} %select_n.22), kind=kOutput, calls=%fused_computation.48.clone.1 | convolution fusion | flops 1627392000 | bytes 24387588 | tf_op jit(solution)/shard_map/while/body/eval_jaxpr/sub | solution.py:80
  361.3 9.4 %fusion.63 = bf16[1,256,8,128]{3,1,2,0:T(8,128)(2,1)S(1)} fusion(bf16[2048,8,128]{2,0,1:T(8,128)(2,1)} %get-tuple-element.149, f32[8,256,2048]{2,1,0:T(8,128)} %get-tuple-element.122, f32[8,256]{1,0:T(8,128)S(1)} %get-tuple-element.123), kind=kOutput, calls=%fused_computation.12.clone.1 | convolution fusion | flops 1082392576 | bytes 21504000 | tf_op jit(solution)/shard_map/while/body/eval_jaxpr/hqk,khv->qhv/dot_general | solution.py:81
  373.6 11.5 %fusion.62 = (f32[8,256]{1,0:T(8,128)S(1)}, f32[8,256,2048]{2,1,0:T(8,128)}) fusion(pred[256,2048]{1,0:T(8,128)(4,1)S(1)} %iota_compare_fusion.2, bf16[2048,8,192]{0,2,1:T(8,128)(2,1)} %get-tuple-element.148, bf16[2048,8,192]{0,2,1:T(8,128)(2,1)} %get-tuple-element.147, s32[]{:T(128)S(6)} %select_n.22), kind=kOutput, calls=%fused_computation.48.clone.1 | convolution fusion | flops 1627392000 | bytes 24387588 | tf_op jit(solution)/shard_map/while/body/eval_jaxpr/sub | solution.py:80
  385.1 9.4 %fusion.63 = bf16[1,256,8,128]{3,1,2,0:T(8,128)(2,1)S(1)} fusion(bf16[2048,8,128]{2,0,1:T(8,128)(2,1)} %get-tuple-element.149, f32[8,256,2048]{2,1,0:T(8,128)} %get-tuple-element.122, f32[8,256]{1,0:T(8,128)S(1)} %get-tuple-element.123), kind=kOutput, calls=%fused_computation.12.clone.1 | convolution fusion | flops 1082392576 | bytes 21504000 | tf_op jit(solution)/shard_map/while/body/eval_jaxpr/hqk,khv->qhv/dot_general | solution.py:81
  397.4 11.5 %fusion.62 = (f32[8,256]{1,0:T(8,128)S(1)}, f32[8,256,2048]{2,1,0:T(8,128)}) fusion(pred[256,2048]{1,0:T(8,128)(4,1)S(1)} %iota_compare_fusion.2, bf16[2048,8,192]{0,2,1:T(8,128)(2,1)} %get-tuple-element.148, bf16[2048,8,192]{0,2,1:T(8,128)(2,1)} %get-tuple-element.147, s32[]{:T(128)S(6)} %select_n.22), kind=kOutput, calls=%fused_computation.48.clone.1 | convolution fusion | flops 1627392000 | bytes 24387588 | tf_op jit(solution)/shard_map/while/body/eval_jaxpr/sub | solution.py:80
  408.9 9.4 %fusion.63 = bf16[1,256,8,128]{3,1,2,0:T(8,128)(2,1)S(1)} fusion(bf16[2048,8,128]{2,0,1:T(8,128)(2,1)} %get-tuple-element.149, f32[8,256,2048]{2,1,0:T(8,128)} %get-tuple-element.122, f32[8,256]{1,0:T(8,128)S(1)} %get-tuple-element.123), kind=kOutput, calls=%fused_computation.12.clone.1 | convolution fusion | flops 1082392576 | bytes 21504000 | tf_op jit(solution)/shard_map/while/body/eval_jaxpr/hqk,khv->qhv/dot_general | solution.py:81
  419.4 7.5 %all-to-all-start.3 = ((bf16[2048,8,128]{2,1,0:T(8,128)(2,1)}), bf16[2048,8,128]{2,1,0:T(8,128)(2,1)}, u32[]{:S(2)}, u32[]{:S(2)}) async-start(bf16[2048,8,128]{2,1,0:T(8,128)(2,1)} %bitcast.62), calls=%async_computation.3 | async-start | bytes 8388608 | tf_op jit(solution)/shard_map/all_to_all | solution.py:84
  427.7 46.0 %all-to-all-done.3 = bf16[2048,8,128]{2,1,0:T(8,128)(2,1)} async-done(((bf16[2048,8,128]{2,1,0:T(8,128)(2,1)}), bf16[2048,8,128]{2,1,0:T(8,128)(2,1)}, u32[]{:S(2)}, u32[]{:S(2)}) %all-to-all-start.3) | async-done | bytes 4194336 | tf_op jit(solution)/shard_map/all_to_all | solution.py:84
  477.1 38.3 %fusion.27 = bf16[256,6144]{1,0:T(8,128)(2,1)} fusion(bf16[256,64,128]{2,0,1:T(8,128)(2,1)S(1)} %bitcast.63, bf16[64,128,6144]{2,1,0:T(8,128)(2,1)} %param.22), kind=kOutput, calls=%fused_computation.27 | convolution fusion | flops 25771376640 | bytes 108003328 | tf_op jit(solution)/shard_map/thv,hvd->td/dot_general | solution.py:85
  (74 shorter events, 54.9 us)
Async XLA Ops:
  0.6 1.9 copy-start
  0.6 8.5 %copy-start.6 = (f32[512]{0:T(512)S(1)}, f32[512]{0:T(512)}, u32[]{:S(2)}) copy-start(f32[512]{0:T(512)} %param.19) | copy-start | bytes 6148
  0.7 8.6 %copy-start.9 = (bf16[512,64,128]{2,1,0:T(8,128)(2,1)S(1)}, bf16[512,64,128]{2,1,0:T(8,128)(2,1)}, u32[]{:S(2)}) copy-start(bf16[512,64,128]{2,1,0:T(8,128)(2,1)} %param.21) | copy-start | bytes 25165828
  8.3 0.8 copy-start.4
  9.3 80.5 %copy-start.2 = (bf16[256,512]{0,1:T(8,128)(2,1)}, bf16[256,512]{0,1:T(8,128)(2,1)S(1)}, u32[]{:S(2)}) copy-start(bf16[256,512]{0,1:T(8,128)(2,1)S(1)} %multiply_convert_fusion.2) | copy-start | bytes 786436
  17.4 5.0 copy-start.7
  17.4 51.9 %all-to-all-start.2 = ((bf16[256,64,128]{2,0,1:T(8,128)(2,1)}), bf16[256,64,128]{2,0,1:T(8,128)(2,1)}, u32[]{:S(2)}, u32[]{:S(2)}) async-start(bf16[256,64,128]{2,0,1:T(8,128)(2,1)} %fusion.28), calls=%async_computation.2 | async-start | bytes 8388608 | tf_op jit(solution)/shard_map/all_to_all | solution.py:71
  22.4 9.2 %copy-start.10 = (f32[1536]{0:T(1024)S(1)}, f32[1536]{0:T(1024)}, u32[]{:S(2)}) copy-start(f32[1536]{0:T(1024)} %param.16) | copy-start | bytes 18436
  52.6 4.0 copy-start.8
  69.3 76.8 %all-to-all-start = ((bf16[256,64,192]{0,2,1:T(8,128)(2,1)}), bf16[256,64,192]{0,2,1:T(8,128)(2,1)}, u32[]{:S(2)}, u32[]{:S(2)}) async-start(bf16[256,64,192]{0,2,1:T(8,128)(2,1)} %pad_maximum_fusion), calls=%async_computation | async-start | bytes 12582912 | tf_op jit(solution)/shard_map/all_to_all | solution.py:69
  96.1 3.6 copy-start.5
  146.2 76.9 %all-to-all-start.1 = ((bf16[256,64,192]{0,2,1:T(8,128)(2,1)}), bf16[256,64,192]{0,2,1:T(8,128)(2,1)}, u32[]{:S(2)}, u32[]{:S(2)}) async-start(bf16[256,64,192]{0,2,1:T(8,128)(2,1)} %pad_maximum_fusion.1), calls=%async_computation.1 | async-start | bytes 12582912 | tf_op jit(solution)/shard_map/all_to_all | solution.py:70
  419.4 7.5 %copy-start.3 = (bf16[256,512]{0,1:T(8,128)(2,1)S(1)}, bf16[256,512]{0,1:T(8,128)(2,1)}, u32[]{:S(2)}) copy-start(bf16[256,512]{0,1:T(8,128)(2,1)} %copy-done.2) | copy-start | bytes 786436
  419.4 54.3 %all-to-all-start.3 = ((bf16[2048,8,128]{2,1,0:T(8,128)(2,1)}), bf16[2048,8,128]{2,1,0:T(8,128)(2,1)}, u32[]{:S(2)}, u32[]{:S(2)}) async-start(bf16[2048,8,128]{2,1,0:T(8,128)(2,1)} %bitcast.62), calls=%async_computation.3 | async-start | bytes 8388608 | tf_op jit(solution)/shard_map/all_to_all | solution.py:84
  477.1 38.3 %copy-start.1 = (bf16[256,6144]{1,0:T(8,128)(2,1)S(1)}, bf16[256,6144]{1,0:T(8,128)(2,1)}, u32[]{:S(2)}) copy-start(bf16[256,6144]{1,0:T(8,128)(2,1)} %param.13) | copy-start | bytes 9437188
where the time goes:
time: 520 us; the launch traced here: 515 us
  matrix products  255 us (49%)
  waiting for transfers between devices  154 us (30%)
  local copies, waits for them, and re-layouts  55.6 us (11%)
  starting transfers between devices  27.6 us (5%)
  other arithmetic  16.7 us (3%)
  loops' own time  5.61 us (1%)
    sub x8, matrix products, block_attention(): attn_prob = jax.nn.softmax(logits, axis=-1).astype(jnp.bfloat16)  92.3 us
    dot_general x8, matrix products, block_attention(): jnp.einsum('hqk,khv->qhv', attn_prob, v_heads, preferred_element_type=jnp...  75 us
    all_to_all x1, waiting for transfers between devices, local_step(): k_heads = lax.all_to_all(k_all, 'sp', 1, 0, tiled=True)  58.3 us
    all_to_all x1, waiting for transfers between devices, local_step(): q_heads = lax.all_to_all(q_all, 'sp', 1, 0, tiled=True)  46.4 us
    all_to_all x1, waiting for transfers between devices, local_step(): o_local = lax.all_to_all(o_heads, 'sp', 0, 1, tiled=True)  46 us
    dot_general x1, matrix products, local_step(): jnp.einsum('thv,hvd->td', o_local, w_o, preferred_element_type=jnp.float32)  38.3 us
    unnamed x2, matrix products  26.6 us
    unnamed x24, local copies, waits for them, and re-layouts  16.4 us
  transfers between devices with their start and end apart: 4, of which 4 were waited for; matrix products, arithmetic and copies ran while one was open for 15% of the time, Pallas kernels for 0%

commit v1 on v0

v1 whole, which is shorter than its diff:
```python
import functools
import math

import jax
import jax.numpy as jnp
from jax import lax
from jax.experimental import pallas as pl
from jax.experimental.pallas import tpu as pltpu
from jax.sharding import PartitionSpec as P

ROPE_THETA = 10000.0
YARN_FACTOR = 40.0
ORIG_CTX = 4096.0
BETA_FAST = 32.0
BETA_SLOW = 1.0
NORM_EPS = 1e-6

MESH = pl.DeviceIdType.MESH
F32 = jnp.float32
BF16 = jnp.bfloat16
NT = (((1,), (1,)), ((), ()))
TT = (((0,), (1,)), ((), ()))


def rope_freqs(rot_dim):
    half_dim = rot_dim // 2
    log_base = 2.0 * math.log(ROPE_THETA)
    low_idx = max(math.floor(rot_dim * math.log(ORIG_CTX / (BETA_FAST * 2.0 * math.pi)) / log_base), 0)
    high_idx = min(math.ceil(rot_dim * math.log(ORIG_CTX / (BETA_SLOW * 2.0 * math.pi)) / log_base), half_dim - 1)
    spread = max(high_idx - low_idx, 0.001)
    freq_list = []
    for freq_idx in range(half_dim):
        base_freq = ROPE_THETA ** (-2.0 * freq_idx / rot_dim)
        ramp_val = min(max((freq_idx - low_idx) / spread, 0.0), 1.0)
        freq_list.append(base_freq / YARN_FACTOR * ramp_val + base_freq * (1.0 - ramp_val))
    return jnp.asarray(freq_list, dtype=jnp.float32)


def front_kernel(ranks, x_hbm, wkv_hbm, wq_hbm, gq_ref, gkv_ref, tab_ref,
                 kv_all, pe_all, cq_all, tab_all, ckv_out, cpe_out,
                 x_v, wkv_v, wq_v, cq_f, kv_v, pe_v, cq_v,
                 w_sem, own_sem, kv_send, kv_recv, pe_send, pe_recv, cq_send, cq_recv, tab_send, tab_recv):
    me = lax.axis_index("sp")
    core = lax.rem(me, 2)
    sib = me + 1 - 2 * core
    chips = ranks // 2
    rows = x_v.shape[0]
    kv_rank = kv_v.shape[1]
    half = (wkv_v.shape[1] - kv_rank) // 2
    far = [lax.rem(me + 2 * d, ranks) for d in range(1, chips)]

    kchunks, nq = wkv_v.shape[0], wq_v.shape[0]
    kc = wkv_v.shape[2]
    nc = wq_v.shape[2]
    x_copy = pltpu.make_async_copy(x_hbm, x_v, w_sem.at[0])
    wkv_copies = [pltpu.make_async_copy(wkv_hbm.at[:, pl.ds(k * kc, kc)], wkv_v.at[k], w_sem.at[1 + k]) for k in range(kchunks)]
    wq_copies = [pltpu.make_async_copy(wq_hbm.at[:, pl.ds(k * nc, nc)], wq_v.at[k], w_sem.at[1 + kchunks + k]) for k in range(nq)]
    x_copy.start()
    for c in wkv_copies + wq_copies:
        c.start()

    barrier = pltpu.get_barrier_semaphore()
    for peer in [sib] + far:
        pl.semaphore_signal(barrier, inc=1, device_id={"sp": peer}, device_id_type=MESH)
    pl.semaphore_wait(barrier, chips)

    def block(ref, idx):
        return ref.at[pl.ds(idx * rows, rows)]

    def remote(src, ref, idx, send, recv, dev):
        return pltpu.make_async_remote_copy(src_ref=src, dst_ref=block(ref, idx), send_sem=send, recv_sem=recv,
                                            device_id={"sp": dev}, device_id_type=MESH)

    tab_copy = remote(tab_ref, tab_all, core, tab_send.at[0], tab_recv.at[0], sib)
    tab_copy.start()
    tab_own = pltpu.make_async_copy(tab_ref, block(tab_all, core), own_sem.at[0])
    tab_own.start()

    x_copy.wait()
    acc = None
    for k in range(kchunks):
        wkv_copies[k].wait()
        part = lax.dot_general(x_v[:, k * kc:(k + 1) * kc], wkv_v[k], NT, preferred_element_type=F32)
        acc = part if acc is None else acc + part
    a = acc[:, :kv_rank]
    inv = lax.rsqrt(jnp.mean(a * a, axis=-1, keepdims=True) + NORM_EPS)
    kv_v[...] = (a * inv * gkv_ref[...]).astype(BF16)
    z1 = acc[:, kv_rank:kv_rank + half]
    z2 = acc[:, kv_rank + half:]
    cos_t = tab_ref[:, :half]
    sin_t = tab_ref[:, half:2 * half]
    pe = jnp.concatenate([z1 * cos_t - z2 * sin_t, z2 * cos_t + z1 * sin_t], axis=-1).astype(BF16)
    pe_v[...] = jnp.zeros_like(pe_v)
    pe_v[:, :2 * half] = pe
    ckv_out[...] = kv_v[...]
    cpe_out[...] = pe

    sends = []
    for n, dev in enumerate([sib] + far):
        slot = 0 if n == 0 else n
        c1 = remote(kv_v, kv_all, me, kv_send.at[n], kv_recv.at[slot], dev)
        c2 = remote(pe_v, pe_all, me, pe_send.at[n], pe_recv.at[slot], dev)
        c1.start()
        c2.start()
        sends += [c1, c2]
    own = [pltpu.make_async_copy(kv_v, block(kv_all, me), own_sem.at[1]),
           pltpu.make_async_copy(pe_v, block(pe_all, me), own_sem.at[2])]
    for c in own:
        c.start()

    ssq = jnp.zeros((rows, 1), F32)
    for k in range(nq):
        wq_copies[k].wait()
        q = jnp.dot(x_v[...], wq_v[k], preferred_element_type=F32)
        cq_f[:, k * nc:(k + 1) * nc] = q
        ssq = ssq + jnp.sum(q * q, axis=-1, keepdims=True)
    inv_q = lax.rsqrt(ssq / cq_f.shape[1] + NORM_EPS)
    cq_v[...] = (cq_f[...] * inv_q * gq_ref[...]).astype(BF16)
    cq_copy = remote(cq_v, cq_all, core, cq_send.at[0], cq_recv.at[0], sib)
    cq_copy.start()
    cq_own = pltpu.make_async_copy(cq_v, block(cq_all, core), own_sem.at[3])
    cq_own.start()

    fwd = []
    for n in range(1, chips):
        src = lax.rem(me + ranks - 2 * n, ranks)
        g1 = remote(block(kv_all, src), kv_all, src, kv_send.at[chips + n - 1], kv_recv.at[chips + n - 1], sib)
        g2 = remote(block(pe_all, src), pe_all, src, pe_send.at[chips + n - 1], pe_recv.at[chips + n - 1], sib)
        sends[2 * n].wait_recv()
        g1.start()
        sends[2 * n + 1].wait_recv()
        g2.start()
        fwd += [g1, g2]
    sends[0].wait_recv()
    sends[1].wait_recv()
    for c in sends:
        c.wait_send()
    for c in fwd:
        c.wait()
    tab_copy.wait()
    cq_copy.wait()
    tab_own.wait()
    cq_own.wait()
    for c in own:
        c.wait()


def attn_kernel(scale2, heads, idx_ref, cq_ref, kv_ref, pe_ref, cosq_ref, sinq_ref,
                wqa_ref, wqb_ref, wka_ref, wkb_ref, wva_ref, wvb_ref, oa_ref, ob_ref,
                k_a, k_b, v_a, v_b, v_p, q_a, q_b, s_a, s_b, m_a, m_b, l_ref, o_ref):
    step = pl.program_id(0)
    full = idx_ref[0]
    blk = k_a.shape[1]
    nope = wka_ref.shape[1]
    half = cosq_ref.shape[0]
    rot = 2 * half
    sub = blk // 2

    @pl.when(step == 0)
    def _():
        for kb in range(k_a.shape[0]):
            pe = pe_ref[kb * blk:(kb + 1) * blk, :]
            k_a[kb, :, nope:] = pe
            k_b[kb, :, nope:] = pe
        q_a[nope + rot:, :] = jnp.zeros((q_a.shape[0] - nope - rot, q_a.shape[1]), BF16)
        q_b[nope + rot:, :] = jnp.zeros((q_b.shape[0] - nope - rot, q_b.shape[1]), BF16)
        v_p[...] = jnp.zeros_like(v_p)
        s_b[...] = jnp.zeros_like(s_b)
        m_b[...] = jnp.zeros_like(m_b)

    def q_proj(w_ref, q_ref):
        u = lax.dot_general(w_ref[0], cq_ref[...], NT, preferred_element_type=F32)
        q_ref[:nope, :] = u[:nope].astype(BF16)
        z1 = u[nope:nope + half]
        z2 = u[nope + half:]
        q_ref[nope:nope + half, :] = (z1 * cosq_ref[...] - z2 * sinq_ref[...]).astype(BF16)
        q_ref[nope + half:nope + rot, :] = (z2 * cosq_ref[...] + z1 * sinq_ref[...]).astype(BF16)

    def kv_proj(kb, wk, wv):
        c = kv_ref[pl.ds(pl.multiple_of(kb * blk, blk), blk), :]
        k = jnp.dot(c, wk, preferred_element_type=F32).astype(BF16)
        k_a[kb, :, :nope] = k[:, :nope]
        k_b[kb, :, :nope] = k[:, nope:]
        v = lax.dot_general(wv, c, NT, preferred_element_type=F32).astype(BF16)
        v_a[kb] = v[:nope]
        v_b[kb] = v[nope:]

    def fold_max(m_ref, s, cols):
        t = jnp.max(s.reshape(s.shape[0] // 8, 8, s.shape[1]), axis=0)
        m_ref[:, cols] = jnp.maximum(m_ref[:, cols], t)

    everything = slice(None)

    def qk(kb, k_ref, q_ref, s_ref, m_ref):
        s = jnp.dot(k_ref[kb], q_ref[...], preferred_element_type=F32)
        s_ref[kb] = s
        fold_max(m_ref, s, everything)

    def qk_diag(kb, k_ref, q_ref, s_ref, m_ref):
        s0 = jnp.dot(k_ref[kb, :sub, :], q_ref[...], preferred_element_type=F32)
        s1 = jnp.dot(k_ref[kb, sub:, :], q_ref[:, sub:], preferred_element_type=F32)
        keep = lax.broadcasted_iota(jnp.int32, (sub, sub), 0) <= lax.broadcasted_iota(jnp.int32, (sub, sub), 1)
        s00 = jnp.where(keep, s0[:, :sub], -jnp.inf)
        s1 = jnp.where(keep, s1, -jnp.inf)
        s01 = s0[:, sub:]
        s_ref[kb, :sub, :sub] = s00
        s_ref[kb, :sub, sub:] = s01
        s_ref[kb, sub:, sub:] = s1
        fold_max(m_ref, s00, slice(0, sub))
        fold_max(m_ref, s01, slice(sub, blk))
        fold_max(m_ref, s1, slice(sub, blk))

    def fold_sum(p, cols):
        l_ref[:, cols] += jnp.sum(p.reshape(p.shape[0] // 8, 8, p.shape[1]), axis=0)

    def top(m_ref):
        return jnp.max(m_ref[...], axis=0, keepdims=True)

    def pv(kb, v_ref, s_ref, m):
        p = jnp.exp2((s_ref[kb] - m) * scale2)
        fold_sum(p, everything)
        o_ref[...] += jnp.dot(v_ref[kb], p.astype(BF16), preferred_element_type=F32)

    def pv_diag(kb, v_ref, s_ref, m):
        p0 = jnp.exp2((s_ref[kb, :sub, :] - m) * scale2)
        p1 = jnp.exp2((s_ref[kb, sub:, sub:] - m[:, sub:]) * scale2)
        fold_sum(p0, everything)
        fold_sum(p1, slice(sub, blk))
        p0 = p0.astype(BF16)
        o_ref[...] += jnp.dot(v_ref[kb, :, :sub], p0, preferred_element_type=F32)
        o_ref[:, sub:] += jnp.dot(v_ref[kb, :, sub:], p1.astype(BF16), preferred_element_type=F32)

    def finish(out_ref):
        l = jnp.sum(l_ref[...], axis=0, keepdims=True)
        out_ref[...] = (o_ref[...] / l).T.astype(BF16)

    def clear():
        l_ref[...] = jnp.zeros_like(l_ref)
        o_ref[...] = jnp.zeros_like(o_ref)

    @pl.when(step < heads)
    def _():
        q_proj(wqa_ref, q_a)
        q_proj(wqb_ref, q_b)
        wk = jnp.concatenate([wka_ref[...], wkb_ref[...]], axis=1)
        wv = jnp.concatenate([wva_ref[...].T, wvb_ref[...].T], axis=0)
        m = top(m_b)
        clear()
        m_a[...] = jnp.full_like(m_a, -jnp.inf)

        def body1(kb, _):
            kv_proj(kb, wk, wv)
            qk(kb, k_a, q_a, s_a, m_a)
            pv(kb, v_p, s_b, m)
            return _

        lax.fori_loop(0, full, body1, 0)
        kv_proj(full, wk, wv)
        qk_diag(full, k_a, q_a, s_a, m_a)
        pv_diag(full, v_p, s_b, m)
        finish(ob_ref)
        m2 = top(m_a)
        clear()
        m_b[...] = jnp.full_like(m_b, -jnp.inf)

        def body2(kb, _):
            qk(kb, k_b, q_b, s_b, m_b)
            pv(kb, v_a, s_a, m2)
            v_p[kb] = v_b[kb]
            return _

        lax.fori_loop(0, full, body2, 0)
        qk_diag(full, k_b, q_b, s_b, m_b)
        pv_diag(full, v_a, s_a, m2)
        v_p[full] = v_b[full]
        finish(oa_ref)

    @pl.when(step == heads)
    def _():
        m = top(m_b)
        clear()

        def body(kb, _):
            pv(kb, v_p, s_b, m)
            return _

        lax.fori_loop(0, full, body, 0)
        pv_diag(full, v_p, s_b, m)
        finish(ob_ref)


def solution(mesh):
    ranks = mesh.shape["sp"]
    tok_spec = P(("dp", "sp"))
    rows_spec = P(("dp", "sp"), None)
    replicated = P()

    def local_step(tok_in, tok_pos, w_dq, g_q, w_uq, w_dkv, g_kv, w_uk, w_uv, w_o):
        rows, model = tok_in.shape
        num_heads = w_uq.shape[1]
        qk_dim = w_uq.shape[2]
        q_rank = w_dq.shape[1]
        kv_rank = g_kv.shape[0]
        rot = w_dkv.shape[1] - kv_rank
        nope = qk_dim - rot
        v_dim = w_uv.shape[2]
        seq = rows * ranks
        half = rot // 2
        chips = ranks // 2
        mine = num_heads // 2
        pairs = mine // 2
        pe_w = 128
        attn_scale = (0.1 * math.log(YARN_FACTOR) + 1.0) ** 2 / math.sqrt(qk_dim)
        me = lax.axis_index("sp")
        core = lax.rem(me, 2)

        angles = tok_pos.astype(F32)[:, None] * rope_freqs(rot)[None, :]
        tab = jnp.concatenate([jnp.cos(angles), jnp.sin(angles), jnp.zeros((rows, 128 - rot), F32)], axis=1)

        kchunks, nq = 2, 3
        any_spec = pl.BlockSpec(memory_space=pl.ANY)
        vmem_spec = pl.BlockSpec(memory_space=pltpu.VMEM)
        dma = pltpu.SemaphoreType.DMA
        kv_all, pe_all, cq_all, tab_all, cache_kv, cache_pe = pl.pallas_call(
            functools.partial(front_kernel, ranks),
            out_shape=(
                jax.ShapeDtypeStruct((seq, kv_rank), BF16),
                jax.ShapeDtypeStruct((seq, pe_w), BF16),
                jax.ShapeDtypeStruct((2 * rows, q_rank), BF16),
                jax.ShapeDtypeStruct((2 * rows, 128), F32),
                jax.ShapeDtypeStruct((rows, kv_rank), BF16),
                jax.ShapeDtypeStruct((rows, rot), BF16),
            ),
            in_specs=[any_spec, any_spec, any_spec, vmem_spec, vmem_spec, vmem_spec],
            out_specs=(any_spec, any_spec, any_spec, any_spec, vmem_spec, vmem_spec),
            scratch_shapes=[
                pltpu.VMEM((rows, model), BF16),
                pltpu.VMEM((kchunks, kv_rank + rot, model // kchunks), BF16),
                pltpu.VMEM((nq, model, q_rank // nq), BF16),
                pltpu.VMEM((rows, q_rank), F32),
                pltpu.VMEM((rows, kv_rank), BF16),
                pltpu.VMEM((rows, pe_w), BF16),
                pltpu.VMEM((rows, q_rank), BF16),
                dma((1 + kchunks + nq,)),
                dma((4,)),
                dma((2 * chips - 1,)),
                dma((2 * chips - 1,)),
                dma((2 * chips - 1,)),
                dma((2 * chips - 1,)),
                dma((1,)),
                dma((1,)),
                dma((1,)),
                dma((1,)),
            ],
            compiler_params=pltpu.CompilerParams(collective_id=0, has_side_effects=True, vmem_limit_bytes=60 << 20),
            cost_estimate=pl.CostEstimate(flops=2 * rows * model * (q_rank + kv_rank + rot), bytes_accessed=2 * model * (q_rank + kv_rank + rot), transcendentals=0),
        )(tok_in, w_dkv.T, w_dq, g_q[None, :], g_kv[None, :], tab)

        wuk_h = lax.dynamic_slice_in_dim(w_uk, core * mine, mine, axis=1).reshape(kv_rank, mine * nope)
        wuv_h = lax.dynamic_slice_in_dim(w_uv, core * mine, mine, axis=1).reshape(kv_rank, mine * v_dim)
        wuq_t = jnp.transpose(w_uq, (1, 2, 0))
        tab_t = tab_all.T
        cos_q, sin_q = tab_t[:half], tab_t[half:2 * half]
        qn = 2 * rows
        nblk = seq // qn
        idx = jnp.stack([me // 2, core * mine]).astype(jnp.int32)

        def whole(shape):
            return pl.BlockSpec(shape, lambda i, s: (0,) * len(shape))

        last = pairs - 1
        o_a, o_b = pl.pallas_call(
            functools.partial(attn_kernel, attn_scale * math.log2(math.e), pairs),
            out_shape=(jax.ShapeDtypeStruct((qn, pairs * v_dim), BF16),) * 2,
            grid_spec=pltpu.PrefetchScalarGridSpec(
                num_scalar_prefetch=1,
                grid=(pairs + 1,),
                in_specs=[
                    whole((qn, q_rank)),
                    whole((seq, kv_rank)),
                    whole((seq, pe_w)),
                    whole((half, qn)),
                    whole((half, qn)),
                    pl.BlockSpec((1, qk_dim, q_rank), lambda i, s: (s[1] + jnp.minimum(i, last), 0, 0)),
                    pl.BlockSpec((1, qk_dim, q_rank), lambda i, s: (s[1] + pairs + jnp.minimum(i, last), 0, 0)),
                    pl.BlockSpec((kv_rank, nope), lambda i, s: (0, jnp.minimum(i, last))),
                    pl.BlockSpec((kv_rank, nope), lambda i, s: (0, pairs + jnp.minimum(i, last))),
                    pl.BlockSpec((kv_rank, v_dim), lambda i, s: (0, jnp.minimum(i, last))),
                    pl.BlockSpec((kv_rank, v_dim), lambda i, s: (0, pairs + jnp.minimum(i, last))),
                ],
                out_specs=(
                    pl.BlockSpec((qn, v_dim), lambda i, s: (0, jnp.minimum(i, last))),
                    pl.BlockSpec((qn, v_dim), lambda i, s: (0, jnp.maximum(i - 1, 0))),
                ),
                scratch_shapes=[
                    pltpu.VMEM((nblk, qn, nope + pe_w), BF16),
                    pltpu.VMEM((nblk, qn, nope + pe_w), BF16),
                    pltpu.VMEM((nblk, v_dim, qn), BF16),
                    pltpu.VMEM((nblk, v_dim, qn), BF16),
                    pltpu.VMEM((nblk, v_dim, qn), BF16),
                    pltpu.VMEM((nope + pe_w, qn), BF16),
                    pltpu.VMEM((nope + pe_w, qn), BF16),
                    pltpu.VMEM((nblk, qn, qn), F32),
                    pltpu.VMEM((nblk, qn, qn), F32),
                    pltpu.VMEM((8, qn), F32),
                    pltpu.VMEM((8, qn), F32),
                    pltpu.VMEM((8, qn), F32),
                    pltpu.VMEM((v_dim, qn), F32),
                ],
            ),
            compiler_params=pltpu.CompilerParams(dimension_semantics=("arbitrary",), vmem_limit_bytes=60 << 20),
        )(idx, cq_all, kv_all, pe_all, cos_q, sin_q, wuq_t, wuq_t, wuk_h, wuk_h, wuv_h, wuv_h)

        o_mine = jnp.concatenate([o_a, o_b], axis=1)
        keep = lax.dynamic_slice_in_dim(o_mine, core * rows, rows, axis=0)
        give = lax.dynamic_slice_in_dim(o_mine, (1 - core) * rows, rows, axis=0)
        swap = [(d, d + 1 - 2 * (d % 2)) for d in range(ranks)]
        got = lax.ppermute(give, "sp", swap)
        first = core == 0
        o_full = jnp.concatenate([jnp.where(first, keep, got), jnp.where(first, got, keep)], axis=1)
        attn_out = jnp.dot(o_full, w_o.reshape(num_heads * v_dim, model), preferred_element_type=F32).astype(BF16)
        return attn_out, cache_kv, cache_pe

    return jax.shard_map(local_step, mesh=mesh,
                         in_specs=(rows_spec, tok_spec) + (replicated,) * 8,
                         out_specs=(rows_spec, rows_spec, rows_spec), check_vma=False)
```

time: 520 us -> 202 us (0.39)
  matrix products: 255 us -> 39.4 us
  waiting for transfers between devices: 154 us -> 3.23 us
  Pallas kernels: 0 us -> 120 us
  starting transfers between devices: 27.6 us -> 0.21 us
  local copies, waits for them, and re-layouts: 55.6 us -> 29.9 us
  other arithmetic: 16.7 us -> 7.82 us
  loops' own time: 5.61 us -> 0 us
    all_to_all x4 -> x0, waiting for transfers between devices: 154 us -> none  [the longest x1 58.3 us: local_step(): k_heads = lax.all_to_all(k_all, 'sp', 1, 0, tiled=True)]
    pallas_call x0 -> x2, Pallas kernels: none -> 120 us  [the longest x1 95.9 us: local_step(): pl.pallas_call(functools.partial(attn_kernel, attn_scale * math.log2(math...]
    dot_general x12 -> x1, matrix products: 136 us -> 39.4 us  [local_step(): jnp.dot(o_full, w_o.reshape(num_heads * v_dim, model), preferred_element_...]
    sub x8 -> x0, matrix products: 92.3 us -> none  [block_attention(): attn_prob = jax.nn.softmax(logits, axis=-1).astype(jnp.bfloat16)]
    all_to_all x4 -> x0, starting transfers between devices: 27.6 us -> none  [the longest x1 7.54 us: local_step(): k_heads = lax.all_to_all(k_all, 'sp', 1, 0, tiled=True)]
    unnamed x2 -> x0, matrix products: 26.6 us -> none
    all_to_all x4 -> x0, local copies, waits for them, and re-layouts: 20.6 us -> none  [the longest x1 6.36 us: local_step(): q_heads = lax.all_to_all(q_all, 'sp', 1, 0, tiled=True)]
    dynamic_update_slice x8 -> x0, local copies, waits for them, and re-layouts: 9.23 us -> none  [local_step(): lax.map(block_attention, jnp.arange(groups))]
  transfers between devices with their start and end apart: 4 -> 1, of which waited for: 4 -> 1; matrix products, arithmetic and copies ran while one was open for 15% -> 0% of each run, Pallas kernels for 0% -> 0%
where the time goes in v1:
time: 202 us
  Pallas kernels  120 us (59%)
  matrix products  39.4 us (20%)
  local copies, waits for them, and re-layouts  29.9 us (15%)
  other arithmetic  7.82 us (4%)
  waiting for transfers between devices  3.23 us (2%)
    pallas_call x1, Pallas kernels, local_step(): pl.pallas_call(functools.partial(attn_kernel, attn_scale * math.log2(math...  95.9 us
    dot_general x1, matrix products, local_step(): jnp.dot(o_full, w_o.reshape(num_heads * v_dim, model), preferred_element_...  39.4 us
    pallas_call x1, Pallas kernels, local_step(): pl.pallas_call(functools.partial(front_kernel, ranks), out_shape=(jax.Sha...  24.4 us
    unnamed x11, local copies, waits for them, and re-layouts  17.2 us
    dynamic_slice x1, local copies, waits for them, and re-layouts, local_step(): lax.dynamic_slice_in_dim(w_uv, core * mine, mine, axis=1)  4.95 us
    select_n x1, other arithmetic, local_step(): jnp.where(first, keep, got)  4.59 us
  transfers between devices with their start and end apart: 1, of which 1 were waited for; matrix products, arithmetic and copies ran while one was open for 0% of the time, Pallas kernels for 0%

profile of v1, /device:TPU:119, one launch (start us, length us, event | category | flops | bytes accessed | tf_op | source)
XLA Modules:
  0.0 201.5 jit_solution(2944130099737476583)
XLA Ops:
  0.6 0.7 convert_element_type.6
  1.3 1.3 broadcast_in_dim.11.gq_ref
  2.6 0.1 pad.4.clone
  2.7 1.2 multiply_cosine_fusion
  3.9 0.8 maximum_maximum_fusion.tab_ref
  4.7 24.4 %shard_map.130 = (bf16[2048,512]{1,0:T(8,128)(2,1)}, bf16[2048,128]{1,0:T(8,128)(2,1)}, bf16[512,1536]{1,0:T(8,128)(2,1)}, f32[512,128]{1,0:T(8,128)}, bf16[256,...) custom-call(bf16[256,6144]{1,0:T(8,128)(2,1)} %x_hbm.1, bf16[576,6144]{1,0:T(8,128)(2,1)} %bitcast.24, ...), custom_call_target="tpu_custom_call" | custom-call | flops 6643777536 | bytes 25952256 | tf_op jit(solution)/shard_map/pallas_call | solution.py:324
  29.1 1.1 copy.17
  30.2 0.7 fusion.4
  30.8 5.0 %constant_dynamic-slice_fusion.1 = (bf16[512,32,128]{2,1,0:T(8,128)(2,1)S(1)}, bf16[512,32,128]{2,1,0:T(8,128)(2,1)S(1)}) fusion(bf16[512,64,128]{2,1,0:T(8,128)(2,1)} %param.19, s32[]{:T(128)S(6)} %select_n.29, bf16[512,64,128]{2,1,0:T(8,128)(2,1)} %param.18), kind=kLoop, calls=%fused_computation.14 | loop fusion | bytes 16777220 | tf_op jit(solution)/shard_map/dynamic_slice | solution.py:360
  35.8 6.3 %copy.23 = bf16[64,8,32,128]{3,1,2,0:T(8,128)(2,1)} copy(bf16[64,8,32,128]{3,2,1,0:T(8,128)(2,1)S(1)} %bitcast.23) | data formatting | bytes 8388608
  42.1 6.1 %copy.24 = bf16[64,8,32,128]{3,1,2,0:T(8,128)(2,1)} copy(bf16[64,8,32,128]{3,2,1,0:T(8,128)(2,1)S(1)} %bitcast.22) | data formatting | bytes 8388608
  48.2 0.6 pad_add_fusion.idx_ref
  48.8 95.9 %shard_map.131 = (bf16[512,2048]{1,0:T(8,128)(2,1)}, bf16[512,2048]{1,0:T(8,128)(2,1)}) custom-call(s32[2]{0:T(128)} %pad_add_fusion.idx_ref, bf16[512,1536]{1,0:T(8,128)(2,1)} %get-tuple-element.11.cq_ref, bf16[2048,512]{1,0:T(8,128)(2,1)} %get-tuple-element.12.kv_ref, bf16[2048,128]{1,0:T(8,128)(2,1)} %get-tuple-element.13.pe_ref, ...), custom_call_target="tpu_custom_call" | custom-call | tf_op jit(solution)/shard_map/pallas_call | solution.py:372
  144.7 0.0 copy-start
  144.7 3.4 %constant_dynamic-update-slice_fusion.1 = bf16[512,4096]{1,0:T(8,128)(2,1)} fusion(bf16[512,2048]{1,0:T(8,128)(2,1)} %get-tuple-element.15), kind=kLoop, calls=%fused_computation.12 | loop fusion | bytes 4194304
  148.1 0.0 copy-done
  148.1 0.0 copy-start.2
  148.1 1.5 constant_dynamic-update-slice_fusion
  149.6 3.1 %constant_dynamic-slice_fusion = bf16[256,4096]{1,0:T(8,128)(2,1)} fusion(bf16[512,4096]{1,0:T(8,128)(2,1)} %constant_dynamic-update-slice_fusion, s32[]{:T(128)S(6)} %select_n.31), kind=kLoop, calls=%fused_computation.13 | loop fusion | bytes 4194308 | tf_op jit(solution)/shard_map/dynamic_slice | solution.py:416
  152.7 0.2 collective-permute-start
  152.9 0.0 copy-done.2
  152.9 0.7 copy.18
  153.6 3.2 %collective-permute-done = bf16[256,4096]{1,0:T(8,128)(2,1)S(1)} collective-permute-done((bf16[256,4096]{1,0:T(8,128)(2,1)}, bf16[256,4096]{1,0:T(8,128)(2,1)S(1)}, u32[]{:S(2)}, u32[]{:S(2)}) %collective-permute-start) | collective-permute-done | bytes 2097184 | tf_op jit(solution)/shard_map/ppermute | solution.py:418
  156.9 4.6 %broadcast_select_fusion.1 = (bf16[256,4096]{1,0:T(8,128)(2,1)}, bf16[256,4096]{1,0:T(8,128)(2,1)}) fusion(bf16[256,4096]{1,0:T(8,128)(2,1)S(1)} %collective-permute-done, pred[]{:T(512)S(6)} %eq.3, bf16[512,4096]{1,0:T(8,128)(2,1)} %constant_dynamic-update-slice_fusion, s32[]{:T(128)S(6)} %select_n.30), kind=kLoop, calls=%fused_computation.7 | loop fusion | flops 2097152 | bytes 8388613 | tf_op jit(solution)/shard_map/jit(_where)/select_n | solution.py:420
  161.4 0.0 copy-start.1
  161.4 39.4 %convolution_convert_fusion = bf16[256,6144]{1,0:T(8,128)(2,1)} fusion(bf16[8192,6144]{1,0:T(8,128)(2,1)} %bitcast.6, bf16[256,4096]{1,0:T(8,128)(2,1)} %get-tuple-element.26, bf16[256,4096]{1,0:T(8,128)(2,1)} %get-tuple-element.25), kind=kOutput, calls=%fused_computation | convolution fusion | flops 25779765248 | bytes 108003328 | tf_op jit(solution)/shard_map/dot_general | solution.py:421
  200.8 0.0 copy-done.1
  200.8 0.7 copy.27
  (1 shorter events, 0.0 us)
Async XLA Ops:
  144.7 3.4 %copy-start = (bf16[512,2048]{1,0:T(8,128)(2,1)S(1)}, bf16[512,2048]{1,0:T(8,128)(2,1)}, u32[]{:S(2)}) copy-start(bf16[512,2048]{1,0:T(8,128)(2,1)} %get-tuple-element.16) | copy-start | bytes 6291460
  148.1 4.8 %copy-start.2 = (bf16[256,64]{1,0:T(8,128)(2,1)S(1)}, bf16[256,64]{1,0:T(8,128)(2,1)}, u32[]{:S(2)}) copy-start(bf16[256,64]{1,0:T(8,128)(2,1)} %get-tuple-element.24) | copy-start | bytes 98308
  152.7 4.2 %collective-permute-start = (bf16[256,4096]{1,0:T(8,128)(2,1)}, bf16[256,4096]{1,0:T(8,128)(2,1)S(1)}, u32[]{:S(2)}, u32[]{:S(2)}) collective-permute-start(bf16[256,4096]{1,0:T(8,128)(2,1)} %constant_dynamic-slice_fusion), channel_id=1, source_target_pairs={{0,1},{1,0},{2,3},{3,2},{4,5},{5,4},{6,7},{7,6},{8,9},{9,8},{10,11... | collective-permute-start | bytes 6291464 | tf_op jit(solution)/shard_map/ppermute | solution.py:418
  161.4 39.4 %copy-start.1 = (bf16[256,512]{1,0:T(8,128)(2,1)S(1)}, bf16[256,512]{1,0:T(8,128)(2,1)}, u32[]{:S(2)}) copy-start(bf16[256,512]{1,0:T(8,128)(2,1)} %get-tuple-element.37) | copy-start | bytes 786436

commit v2 on v1

v2 whole, which is shorter than its diff:
```python
import functools
import math

import jax
import jax.numpy as jnp
from jax import lax
from jax.experimental import pallas as pl
from jax.experimental.pallas import tpu as pltpu
from jax.sharding import PartitionSpec as P

ROPE_THETA = 10000.0
YARN_FACTOR = 40.0
ORIG_CTX = 4096.0
BETA_FAST = 32.0
BETA_SLOW = 1.0
NORM_EPS = 1e-6

MESH = pl.DeviceIdType.MESH
F32 = jnp.float32
BF16 = jnp.bfloat16
NT = (((1,), (1,)), ((), ()))
TT = (((0,), (1,)), ((), ()))


def rope_freqs(rot_dim):
    half_dim = rot_dim // 2
    log_base = 2.0 * math.log(ROPE_THETA)
    low_idx = max(math.floor(rot_dim * math.log(ORIG_CTX / (BETA_FAST * 2.0 * math.pi)) / log_base), 0)
    high_idx = min(math.ceil(rot_dim * math.log(ORIG_CTX / (BETA_SLOW * 2.0 * math.pi)) / log_base), half_dim - 1)
    spread = max(high_idx - low_idx, 0.001)
    freq_list = []
    for freq_idx in range(half_dim):
        base_freq = ROPE_THETA ** (-2.0 * freq_idx / rot_dim)
        ramp_val = min(max((freq_idx - low_idx) / spread, 0.0), 1.0)
        freq_list.append(base_freq / YARN_FACTOR * ramp_val + base_freq * (1.0 - ramp_val))
    return jnp.asarray(freq_list, dtype=jnp.float32)


def front_kernel(ranks, heads, x_hbm, wkv_hbm, wq_hbm, wuk_hbm, wuv_hbm, gq_ref, gkv_ref, cos_ref, sin_ref,
                 kv_all, cq_all, tab_all, wk_out, wv_out, ckv_out, cpe_out,
                 x_v, wkv_v, wq_v, wu_v, wo_v, wide_v, cq_f, kv_v, cq_v, tab_v,
                 w_sem, own_sem, kv_send, kv_recv, pair_send, pair_recv):
    me = lax.axis_index("sp")
    core = lax.rem(me, 2)
    sib = me + 1 - 2 * core
    rows = x_v.shape[0]
    half = cos_ref.shape[0]
    kv_rank = gkv_ref.shape[1]
    right = lax.rem(me + 2, ranks)
    left = lax.rem(me + ranks - 2, ranks)
    across = lax.rem(me + 4, ranks)

    kchunks, nq = wkv_v.shape[0], wq_v.shape[0]
    kc = wkv_v.shape[2]
    nc = wq_v.shape[2]
    first = core * heads
    loads = [pltpu.make_async_copy(x_hbm, x_v, w_sem.at[0])]
    loads += [pltpu.make_async_copy(wkv_hbm.at[:, pl.ds(k * kc, kc)], wkv_v.at[k], w_sem.at[1 + k]) for k in range(kchunks)]
    loads += [pltpu.make_async_copy(wq_hbm.at[:, pl.ds(k * nc, nc)], wq_v.at[k], w_sem.at[1 + kchunks + k]) for k in range(nq)]
    loads += [pltpu.make_async_copy(h.at[:, pl.ds(first, heads), :], wu_v.at[k], w_sem.at[1 + kchunks + nq + k])
              for k, h in enumerate((wuk_hbm, wuv_hbm))]
    for c in loads:
        c.start()

    barrier = pltpu.get_barrier_semaphore()
    for peer in (sib, right, left):
        pl.semaphore_signal(barrier, inc=1, device_id={"sp": peer}, device_id_type=MESH)
    pl.semaphore_wait(barrier, 3)

    def block(idx, start=0, size=None):
        return kv_all.at[pl.ds(idx * rows + start, size or rows)]

    def remote(src, dst, send, recv, dev):
        return pltpu.make_async_remote_copy(src_ref=src, dst_ref=dst, send_sem=send, recv_sem=recv,
                                            device_id={"sp": dev}, device_id_type=MESH)

    loads[0].wait()
    acc = None
    for k in range(kchunks):
        loads[1 + k].wait()
        part = lax.dot_general(x_v[:, k * kc:(k + 1) * kc], wkv_v[k], NT, preferred_element_type=F32)
        acc = part if acc is None else acc + part
    a = acc[:, :kv_rank]
    inv = lax.rsqrt(jnp.mean(a * a, axis=-1, keepdims=True) + NORM_EPS)
    ckv = (a * inv * gkv_ref[...]).astype(BF16)
    tab_v[:half, :] = cos_ref[...]
    tab_v[half:, :] = sin_ref[...]
    tab = tab_v[...].T
    cos_t, sin_t = tab[:, :half], tab[:, half:]
    z1 = acc[:, kv_rank:kv_rank + half]
    z2 = acc[:, kv_rank + half:]
    pe = jnp.concatenate([z1 * cos_t - z2 * sin_t, z2 * cos_t + z1 * sin_t], axis=-1).astype(BF16)
    kv_v[:, :kv_rank] = ckv
    kv_v[:, kv_rank:] = jnp.concatenate([pe, jnp.zeros((rows, kv_v.shape[1] - kv_rank - 2 * half), BF16)], axis=-1)
    ckv_out[...] = ckv
    cpe_out[...] = pe

    to_sib = remote(kv_v, block(me), kv_send.at[0], kv_recv.at[0], sib)
    to_right = remote(kv_v, block(me), kv_send.at[1], kv_recv.at[1], right)
    to_left = remote(kv_v, block(me), kv_send.at[2], kv_recv.at[2], left)
    tab_copy = remote(tab_v, tab_all.at[core], pair_send.at[0], pair_recv.at[0], sib)
    for c in (to_right, to_left, to_sib, tab_copy):
        c.start()
    own = [pltpu.make_async_copy(kv_v, block(me), own_sem.at[0]),
           pltpu.make_async_copy(tab_v, tab_all.at[core], own_sem.at[1])]
    for c in own:
        c.start()

    ssq = jnp.zeros((rows, 1), F32)
    for k in range(nq):
        loads[1 + kchunks + k].wait()
        q = jnp.dot(x_v[...], wq_v[k], preferred_element_type=F32)
        cq_f[:, k * nc:(k + 1) * nc] = q
        ssq = ssq + jnp.sum(q * q, axis=-1, keepdims=True)
    inv_q = lax.rsqrt(ssq / cq_f.shape[1] + NORM_EPS)
    cq_v[...] = (cq_f[...] * inv_q * gq_ref[...]).astype(BF16)
    cq_copy = remote(cq_v, cq_all.at[pl.ds(core * rows, rows)], pair_send.at[1], pair_recv.at[1], sib)
    cq_copy.start()
    own.append(pltpu.make_async_copy(cq_v, cq_all.at[pl.ds(core * rows, rows)], own_sem.at[2]))
    own[-1].start()

    mid = rows // 2
    to_right.wait_recv()
    half_right = remote(block(left, 0, mid), block(left, 0, mid), kv_send.at[3], kv_recv.at[3], right)
    half_right.start()
    sib_left = remote(block(left), block(left), kv_send.at[5], kv_recv.at[5], sib)
    sib_left.start()
    to_left.wait_recv()
    half_left = remote(block(right, mid, mid), block(right, mid, mid), kv_send.at[4], kv_recv.at[4], left)
    half_left.start()
    sib_right = remote(block(right), block(right), kv_send.at[6], kv_recv.at[6], sib)
    sib_right.start()

    depth = wide_v.shape[1] // 8
    groups = wide_v.shape[0]
    width = wide_v.shape[2]
    for t, out in enumerate((wk_out, wv_out)):
        loads[1 + kchunks + nq + t].wait()

        def relayout(i, _, t=t):
            base = pl.multiple_of(i * depth, depth)
            for g in range(groups):
                wide_v[g] = wu_v[t, pl.ds(base, depth), g * 8:(g + 1) * 8, :].astype(F32).reshape(depth * 8, width)
            for g in range(groups):
                for h in range(8):
                    col = (g * 8 + h) * width
                    wo_v[t, pl.ds(base, depth), col:col + width] = wide_v[g, pl.ds(h, depth, stride=8), :].astype(BF16)
            return _

        lax.fori_loop(0, wu_v.shape[1] // depth, relayout, 0)
        own.append(pltpu.make_async_copy(wo_v.at[t], out, own_sem.at[3 + t]))
        own[-1].start()

    half_right.wait_recv()
    half_left.wait_recv()
    sib_across = remote(block(across), block(across), kv_send.at[7], kv_recv.at[7], sib)
    sib_across.start()
    to_sib.wait()
    to_right.wait_send()
    to_left.wait_send()
    half_right.wait_send()
    half_left.wait_send()
    for c in (sib_left, sib_right, sib_across, tab_copy, cq_copy):
        c.wait()
    for c in own:
        c.wait()


def attn_kernel(scale2, heads, idx_ref, cq_ref, kv_ref, tab_ref,
                wqa_ref, wqb_ref, wka_ref, wkb_ref, wva_ref, wvb_ref, oa_ref, ob_ref,
                k_a, k_b, v_a, v_b, v_p, q_a, q_b, s_a, s_b, m_a, m_b, l_a, l_b, o_a, o_b, cosq_ref, sinq_ref):
    step = pl.program_id(0)
    full = idx_ref[0]
    blk = k_a.shape[1]
    nope = wka_ref.shape[1]
    kv_rank = wka_ref.shape[0]
    half = cosq_ref.shape[0]
    rot = 2 * half
    sub = blk // 2

    @pl.when(step == 0)
    def _():
        for kb in range(k_a.shape[0]):
            pe = kv_ref[kb * blk:(kb + 1) * blk, kv_rank:]
            k_a[kb, :, nope:] = pe
            k_b[kb, :, nope:] = pe
        q_a[nope + rot:, :] = jnp.zeros((q_a.shape[0] - nope - rot, q_a.shape[1]), BF16)
        q_b[nope + rot:, :] = jnp.zeros((q_b.shape[0] - nope - rot, q_b.shape[1]), BF16)
        for c in range(2):
            cosq_ref[:, c * sub:(c + 1) * sub] = tab_ref[c, :half, :]
            sinq_ref[:, c * sub:(c + 1) * sub] = tab_ref[c, half:, :]
        v_p[...] = jnp.zeros_like(v_p)
        o_a[...] = jnp.zeros_like(o_a)
        l_a[...] = jnp.ones_like(l_a)
        s_b[...] = jnp.zeros_like(s_b)
        m_b[...] = jnp.zeros_like(m_b)

    def q_proj(w_ref, q_ref):
        u = lax.dot_general(w_ref[0], cq_ref[...], NT, preferred_element_type=F32)
        q_ref[:nope, :] = u[:nope].astype(BF16)
        z1 = u[nope:nope + half]
        z2 = u[nope + half:]
        q_ref[nope:nope + half, :] = (z1 * cosq_ref[...] - z2 * sinq_ref[...]).astype(BF16)
        q_ref[nope + half:nope + rot, :] = (z2 * cosq_ref[...] + z1 * sinq_ref[...]).astype(BF16)

    def kv_proj(kb, wk, wv):
        c = kv_ref[pl.ds(pl.multiple_of(kb * blk, blk), blk), :kv_rank]
        k = jnp.dot(c, wk, preferred_element_type=F32).astype(BF16)
        k_a[kb, :, :nope] = k[:, :nope]
        k_b[kb, :, :nope] = k[:, nope:]
        v = lax.dot_general(wv, c, NT, preferred_element_type=F32).astype(BF16)
        v_a[kb] = v[:nope]
        v_b[kb] = v[nope:]

    def fold_max(m_ref, s, cols):
        t = jnp.max(s.reshape(s.shape[0] // 8, 8, s.shape[1]), axis=0)
        m_ref[:, cols] = jnp.maximum(m_ref[:, cols], t)

    everything = slice(None)

    def qk(kb, k_ref, q_ref, s_ref, m_ref):
        s = jnp.dot(k_ref[kb], q_ref[...], preferred_element_type=F32)
        s_ref[kb] = s
        fold_max(m_ref, s, everything)

    def qk_diag(kb, k_ref, q_ref, s_ref, m_ref):
        s0 = jnp.dot(k_ref[kb, :sub, :], q_ref[...], preferred_element_type=F32)
        s1 = jnp.dot(k_ref[kb, sub:, :], q_ref[:, sub:], preferred_element_type=F32)
        keep = lax.broadcasted_iota(jnp.int32, (sub, sub), 0) <= lax.broadcasted_iota(jnp.int32, (sub, sub), 1)
        s00 = jnp.where(keep, s0[:, :sub], -jnp.inf)
        s1 = jnp.where(keep, s1, -jnp.inf)
        s01 = s0[:, sub:]
        s_ref[kb, :sub, :sub] = s00
        s_ref[kb, :sub, sub:] = s01
        s_ref[kb, sub:, sub:] = s1
        fold_max(m_ref, s00, slice(0, sub))
        fold_max(m_ref, s01, slice(sub, blk))
        fold_max(m_ref, s1, slice(sub, blk))

    def fold_sum(l_ref, p, cols):
        l_ref[:, cols] += jnp.sum(p.reshape(p.shape[0] // 8, 8, p.shape[1]), axis=0)

    def top(m_ref):
        return jnp.max(m_ref[...], axis=0, keepdims=True)

    def pv(kb, v_ref, s_ref, m, l_ref, o_ref):
        p = jnp.exp2((s_ref[kb] - m) * scale2)
        fold_sum(l_ref, p, everything)
        o_ref[...] += jnp.dot(v_ref[kb], p.astype(BF16), preferred_element_type=F32)

    def pv_diag(kb, v_ref, s_ref, m, l_ref, o_ref):
        p0 = jnp.exp2((s_ref[kb, :sub, :] - m) * scale2)
        p1 = jnp.exp2((s_ref[kb, sub:, sub:] - m[:, sub:]) * scale2)
        fold_sum(l_ref, p0, everything)
        fold_sum(l_ref, p1, slice(sub, blk))
        p0 = p0.astype(BF16)
        o_ref[...] += jnp.dot(v_ref[kb, :, :sub], p0, preferred_element_type=F32)
        o_ref[:, sub:] += jnp.dot(v_ref[kb, :, sub:], p1.astype(BF16), preferred_element_type=F32)

    def finish(l_ref, o_ref, out_ref):
        l = jnp.sum(l_ref[...], axis=0, keepdims=True)
        out_ref[...] = (o_ref[...] / l).T.astype(BF16)

    def clear(l_ref, o_ref):
        l_ref[...] = jnp.zeros_like(l_ref)
        o_ref[...] = jnp.zeros_like(o_ref)

    @pl.when(step < heads)
    def _():
        m = top(m_b)
        clear(l_b, o_b)
        m_a[...] = jnp.full_like(m_a, -jnp.inf)
        finish(l_a, o_a, oa_ref)
        q_proj(wqa_ref, q_a)
        q_proj(wqb_ref, q_b)
        wk = jnp.concatenate([wka_ref[...], wkb_ref[...]], axis=1)
        wv = jnp.concatenate([wva_ref[...].T, wvb_ref[...].T], axis=0)

        def body1(kb, _):
            kv_proj(kb, wk, wv)
            qk(kb, k_a, q_a, s_a, m_a)
            pv(kb, v_p, s_b, m, l_b, o_b)
            return _

        lax.fori_loop(0, full, body1, 0)
        clear(l_a, o_a)
        kv_proj(full, wk, wv)
        qk_diag(full, k_a, q_a, s_a, m_a)
        pv_diag(full, v_p, s_b, m, l_b, o_b)
        m2 = top(m_a)
        m_b[...] = jnp.full_like(m_b, -jnp.inf)

        def body2(kb, _):
            qk(kb, k_b, q_b, s_b, m_b)
            pv(kb, v_a, s_a, m2, l_a, o_a)
            v_p[kb] = v_b[kb]
            return _

        lax.fori_loop(0, full, body2, 0)
        finish(l_b, o_b, ob_ref)
        qk_diag(full, k_b, q_b, s_b, m_b)
        pv_diag(full, v_a, s_a, m2, l_a, o_a)
        v_p[full] = v_b[full]

    @pl.when(step == heads)
    def _():
        m = top(m_b)
        clear(l_b, o_b)
        finish(l_a, o_a, oa_ref)

        def body(kb, _):
            pv(kb, v_p, s_b, m, l_b, o_b)
            return _

        lax.fori_loop(0, full, body, 0)
        pv_diag(full, v_p, s_b, m, l_b, o_b)
        finish(l_b, o_b, ob_ref)


def out_kernel(oa_hbm, ob_hbm, wo_hbm, out_hbm, own_v, sib_v, w_v, out_v,
               o_sem, w_sem, out_sem, send_sem, recv_sem):
    me = lax.axis_index("sp")
    core = lax.rem(me, 2)
    sib = me + 1 - 2 * core
    rows, span = own_v.shape
    wide = oa_hbm.shape[1]
    bufs, _, _, nc = w_v.shape
    steps = out_hbm.shape[1] // nc

    def fetch(n, slot, part):
        owner = core if part == 0 else 1 - core
        return pltpu.make_async_copy(
            wo_hbm.at[pl.ds(pl.multiple_of(owner * span, span), span), pl.ds(pl.multiple_of(n * nc, nc), nc)],
            w_v.at[slot, part], w_sem.at[slot, part])

    fetch(0, 0, 0).start()
    own = [pltpu.make_async_copy(h.at[pl.ds(core * rows, rows)], own_v.at[:, pl.ds(k * wide, wide)], o_sem.at[k])
           for k, h in enumerate((oa_hbm, ob_hbm))]
    for c in own:
        c.start()
    fetch(0, 0, 1).start()
    for n in range(1, bufs):
        for part in range(2):
            fetch(n, n, part).start()

    barrier = pltpu.get_barrier_semaphore()
    pl.semaphore_signal(barrier, inc=1, device_id={"sp": sib}, device_id_type=MESH)
    pl.semaphore_wait(barrier, 1)
    swap = [pltpu.make_async_remote_copy(
        src_ref=h.at[pl.ds((1 - core) * rows, rows)], dst_ref=sib_v.at[:, pl.ds(k * wide, wide)],
        send_sem=send_sem.at[k], recv_sem=recv_sem.at[k], device_id={"sp": sib}, device_id_type=MESH)
        for k, h in enumerate((oa_hbm, ob_hbm))]
    for c in swap:
        c.start()
    for c in own:
        c.wait()

    def store(n, slot):
        return pltpu.make_async_copy(out_v.at[slot], out_hbm.at[:, pl.ds(pl.multiple_of(n * nc, nc), nc)], out_sem.at[slot])

    def body(n, carry):
        slot = lax.rem(n, bufs)
        oslot = lax.rem(n, 2)
        fetch(n, slot, 0).wait()
        acc = jnp.dot(own_v[...], w_v[slot, 0], preferred_element_type=F32)

        @pl.when(n == 0)
        def _():
            for c in swap:
                c.wait()

        @pl.when(n >= 2)
        def _():
            store(n - 2, oslot).wait()

        fetch(n, slot, 1).wait()
        acc = acc + jnp.dot(sib_v[...], w_v[slot, 1], preferred_element_type=F32)
        out_v[oslot] = acc.astype(BF16)
        store(n, oslot).start()

        @pl.when(n + bufs < steps)
        def _():
            fetch(n + bufs, slot, 0).start()
            fetch(n + bufs, slot, 1).start()

        return carry

    lax.fori_loop(0, steps, body, 0)
    for n in range(steps - 2, steps):
        store(n, n % 2).wait()


def solution(mesh):
    ranks = mesh.shape["sp"]
    tok_spec = P(("dp", "sp"))
    rows_spec = P(("dp", "sp"), None)
    replicated = P()

    def local_step(tok_in, tok_pos, w_dq, g_q, w_uq, w_dkv, g_kv, w_uk, w_uv, w_o):
        rows, model = tok_in.shape
        num_heads = w_uq.shape[1]
        qk_dim = w_uq.shape[2]
        q_rank = w_dq.shape[1]
        kv_rank = g_kv.shape[0]
        rot = w_dkv.shape[1] - kv_rank
        nope = qk_dim - rot
        v_dim = w_uv.shape[2]
        seq = rows * ranks
        half = rot // 2
        chips = ranks // 2
        mine = num_heads // 2
        pairs = mine // 2
        pe_w = 128
        attn_scale = (0.1 * math.log(YARN_FACTOR) + 1.0) ** 2 / math.sqrt(qk_dim)
        me = lax.axis_index("sp")
        core = lax.rem(me, 2)

        angles = rope_freqs(rot)[:, None] * tok_pos.astype(F32)[None, :]
        cos_t, sin_t = jnp.cos(angles), jnp.sin(angles)

        kchunks, nq, depth = 2, 3, 64
        kv_w = kv_rank + pe_w
        any_spec = pl.BlockSpec(memory_space=pl.ANY)
        vmem_spec = pl.BlockSpec(memory_space=pltpu.VMEM)
        dma = pltpu.SemaphoreType.DMA
        kv_all, cq_all, tab_all, wk2, wv2, cache_kv, cache_pe = pl.pallas_call(
            functools.partial(front_kernel, ranks, mine),
            out_shape=(
                jax.ShapeDtypeStruct((seq, kv_w), BF16),
                jax.ShapeDtypeStruct((2 * rows, q_rank), BF16),
                jax.ShapeDtypeStruct((2, rot, rows), F32),
                jax.ShapeDtypeStruct((kv_rank, mine * nope), BF16),
                jax.ShapeDtypeStruct((kv_rank, mine * v_dim), BF16),
                jax.ShapeDtypeStruct((rows, kv_rank), BF16),
                jax.ShapeDtypeStruct((rows, rot), BF16),
            ),
            in_specs=[any_spec] * 5 + [vmem_spec] * 4,
            out_specs=(any_spec,) * 5 + (vmem_spec, vmem_spec),
            scratch_shapes=[
                pltpu.VMEM((rows, model), BF16),
                pltpu.VMEM((kchunks, kv_rank + rot, model // kchunks), BF16),
                pltpu.VMEM((nq, model, q_rank // nq), BF16),
                pltpu.VMEM((2, kv_rank, mine, nope), BF16),
                pltpu.VMEM((2, kv_rank, mine * nope), BF16),
                pltpu.VMEM((mine // 8, depth * 8, nope), F32),
                pltpu.VMEM((rows, q_rank), F32),
                pltpu.VMEM((rows, kv_w), BF16),
                pltpu.VMEM((rows, q_rank), BF16),
                pltpu.VMEM((rot, rows), F32),
                dma((1 + kchunks + nq + 2,)),
                dma((5,)),
                dma((8,)),
                dma((8,)),
                dma((2,)),
                dma((2,)),
            ],
            compiler_params=pltpu.CompilerParams(collective_id=0, has_side_effects=True, vmem_limit_bytes=60 << 20),
            cost_estimate=pl.CostEstimate(flops=2 * rows * model * (q_rank + kv_rank + rot), bytes_accessed=2 * model * (q_rank + kv_rank + rot), transcendentals=0),
        )(tok_in, w_dkv.T, w_dq, w_uk, w_uv, g_q[None, :], g_kv[None, :], cos_t, sin_t)

        wuq_t = jnp.transpose(w_uq, (1, 2, 0))
        qn = 2 * rows
        nblk = seq // qn
        idx = jnp.stack([me // 2, core * mine]).astype(jnp.int32)

        def whole(shape):
            return pl.BlockSpec(shape, lambda i, s: (0,) * len(shape))

        last = pairs - 1
        head_v = pltpu.VMEM((nblk, v_dim, qn), BF16)
        head_k = pltpu.VMEM((nblk, qn, nope + pe_w), BF16)
        head_q = pltpu.VMEM((nope + pe_w, qn), BF16)
        scores = pltpu.VMEM((nblk, qn, qn), F32)
        stat = pltpu.VMEM((8, qn), F32)
        head_o = pltpu.VMEM((v_dim, qn), F32)
        o_a, o_b = pl.pallas_call(
            functools.partial(attn_kernel, attn_scale * math.log2(math.e), pairs),
            out_shape=(jax.ShapeDtypeStruct((qn, pairs * v_dim), BF16),) * 2,
            grid_spec=pltpu.PrefetchScalarGridSpec(
                num_scalar_prefetch=1,
                grid=(pairs + 1,),
                in_specs=[
                    whole((qn, q_rank)),
                    whole((seq, kv_w)),
                    whole((2, rot, rows)),
                    pl.BlockSpec((1, qk_dim, q_rank), lambda i, s: (s[1] + jnp.minimum(i, last), 0, 0)),
                    pl.BlockSpec((1, qk_dim, q_rank), lambda i, s: (s[1] + pairs + jnp.minimum(i, last), 0, 0)),
                    pl.BlockSpec((kv_rank, nope), lambda i, s: (0, jnp.minimum(i, last))),
                    pl.BlockSpec((kv_rank, nope), lambda i, s: (0, pairs + jnp.minimum(i, last))),
                    pl.BlockSpec((kv_rank, v_dim), lambda i, s: (0, jnp.minimum(i, last))),
                    pl.BlockSpec((kv_rank, v_dim), lambda i, s: (0, pairs + jnp.minimum(i, last))),
                ],
                out_specs=(pl.BlockSpec((qn, v_dim), lambda i, s: (0, jnp.maximum(i - 1, 0))),) * 2,
                scratch_shapes=[head_k, head_k, head_v, head_v, head_v, head_q, head_q, scores, scores,
                                stat, stat, stat, stat, head_o, head_o,
                                pltpu.VMEM((half, qn), F32), pltpu.VMEM((half, qn), F32)],
            ),
            compiler_params=pltpu.CompilerParams(dimension_semantics=("arbitrary",), vmem_limit_bytes=60 << 20),
        )(idx, cq_all, kv_all, tab_all, wuq_t, wuq_t, wk2, wk2, wv2, wv2)

        nc, bufs = 512, 4
        span = mine * v_dim
        attn_out = pl.pallas_call(
            out_kernel,
            out_shape=jax.ShapeDtypeStruct((rows, model), BF16),
            in_specs=[any_spec] * 3,
            out_specs=any_spec,
            scratch_shapes=[
                pltpu.VMEM((rows, span), BF16),
                pltpu.VMEM((rows, span), BF16),
                pltpu.VMEM((bufs, 2, span, nc), BF16),
                pltpu.VMEM((2, rows, nc), BF16),
                dma((2,)),
                dma((bufs, 2)),
                dma((2,)),
                dma((2,)),
                dma((2,)),
            ],
            compiler_params=pltpu.CompilerParams(collective_id=1, has_side_effects=True, vmem_limit_bytes=60 << 20),
        )(o_a, o_b, w_o.reshape(num_heads * v_dim, model))
        return attn_out, cache_kv, cache_pe

    return jax.shard_map(local_step, mesh=mesh,
                         in_specs=(rows_spec, tok_spec) + (replicated,) * 8,
                         out_specs=(rows_spec, rows_spec, rows_spec), check_vma=False)
```

time: 202 us -> 173 us (0.86)
  Pallas kernels: 120 us -> 163 us
  matrix products: 39.4 us -> 0 us
  local copies, waits for them, and re-layouts: 29.9 us -> 6.6 us
  other arithmetic: 7.82 us -> 2.82 us
  waiting for transfers between devices: 3.23 us -> 0 us
    pallas_call x1 -> x2, Pallas kernels: 24.4 us -> 69 us  [the longest x1 43.8 us: local_step(): pl.pallas_call(out_kernel, out_shape=jax.ShapeDtypeStruct((rows, model),...]
    dot_general x1 -> x0, matrix products: 39.4 us -> none  [local_step(): jnp.dot(o_full, w_o.reshape(num_heads * v_dim, model), preferred_element_...]
    unnamed x11 -> x7, local copies, waits for them, and re-layouts: 17.2 us -> 5.3 us
    dynamic_slice x2 -> x0, local copies, waits for them, and re-layouts: 8.08 us -> none  [the longest x1 4.95 us: local_step(): lax.dynamic_slice_in_dim(w_uv, core * mine, mine, axis=1)]
    select_n x1 -> x0, other arithmetic: 4.59 us -> none  [local_step(): jnp.where(first, keep, got)]
    ppermute x1 -> x0, waiting for transfers between devices: 3.23 us -> none  [local_step(): got = lax.ppermute(give, 'sp', swap)]
    pallas_call x1, Pallas kernels: 95.9 us -> 93.7 us  [local_step(): pl.pallas_call(functools.partial(attn_kernel, attn_scale * math.log2(math...]
  transfers between devices with their start and end apart: 1 -> 0, of which waited for: 1 -> 0; matrix products, arithmetic and copies ran while one was open for 0% -> 0% of each run, Pallas kernels for 0% -> 0%
where the time goes in v2:
time: 173 us
  Pallas kernels  163 us (94%)
  local copies, waits for them, and re-layouts  6.6 us (4%)
  other arithmetic  2.82 us (2%)
    pallas_call x1, Pallas kernels, local_step(): pl.pallas_call(functools.partial(attn_kernel, attn_scale * math.log2(math...  93.7 us
    pallas_call x1, Pallas kernels, local_step(): pl.pallas_call(out_kernel, out_shape=jax.ShapeDtypeStruct((rows, model),...  43.8 us
    pallas_call x1, Pallas kernels, local_step(): pl.pallas_call(functools.partial(front_kernel, ranks, mine), out_shape=(j...  25.3 us
    unnamed x7, local copies, waits for them, and re-layouts  5.3 us

profile of v2, /device:TPU:119, one launch (start us, length us, event | category | flops | bytes accessed | tf_op | source)
XLA Modules:
  0.0 172.9 jit_solution(16770694210693230072)
XLA Ops:
  0.6 0.7 pad_add_fusion.idx_ref
  1.3 0.7 convert_element_type.3
  2.0 1.3 broadcast_in_dim.8.gq_ref
  3.3 1.5 multiply_sine_fusion
  4.8 25.3 %shard_map.130 = (bf16[2048,640]{1,0:T(8,128)(2,1)}, bf16[512,1536]{1,0:T(8,128)(2,1)}, f32[2,64,256]{2,1,0:T(8,128)}, bf16[512,4096]{1,0:T(8,128)(2,1)}, bf16[5...) custom-call(bf16[256,6144]{1,0:T(8,128)(2,1)} %x_hbm.1, bf16[576,6144]{1,0:T(8,128)(2,1)} %bitcast.8, ...), custom_call_target="tpu_custom_call" | custom-call | flops 6643777536 | bytes 25952256 | tf_op jit(solution)/shard_map/pallas_call | solution.py:426
  30.0 93.7 %shard_map.131 = (bf16[512,2048]{1,0:T(8,128)(2,1)}, bf16[512,2048]{1,0:T(8,128)(2,1)}) custom-call(s32[2]{0:T(128)} %pad_add_fusion.idx_ref, bf16[512,1536]{1,0:T(8,128)(2,1)} %get-tuple-element.12.cq_ref, bf16[2048,640]{1,0:T(8,128)(2,1)} %get-tuple-element.13.kv_ref, f32[2,64,256]{2,1,0:T(8,128)} %get-tuple-element.14.tab_ref, ...), custom_call_target="tpu_custom_call" | custom-call | tf_op jit(solution)/shard_map/pallas_call | solution.py:476
  123.7 0.0 copy-start.1
  123.7 43.8 %shard_map.132 = bf16[256,6144]{1,0:T(8,128)(2,1)} custom-call(bf16[512,2048]{1,0:T(8,128)(2,1)} %get-tuple-element.17.oa_hbm, bf16[512,2048]{1,0:T(8,128)(2,1)} %get-tuple-element.18.ob_hbm, bf16[8192,6144]{1,0:T(8,128)(2,1)} %bitcast.5.wo_hbm), custom_call_target="tpu_custom_call" | custom-call | tf_op jit(solution)/shard_map/pallas_call | solution.py:503
  167.5 0.0 copy-done.1
  167.5 0.0 copy-start
  167.6 0.7 copy.14
  168.3 3.9 %copy.17 = bf16[256,6144]{1,0:T(8,128)(2,1)} copy(bf16[256,6144]{1,0:T(8,128)(2,1)} %shard_map.132) | data formatting | bytes 6291456
  172.1 0.0 copy-done
  172.1 0.7 copy.18
Async XLA Ops:
  123.7 43.8 %copy-start.1 = (bf16[256,64]{1,0:T(8,128)(2,1)S(1)}, bf16[256,64]{1,0:T(8,128)(2,1)}, u32[]{:S(2)}) copy-start(bf16[256,64]{1,0:T(8,128)(2,1)} %get-tuple-element.23) | copy-start | bytes 98308
  167.5 4.6 %copy-start = (bf16[256,512]{1,0:T(8,128)(2,1)S(1)}, bf16[256,512]{1,0:T(8,128)(2,1)}, u32[]{:S(2)}) copy-start(bf16[256,512]{1,0:T(8,128)(2,1)} %get-tuple-element.30) | copy-start | bytes 786436

commit v3 on v2

v3 whole, which is shorter than its diff:
```python
import functools
import math

import jax
import jax.numpy as jnp
from jax import lax
from jax.experimental import pallas as pl
from jax.experimental.pallas import tpu as pltpu
from jax.sharding import PartitionSpec as P

ROPE_THETA = 10000.0
YARN_FACTOR = 40.0
ORIG_CTX = 4096.0
BETA_FAST = 32.0
BETA_SLOW = 1.0
NORM_EPS = 1e-6

MESH = pl.DeviceIdType.MESH
F32 = jnp.float32
BF16 = jnp.bfloat16
NT = (((1,), (1,)), ((), ()))
TT = (((0,), (1,)), ((), ()))


def rope_freqs(rot_dim):
    half_dim = rot_dim // 2
    log_base = 2.0 * math.log(ROPE_THETA)
    low_idx = max(math.floor(rot_dim * math.log(ORIG_CTX / (BETA_FAST * 2.0 * math.pi)) / log_base), 0)
    high_idx = min(math.ceil(rot_dim * math.log(ORIG_CTX / (BETA_SLOW * 2.0 * math.pi)) / log_base), half_dim - 1)
    spread = max(high_idx - low_idx, 0.001)
    freq_list = []
    for freq_idx in range(half_dim):
        base_freq = ROPE_THETA ** (-2.0 * freq_idx / rot_dim)
        ramp_val = min(max((freq_idx - low_idx) / spread, 0.0), 1.0)
        freq_list.append(base_freq / YARN_FACTOR * ramp_val + base_freq * (1.0 - ramp_val))
    return jnp.asarray(freq_list, dtype=jnp.float32)


def front_kernel(ranks, heads, x_hbm, wkv_hbm, wq_hbm, wuk_hbm, wuv_hbm, gq_ref, gkv_ref, cos_ref, sin_ref,
                 kv_all, cq_all, tab_all, wk_out, wv_out,
                 x_v, wkv_v, wq_v, wu_v, wo_v, wide_v, cq_f, kv_v, cq_v, tab_v,
                 w_sem, own_sem, kv_send, kv_recv, pair_send, pair_recv):
    me = lax.axis_index("sp")
    core = lax.rem(me, 2)
    sib = me + 1 - 2 * core
    rows = x_v.shape[0]
    half = cos_ref.shape[0]
    kv_rank = gkv_ref.shape[0]
    right = lax.rem(me + 2, ranks)
    left = lax.rem(me + ranks - 2, ranks)
    across = lax.rem(me + 4, ranks)

    kchunks, nq = wkv_v.shape[0], wq_v.shape[0]
    kc = wkv_v.shape[2]
    nc = wq_v.shape[2]
    first = core * heads
    loads = [pltpu.make_async_copy(x_hbm, x_v, w_sem.at[0])]
    loads += [pltpu.make_async_copy(wkv_hbm.at[:, pl.ds(k * kc, kc)], wkv_v.at[k], w_sem.at[1 + k]) for k in range(kchunks)]
    loads += [pltpu.make_async_copy(wq_hbm.at[:, pl.ds(k * nc, nc)], wq_v.at[k], w_sem.at[1 + kchunks + k]) for k in range(nq)]
    loads += [pltpu.make_async_copy(h.at[:, pl.ds(first, heads), :], wu_v.at[k], w_sem.at[1 + kchunks + nq + k])
              for k, h in enumerate((wuk_hbm, wuv_hbm))]
    for c in loads:
        c.start()

    barrier = pltpu.get_barrier_semaphore()
    for peer in (sib, right, left):
        pl.semaphore_signal(barrier, inc=1, device_id={"sp": peer}, device_id_type=MESH)
    pl.semaphore_wait(barrier, 3)

    def block(idx, start=0, size=None):
        return kv_all.at[pl.ds(idx * rows + start, size or rows)]

    def remote(src, dst, send, recv, dev):
        return pltpu.make_async_remote_copy(src_ref=src, dst_ref=dst, send_sem=send, recv_sem=recv,
                                            device_id={"sp": dev}, device_id_type=MESH)

    loads[0].wait()
    acc = None
    for k in range(kchunks):
        loads[1 + k].wait()
        part = lax.dot_general(x_v[:, k * kc:(k + 1) * kc], wkv_v[k], NT, preferred_element_type=F32)
        acc = part if acc is None else acc + part
    a = acc[:, :kv_rank]
    inv = lax.rsqrt(jnp.mean(a * a, axis=-1, keepdims=True) + NORM_EPS)
    ckv = (a * inv * gkv_ref[...][None, :]).astype(BF16)
    tab_v[:half, :] = cos_ref[...]
    tab_v[half:, :] = sin_ref[...]
    tab = tab_v[...].T
    cos_t, sin_t = tab[:, :half], tab[:, half:]
    z1 = acc[:, kv_rank:kv_rank + half]
    z2 = acc[:, kv_rank + half:]
    pe = jnp.concatenate([z1 * cos_t - z2 * sin_t, z2 * cos_t + z1 * sin_t], axis=-1).astype(BF16)
    kv_v[:, :kv_rank] = ckv
    kv_v[:, kv_rank:] = jnp.concatenate([pe, jnp.zeros((rows, kv_v.shape[1] - kv_rank - 2 * half), BF16)], axis=-1)

    to_sib = remote(kv_v, block(me), kv_send.at[0], kv_recv.at[0], sib)
    to_right = remote(kv_v, block(me), kv_send.at[1], kv_recv.at[1], right)
    to_left = remote(kv_v, block(me), kv_send.at[2], kv_recv.at[2], left)
    tab_copy = remote(tab_v, tab_all.at[core], pair_send.at[0], pair_recv.at[0], sib)
    for c in (to_right, to_left, to_sib, tab_copy):
        c.start()
    own = [pltpu.make_async_copy(kv_v, block(me), own_sem.at[0]),
           pltpu.make_async_copy(tab_v, tab_all.at[core], own_sem.at[1])]
    for c in own:
        c.start()

    ssq = jnp.zeros((rows, 1), F32)
    for k in range(nq):
        loads[1 + kchunks + k].wait()
        q = jnp.dot(x_v[...], wq_v[k], preferred_element_type=F32)
        cq_f[:, k * nc:(k + 1) * nc] = q
        ssq = ssq + jnp.sum(q * q, axis=-1, keepdims=True)
    inv_q = lax.rsqrt(ssq / cq_f.shape[1] + NORM_EPS)
    cq_v[...] = (cq_f[...] * inv_q * gq_ref[...][None, :]).astype(BF16)
    cq_copy = remote(cq_v, cq_all.at[pl.ds(core * rows, rows)], pair_send.at[1], pair_recv.at[1], sib)
    cq_copy.start()
    own.append(pltpu.make_async_copy(cq_v, cq_all.at[pl.ds(core * rows, rows)], own_sem.at[2]))
    own[-1].start()

    mid = rows // 2
    to_right.wait_recv()
    half_right = remote(block(left, 0, mid), block(left, 0, mid), kv_send.at[3], kv_recv.at[3], right)
    half_right.start()
    sib_left = remote(block(left), block(left), kv_send.at[5], kv_recv.at[5], sib)
    sib_left.start()
    to_left.wait_recv()
    half_left = remote(block(right, mid, mid), block(right, mid, mid), kv_send.at[4], kv_recv.at[4], left)
    half_left.start()
    sib_right = remote(block(right), block(right), kv_send.at[6], kv_recv.at[6], sib)
    sib_right.start()

    depth = wide_v.shape[1] // 8
    groups = wide_v.shape[0]
    width = wide_v.shape[2]
    for t, out in enumerate((wk_out, wv_out)):
        loads[1 + kchunks + nq + t].wait()

        def relayout(i, _, t=t):
            base = pl.multiple_of(i * depth, depth)
            for g in range(groups):
                wide_v[g] = wu_v[t, pl.ds(base, depth), g * 8:(g + 1) * 8, :].astype(F32).reshape(depth * 8, width)
            for g in range(groups):
                for h in range(8):
                    col = (g * 8 + h) * width
                    wo_v[t, pl.ds(base, depth), col:col + width] = wide_v[g, pl.ds(h, depth, stride=8), :].astype(BF16)
            return _

        lax.fori_loop(0, wu_v.shape[1] // depth, relayout, 0)
        own.append(pltpu.make_async_copy(wo_v.at[t], out, own_sem.at[3 + t]))
        own[-1].start()

    half_right.wait_recv()
    half_left.wait_recv()
    sib_across = remote(block(across), block(across), kv_send.at[7], kv_recv.at[7], sib)
    sib_across.start()
    to_sib.wait()
    to_right.wait_send()
    to_left.wait_send()
    half_right.wait_send()
    half_left.wait_send()
    for c in (sib_left, sib_right, sib_across, tab_copy, cq_copy):
        c.wait()
    for c in own:
        c.wait()


def attn_kernel(scale2, steps, cq_ref, kv_ref, tab_ref,
                wqa_ref, wqb_ref, wka_ref, wkb_ref, wva_ref, wvb_ref, oa_ref, ob_ref, ckv_ref, cpe_ref,
                k_v, v_a, v_b, q_v, s_a, s_b, m_a, m_b, l_a, l_b, o_a, o_b, cosq_ref, sinq_ref):
    step = pl.program_id(0)
    me = lax.axis_index("sp")
    full = me // 2
    _, blocks, blk, kdim = k_v.shape
    kv_rank = wka_ref.shape[0]
    nope = wka_ref.shape[1] // 2
    half = cosq_ref.shape[0]
    rot = 2 * half
    sub = blk // 2
    everything = slice(None)

    @pl.when(step == 0)
    def _():
        for kb in range(blocks):
            pe = kv_ref[kb * blk:(kb + 1) * blk, kv_rank:]
            k_v[0, kb, :, nope:] = pe
            k_v[1, kb, :, nope:] = pe
        q_v[:, nope + rot:, :] = jnp.zeros((2, kdim - nope - rot, blk), BF16)
        for c in range(2):
            cosq_ref[:, c * sub:(c + 1) * sub] = tab_ref[c, :half, :]
            sinq_ref[:, c * sub:(c + 1) * sub] = tab_ref[c, half:, :]
        v_b[...] = jnp.zeros_like(v_b)
        s_b[...] = jnp.zeros_like(s_b)
        m_b[...] = jnp.zeros_like(m_b)
        o_a[...] = jnp.zeros_like(o_a)
        l_a[...] = jnp.ones_like(l_a)
        rows = ckv_ref.shape[0]
        own = kv_ref[pl.ds(pl.multiple_of(me * rows, rows), rows), :]
        ckv_ref[...] = own[:, :kv_rank]
        cpe_ref[...] = own[:, kv_rank:kv_rank + rot]

    def q_proj(w_ref):
        w = jnp.concatenate([w_ref[0], w_ref[1]], axis=0)
        both = lax.dot_general(w, cq_ref[...], NT, preferred_element_type=F32)
        for h in range(2):
            u = both[h * (nope + rot):(h + 1) * (nope + rot)]
            q_v[h, :nope, :] = u[:nope].astype(BF16)
            z1 = u[nope:nope + half]
            z2 = u[nope + half:]
            q_v[h, nope:nope + half, :] = (z1 * cosq_ref[...] - z2 * sinq_ref[...]).astype(BF16)
            q_v[h, nope + half:nope + rot, :] = (z2 * cosq_ref[...] + z1 * sinq_ref[...]).astype(BF16)

    def kv_proj(kb, wk, wv, v_ref):
        c = kv_ref[pl.ds(pl.multiple_of(kb * blk, blk), blk), :kv_rank]
        k = jnp.dot(c, wk, preferred_element_type=F32).astype(BF16)
        v = lax.dot_general(wv, c, NT, preferred_element_type=F32).astype(BF16)
        for h in range(2):
            k_v[h, kb, :, :nope] = k[:, h * nope:(h + 1) * nope]
            v_ref[h, kb] = v[h * nope:(h + 1) * nope]

    def fold_max(m_ref, h, s, cols):
        t = jnp.max(s.reshape(s.shape[0] // 8, 8, s.shape[1]), axis=0)
        m_ref[h, :, cols] = jnp.maximum(m_ref[h, :, cols], t)

    def qk(h, kb, s_ref, m_ref):
        s = jnp.dot(k_v[h, kb], q_v[h], preferred_element_type=F32)
        s_ref[h, kb] = s
        fold_max(m_ref, h, s, everything)

    def qk_diag(h, kb, s_ref, m_ref):
        s0 = jnp.dot(k_v[h, kb, :sub, :], q_v[h], preferred_element_type=F32)
        s1 = jnp.dot(k_v[h, kb, sub:, :], q_v[h, :, sub:], preferred_element_type=F32)
        keep = lax.broadcasted_iota(jnp.int32, (sub, sub), 0) <= lax.broadcasted_iota(jnp.int32, (sub, sub), 1)
        s00 = jnp.where(keep, s0[:, :sub], -jnp.inf)
        s1 = jnp.where(keep, s1, -jnp.inf)
        s01 = s0[:, sub:]
        s_ref[h, kb, :sub, :sub] = s00
        s_ref[h, kb, :sub, sub:] = s01
        s_ref[h, kb, sub:, sub:] = s1
        fold_max(m_ref, h, s00, slice(0, sub))
        fold_max(m_ref, h, s01, slice(sub, blk))
        fold_max(m_ref, h, s1, slice(sub, blk))

    def fold_sum(l_ref, h, p, cols):
        l_ref[h, :, cols] += jnp.sum(p.reshape(p.shape[0] // 8, 8, p.shape[1]), axis=0)

    def top(m_ref):
        return [jnp.max(m_ref[h], axis=0, keepdims=True) for h in range(2)]

    def pv(h, kb, v_ref, s_ref, m, l_ref, o_ref):
        p = jnp.exp2((s_ref[h, kb] - m[h]) * scale2)
        fold_sum(l_ref, h, p, everything)
        o_ref[h] += jnp.dot(v_ref[h, kb], p.astype(BF16), preferred_element_type=F32)

    def pv_diag(h, kb, v_ref, s_ref, m, l_ref, o_ref):
        p0 = jnp.exp2((s_ref[h, kb, :sub, :] - m[h]) * scale2)
        p1 = jnp.exp2((s_ref[h, kb, sub:, sub:] - m[h][:, sub:]) * scale2)
        fold_sum(l_ref, h, p0, everything)
        fold_sum(l_ref, h, p1, slice(sub, blk))
        p0 = p0.astype(BF16)
        o_ref[h] += jnp.dot(v_ref[h, kb, :, :sub], p0, preferred_element_type=F32)
        o_ref[h, :, sub:] += jnp.dot(v_ref[h, kb, :, sub:], p1.astype(BF16), preferred_element_type=F32)

    def finish(l_ref, o_ref, out_ref):
        for h in range(2):
            l = jnp.sum(l_ref[h], axis=0, keepdims=True)
            out_ref[:, h * nope:(h + 1) * nope] = (o_ref[h] / l).T.astype(BF16)

    def clear(l_ref, o_ref):
        l_ref[...] = jnp.zeros_like(l_ref)
        o_ref[...] = jnp.zeros_like(o_ref)

    def stage(wq_ref, wk_ref, wv_ref, new, old, done, done_out):
        s_n, m_n, v_n = new
        s_o, m_o, v_o, l_o, out_o = old
        m = top(m_o)
        q_proj(wq_ref)
        finish(done[0], done[1], done_out)
        clear(l_o, out_o)
        m_n[...] = jnp.full_like(m_n, -jnp.inf)
        wk = wk_ref[...]
        wv = wv_ref[...].T

        def body(kb, carry):
            kv_proj(kb, wk, wv, v_n)
            for h in range(2):
                pv(h, kb, v_o, s_o, m, l_o, out_o)
                qk(h, kb, s_n, m_n)
            return carry

        lax.fori_loop(0, full, body, 0)
        kv_proj(full, wk, wv, v_n)
        for h in range(2):
            pv_diag(h, full, v_o, s_o, m, l_o, out_o)
            qk_diag(h, full, s_n, m_n)

    @pl.when(step < steps)
    def _():
        stage(wqa_ref, wka_ref, wva_ref, (s_a, m_a, v_a), (s_b, m_b, v_b, l_b, o_b), (l_a, o_a), oa_ref)
        stage(wqb_ref, wkb_ref, wvb_ref, (s_b, m_b, v_b), (s_a, m_a, v_a, l_a, o_a), (l_b, o_b), ob_ref)

    @pl.when(step == steps)
    def _():
        m = top(m_b)
        clear(l_b, o_b)
        finish(l_a, o_a, oa_ref)

        def body(kb, carry):
            for h in range(2):
                pv(h, kb, v_b, s_b, m, l_b, o_b)
            return carry

        lax.fori_loop(0, full, body, 0)
        for h in range(2):
            pv_diag(h, full, v_b, s_b, m, l_b, o_b)
        finish(l_b, o_b, ob_ref)


def out_kernel(oa_hbm, ob_hbm, wo_hbm, out_hbm, own_v, sib_v, w_v, acc_v, out_v,
               o_sem, w_sem, out_sem, swap_send, swap_recv, res_send, res_recv):
    me = lax.axis_index("sp")
    core = lax.rem(me, 2)
    sib = me + 1 - 2 * core
    wide = oa_hbm.shape[1]
    span = own_v.shape[1]
    rows = out_hbm.shape[0]
    bufs, _, nc = w_v.shape
    steps = acc_v.shape[0]

    def fetch(i):
        part = i // steps
        owner = core + part - 2 * core * part
        col = core * (steps * nc) + lax.rem(i, steps) * nc
        slot = lax.rem(i, bufs)
        return pltpu.make_async_copy(
            wo_hbm.at[pl.ds(pl.multiple_of(owner * span, span), span), pl.ds(pl.multiple_of(col, nc), nc)],
            w_v.at[slot], w_sem.at[slot])

    own = [pltpu.make_async_copy(h, own_v.at[:, pl.ds(k * wide, wide)], o_sem.at[k])
           for k, h in enumerate((oa_hbm, ob_hbm))]
    fetch(0).start()
    for c in own:
        c.start()
    for i in range(1, bufs):
        fetch(i).start()

    barrier = pltpu.get_barrier_semaphore()
    pl.semaphore_signal(barrier, inc=1, device_id={"sp": sib}, device_id_type=MESH)
    pl.semaphore_wait(barrier, 1)
    swap = [pltpu.make_async_remote_copy(
        src_ref=h, dst_ref=sib_v.at[:, pl.ds(k * wide, wide)],
        send_sem=swap_send.at[k], recv_sem=swap_recv.at[k], device_id={"sp": sib}, device_id_type=MESH)
        for k, h in enumerate((oa_hbm, ob_hbm))]
    for c in swap:
        c.start()
    for c in own:
        c.wait()

    def own_half(i, carry):
        fetch(i).wait()
        acc_v[i] = jnp.dot(own_v[...], w_v[lax.rem(i, bufs)], preferred_element_type=F32)

        @pl.when(i + bufs < 2 * steps)
        def _():
            fetch(i + bufs).start()

        return carry

    lax.fori_loop(0, steps, own_half, 0)
    for c in swap:
        c.wait()

    def store(n):
        slot = lax.rem(n, 2)
        cols = pl.ds(pl.multiple_of(core * (steps * nc) + n * nc, nc), nc)
        keep = pltpu.make_async_copy(out_v.at[slot, pl.ds(pl.multiple_of(core * rows, rows), rows)],
                                     out_hbm.at[:, cols], out_sem.at[slot])
        give = pltpu.make_async_remote_copy(
            src_ref=out_v.at[slot, pl.ds(pl.multiple_of((1 - core) * rows, rows), rows)], dst_ref=out_hbm.at[:, cols],
            send_sem=res_send.at[n], recv_sem=res_recv.at[n], device_id={"sp": sib}, device_id_type=MESH)
        return keep, give

    def sib_half(n, carry):
        i = n + steps
        fetch(i).wait()

        @pl.when(n >= 2)
        def _():
            keep, give = store(n - 2)
            keep.wait()
            give.wait_send()

        out_v[lax.rem(n, 2)] = (acc_v[n] + jnp.dot(sib_v[...], w_v[lax.rem(i, bufs)], preferred_element_type=F32)).astype(BF16)
        for c in store(n):
            c.start()

        @pl.when(i + bufs < 2 * steps)
        def _():
            fetch(i + bufs).start()

        return carry

    lax.fori_loop(0, steps, sib_half, 0)
    for n in range(steps - 2, steps):
        keep, give = store(n)
        keep.wait()
        give.wait_send()
    for n in range(steps):
        store(n)[1].wait_recv()


def solution(mesh):
    ranks = mesh.shape["sp"]
    tok_spec = P(("dp", "sp"))
    rows_spec = P(("dp", "sp"), None)
    replicated = P()

    def local_step(tok_in, tok_pos, w_dq, g_q, w_uq, w_dkv, g_kv, w_uk, w_uv, w_o):
        rows, model = tok_in.shape
        num_heads = w_uq.shape[1]
        qk_dim = w_uq.shape[2]
        q_rank = w_dq.shape[1]
        kv_rank = g_kv.shape[0]
        rot = w_dkv.shape[1] - kv_rank
        nope = qk_dim - rot
        v_dim = w_uv.shape[2]
        seq = rows * ranks
        half = rot // 2
        mine = num_heads // 2
        pe_w = 128
        attn_scale = (0.1 * math.log(YARN_FACTOR) + 1.0) ** 2 / math.sqrt(qk_dim)
        angles = rope_freqs(rot)[:, None] * tok_pos.astype(F32)[None, :]
        cos_t, sin_t = jnp.cos(angles), jnp.sin(angles)

        kchunks, nq, depth = 2, 3, 64
        kv_w = kv_rank + pe_w
        any_spec = pl.BlockSpec(memory_space=pl.ANY)
        vmem_spec = pl.BlockSpec(memory_space=pltpu.VMEM)
        dma = pltpu.SemaphoreType.DMA
        kv_all, cq_all, tab_all, wk2, wv2 = pl.pallas_call(
            functools.partial(front_kernel, ranks, mine),
            out_shape=(
                jax.ShapeDtypeStruct((seq, kv_w), BF16),
                jax.ShapeDtypeStruct((2 * rows, q_rank), BF16),
                jax.ShapeDtypeStruct((2, rot, rows), F32),
                jax.ShapeDtypeStruct((kv_rank, mine * nope), BF16),
                jax.ShapeDtypeStruct((kv_rank, mine * v_dim), BF16),
            ),
            in_specs=[any_spec] * 5 + [vmem_spec] * 4,
            out_specs=(any_spec,) * 5,
            scratch_shapes=[
                pltpu.VMEM((rows, model), BF16),
                pltpu.VMEM((kchunks, kv_rank + rot, model // kchunks), BF16),
                pltpu.VMEM((nq, model, q_rank // nq), BF16),
                pltpu.VMEM((2, kv_rank, mine, nope), BF16),
                pltpu.VMEM((2, kv_rank, mine * nope), BF16),
                pltpu.VMEM((mine // 8, depth * 8, nope), F32),
                pltpu.VMEM((rows, q_rank), F32),
                pltpu.VMEM((rows, kv_w), BF16),
                pltpu.VMEM((rows, q_rank), BF16),
                pltpu.VMEM((rot, rows), F32),
                dma((1 + kchunks + nq + 2,)),
                dma((5,)),
                dma((8,)),
                dma((8,)),
                dma((2,)),
                dma((2,)),
            ],
            compiler_params=pltpu.CompilerParams(collective_id=0, has_side_effects=True, vmem_limit_bytes=60 << 20),
            cost_estimate=pl.CostEstimate(flops=2 * rows * model * (q_rank + kv_rank + rot), bytes_accessed=2 * model * (q_rank + kv_rank + rot), transcendentals=0),
        )(tok_in, w_dkv.T, w_dq, w_uk, w_uv, g_q, g_kv, cos_t, sin_t)

        wuq_t = jnp.transpose(w_uq, (1, 2, 0))
        qn = 2 * rows
        nblk = seq // qn
        steps = mine // 4
        last = steps - 1

        def whole(shape):
            return pl.BlockSpec(shape, lambda i: (0,) * len(shape))

        def up_spec(part):
            return pl.BlockSpec((2, qk_dim, q_rank), lambda i: (lax.rem(lax.axis_index("sp"), 2) * (mine // 2) + part * steps + jnp.minimum(i, last), 0, 0))

        def lat_spec(part):
            return pl.BlockSpec((kv_rank, 2 * nope), lambda i: (0, part * steps + jnp.minimum(i, last)))

        head_v = pltpu.VMEM((2, nblk, v_dim, qn), BF16)
        scores = pltpu.VMEM((2, nblk, qn, qn), F32)
        stat = pltpu.VMEM((2, 8, qn), F32)
        head_o = pltpu.VMEM((2, v_dim, qn), F32)
        o_a, o_b, cache_kv, cache_pe = pl.pallas_call(
            functools.partial(attn_kernel, attn_scale * math.log2(math.e), steps),
            out_shape=(jax.ShapeDtypeStruct((qn, 2 * steps * v_dim), BF16),) * 2 + (
                jax.ShapeDtypeStruct((rows, kv_rank), BF16),
                jax.ShapeDtypeStruct((rows, rot), BF16),
            ),
            grid=(steps + 1,),
            in_specs=[
                whole((qn, q_rank)),
                whole((seq, kv_w)),
                whole((2, rot, rows)),
                up_spec(0), up_spec(1), lat_spec(0), lat_spec(1), lat_spec(0), lat_spec(1),
            ],
            out_specs=(pl.BlockSpec((qn, 2 * v_dim), lambda i: (0, jnp.maximum(i - 1, 0))),) * 2 + (
                whole((rows, kv_rank)), whole((rows, rot))),
            scratch_shapes=[pltpu.VMEM((2, nblk, qn, nope + pe_w), BF16), head_v, head_v, pltpu.VMEM((2, nope + pe_w, qn), BF16),
                            scores, scores, stat, stat, stat, stat, head_o, head_o,
                            pltpu.VMEM((half, qn), F32), pltpu.VMEM((half, qn), F32)],
            compiler_params=pltpu.CompilerParams(dimension_semantics=("arbitrary",), vmem_limit_bytes=60 << 20),
        )(cq_all, kv_all, tab_all, wuq_t, wuq_t, wk2, wk2, wv2, wv2)

        nc, bufs = 512, 6
        span = mine * v_dim
        pieces = model // 2 // nc
        attn_out = pl.pallas_call(
            out_kernel,
            out_shape=jax.ShapeDtypeStruct((rows, model), BF16),
            in_specs=[any_spec] * 3,
            out_specs=any_spec,
            scratch_shapes=[
                pltpu.VMEM((qn, span), BF16),
                pltpu.VMEM((qn, span), BF16),
                pltpu.VMEM((bufs, span, nc), BF16),
                pltpu.VMEM((pieces, qn, nc), F32),
                pltpu.VMEM((2, qn, nc), BF16),
                dma((2,)),
                dma((bufs,)),
                dma((2,)),
                dma((2,)),
                dma((2,)),
                dma((pieces,)),
                dma((pieces,)),
            ],
            compiler_params=pltpu.CompilerParams(collective_id=1, has_side_effects=True, vmem_limit_bytes=60 << 20),
        )(o_a, o_b, w_o.reshape(num_heads * v_dim, model))
        return attn_out, cache_kv, cache_pe

    return jax.shard_map(local_step, mesh=mesh,
                         in_specs=(rows_spec, tok_spec) + (replicated,) * 8,
                         out_specs=(rows_spec, rows_spec, rows_spec), check_vma=False)
```

time: 173 us -> 145 us (0.84)
  Pallas kernels: 163 us -> 138 us
  local copies, waits for them, and re-layouts: 6.6 us -> 4.6 us
    pallas_call x1, Pallas kernels: 93.7 us -> 75.4 us  [local_step(): pl.pallas_call(functools.partial(attn_kernel, attn_scale * math.log2(math...]
    pallas_call x1, Pallas kernels: 43.8 us -> 37.9 us  [local_step(): pl.pallas_call(out_kernel, out_shape=jax.ShapeDtypeStruct((rows, model),...]
    unnamed x7 -> x4, local copies, waits for them, and re-layouts: 5.3 us -> 4.6 us
where the time goes in v3:
time: 145 us
  Pallas kernels  138 us (95%)
  local copies, waits for them, and re-layouts  4.6 us (3%)
  other arithmetic  2.16 us (1%)
    pallas_call x1, Pallas kernels, local_step(): pl.pallas_call(functools.partial(attn_kernel, attn_scale * math.log2(math...  75.4 us
    pallas_call x1, Pallas kernels, local_step(): pl.pallas_call(out_kernel, out_shape=jax.ShapeDtypeStruct((rows, model),...  37.9 us
    pallas_call x1, Pallas kernels, local_step(): pl.pallas_call(functools.partial(front_kernel, ranks, mine), out_shape=(j...  24.5 us
    unnamed x4, local copies, waits for them, and re-layouts  4.6 us

profile of v3, /device:TPU:119, one launch (start us, length us, event | category | flops | bytes accessed | tf_op | source)
XLA Modules:
  0.0 145.3 jit_solution(12747010055728923743)
XLA Ops:
  0.6 0.7 convert_element_type.3
  1.3 1.5 %multiply_sine_fusion = (f32[32,256]{1,0:T(8,128)}, f32[32,256]{1,0:T(8,128)}) fusion(f32[256]{0:T(256)S(1)} %convert_element_type.3, f32[32]{0:T(128)} %constant.2.clone), kind=kLoop, calls=%fused_computation | loop fusion | flops 8192 | bytes 66688 | tf_op jit(solution)/shard_map/sin | solution.py:432
  2.8 24.5 %shard_map.130 = (bf16[2048,640]{1,0:T(8,128)(2,1)}, bf16[512,1536]{1,0:T(8,128)(2,1)}, f32[2,64,256]{2,1,0:T(8,128)}, bf16[512,4096]{1,0:T(8,128)(2,1)}, bf16[512,4096]{1,0:T(8,128)(2,1)}) custom-call(bf16[256,6144]{1,0:T(8,128)(2,1)} %x_hbm.1, bf16[576,6144]{1,0:T(8,128)(2,1)} %bitcast.5, bf16[6144,1536]{1,0:T(8,128)(2,1)} %wq_hbm.1, ...), custom_call_target="tpu_custom_call" | custom-call | flops 6643777536 | bytes 25952256 | tf_op jit(solution)/shard_map/pallas_call | solution.py:439
  27.3 75.4 %shard_map.131 = (bf16[512,2048]{1,0:T(8,128)(2,1)}, bf16[512,2048]{1,0:T(8,128)(2,1)}, bf16[256,512]{1,0:T(8,128)(2,1)}, bf16[256,64]{1,0:T(8,128)(2,1)}) custom-call(bf16[512,1536]{1,0:T(8,128)(2,1)} %get-tuple-element.12.cq_ref, bf16[2048,640]{1,0:T(8,128)(2,1)} %get-tuple-element.13.kv_ref, f32[2,64,256]{2,1,0:T(8,128)} %get-tuple-element.14.tab_ref, ...), custom_call_target="tpu_custom_call" | custom-call | tf_op jit(solution)/shard_map/pallas_call | solution.py:491
  102.7 0.0 copy-start
  102.7 37.9 %shard_map.132 = bf16[256,6144]{1,0:T(8,128)(2,1)} custom-call(bf16[512,2048]{1,0:T(8,128)(2,1)} %get-tuple-element.17.oa_hbm, bf16[512,2048]{1,0:T(8,128)(2,1)} %get-tuple-element.18.ob_hbm, bf16[8192,6144]{1,0:T(8,128)(2,1)} %bitcast.2.wo_hbm), custom_call_target="tpu_custom_call" | custom-call | tf_op jit(solution)/shard_map/pallas_call | solution.py:515
  140.7 0.0 copy-done
  140.7 0.7 copy.14
  141.4 3.9 %copy.16 = bf16[256,6144]{1,0:T(8,128)(2,1)} copy(bf16[256,6144]{1,0:T(8,128)(2,1)} %shard_map.132) | data formatting | bytes 6291456
Async XLA Ops:
  102.7 37.9 %copy-start = (bf16[256,64]{1,0:T(8,128)(2,1)S(1)}, bf16[256,64]{1,0:T(8,128)(2,1)}, u32[]{:S(2)}) copy-start(bf16[256,64]{1,0:T(8,128)(2,1)} %get-tuple-element.23) | copy-start | bytes 98308

commit v4 on v3

--- a/solution.py
+++ b/solution.py
@@ -54,13 +54,29 @@
     kc = wkv_v.shape[2]
     nc = wq_v.shape[2]
     first = core * heads
-    loads = [pltpu.make_async_copy(x_hbm, x_v, w_sem.at[0])]
-    loads += [pltpu.make_async_copy(wkv_hbm.at[:, pl.ds(k * kc, kc)], wkv_v.at[k], w_sem.at[1 + k]) for k in range(kchunks)]
-    loads += [pltpu.make_async_copy(wq_hbm.at[:, pl.ds(k * nc, nc)], wq_v.at[k], w_sem.at[1 + kchunks + k]) for k in range(nq)]
-    loads += [pltpu.make_async_copy(h.at[:, pl.ds(first, heads), :], wu_v.at[k], w_sem.at[1 + kchunks + nq + k])
+    loads = []
+    for k in range(kchunks):
+        cols = pl.ds(k * kc, kc)
+        loads.append([pltpu.make_async_copy(x_hbm.at[:, cols], x_v.at[:, cols], w_sem.at[2 * k]),
+                      pltpu.make_async_copy(wkv_hbm.at[:, cols], wkv_v.at[k], w_sem.at[2 * k + 1])])
+    base = 2 * kchunks
+    loads += [[pltpu.make_async_copy(wq_hbm.at[:, pl.ds(k * nc, nc)], wq_v.at[k], w_sem.at[base + k])] for k in range(nq)]
+    loads += [[pltpu.make_async_copy(h.at[:, pl.ds(first, heads), :], wu_v.at[k], w_sem.at[base + nq + k])]
               for k, h in enumerate((wuk_hbm, wuv_hbm))]
-    for c in loads:
-        c.start()
+    ahead = 3
+
+    def launch(i):
+        if i < len(loads):
+            for c in loads[i]:
+                c.start()
+
+    def arrive(i):
+        for c in loads[i]:
+            c.wait()
+        launch(i + ahead)
+
+    for i in range(ahead):
+        launch(i)
 
     barrier = pltpu.get_barrier_semaphore()
     for peer in (sib, right, left):
@@ -74,10 +90,9 @@
         return pltpu.make_async_remote_copy(src_ref=src, dst_ref=dst, send_sem=send, recv_sem=recv,
                                             device_id={"sp": dev}, device_id_type=MESH)
 
-    loads[0].wait()
     acc = None
     for k in range(kchunks):
-        loads[1 + k].wait()
+        arrive(k)
         part = lax.dot_general(x_v[:, k * kc:(k + 1) * kc], wkv_v[k], NT, preferred_element_type=F32)
         acc = part if acc is None else acc + part
     a = acc[:, :kv_rank]
@@ -106,7 +121,7 @@
 
     ssq = jnp.zeros((rows, 1), F32)
     for k in range(nq):
-        loads[1 + kchunks + k].wait()
+        arrive(kchunks + k)
         q = jnp.dot(x_v[...], wq_v[k], preferred_element_type=F32)
         cq_f[:, k * nc:(k + 1) * nc] = q
         ssq = ssq + jnp.sum(q * q, axis=-1, keepdims=True)
@@ -133,7 +148,7 @@
     groups = wide_v.shape[0]
     width = wide_v.shape[2]
     for t, out in enumerate((wk_out, wv_out)):
-        loads[1 + kchunks + nq + t].wait()
+        arrive(kchunks + nq + t)
 
         def relayout(i, _, t=t):
             base = pl.multiple_of(i * depth, depth)
@@ -188,11 +203,6 @@
         for c in range(2):
             cosq_ref[:, c * sub:(c + 1) * sub] = tab_ref[c, :half, :]
             sinq_ref[:, c * sub:(c + 1) * sub] = tab_ref[c, half:, :]
-        v_b[...] = jnp.zeros_like(v_b)
-        s_b[...] = jnp.zeros_like(s_b)
-        m_b[...] = jnp.zeros_like(m_b)
-        o_a[...] = jnp.zeros_like(o_a)
-        l_a[...] = jnp.ones_like(l_a)
         rows = ckv_ref.shape[0]
         own = kv_ref[pl.ds(pl.multiple_of(me * rows, rows), rows), :]
         ckv_ref[...] = own[:, :kv_rank]
@@ -340,8 +350,7 @@
     fetch(0).start()
     for c in own:
         c.start()
-    for i in range(1, bufs):
-        fetch(i).start()
+    fetch(1).start()
 
     barrier = pltpu.get_barrier_semaphore()
     pl.semaphore_signal(barrier, inc=1, device_id={"sp": sib}, device_id_type=MESH)
@@ -350,19 +359,15 @@
         src_ref=h, dst_ref=sib_v.at[:, pl.ds(k * wide, wide)],
         send_sem=swap_send.at[k], recv_sem=swap_recv.at[k], device_id={"sp": sib}, device_id_type=MESH)
         for k, h in enumerate((oa_hbm, ob_hbm))]
+    for c in own:
+        c.wait()
     for c in swap:
         c.start()
-    for c in own:
-        c.wait()
 
     def own_half(i, carry):
         fetch(i).wait()
+        fetch(i + 2).start()
         acc_v[i] = jnp.dot(own_v[...], w_v[lax.rem(i, bufs)], preferred_element_type=F32)
-
-        @pl.when(i + bufs < 2 * steps)
-        def _():
-            fetch(i + bufs).start()
-
         return carry
 
     lax.fori_loop(0, steps, own_half, 0)
@@ -383,6 +388,10 @@
         i = n + steps
         fetch(i).wait()
 
+        @pl.when(i + 2 < 2 * steps)
+        def _():
+            fetch(i + 2).start()
+
         @pl.when(n >= 2)
         def _():
             keep, give = store(n - 2)
@@ -392,11 +401,6 @@
         out_v[lax.rem(n, 2)] = (acc_v[n] + jnp.dot(sib_v[...], w_v[lax.rem(i, bufs)], preferred_element_type=F32)).astype(BF16)
         for c in store(n):
             c.start()
-
-        @pl.when(i + bufs < 2 * steps)
-        def _():
-            fetch(i + bufs).start()
-
         return carry
 
     lax.fori_loop(0, steps, sib_half, 0)
@@ -431,7 +435,7 @@
         angles = rope_freqs(rot)[:, None] * tok_pos.astype(F32)[None, :]
         cos_t, sin_t = jnp.cos(angles), jnp.sin(angles)
 
-        kchunks, nq, depth = 2, 3, 64
+        kchunks, nq, depth = 4, 3, 64
         kv_w = kv_rank + pe_w
         any_spec = pl.BlockSpec(memory_space=pl.ANY)
         vmem_spec = pl.BlockSpec(memory_space=pltpu.VMEM)
@@ -458,7 +462,7 @@
                 pltpu.VMEM((rows, kv_w), BF16),
                 pltpu.VMEM((rows, q_rank), BF16),
                 pltpu.VMEM((rot, rows), F32),
-                dma((1 + kchunks + nq + 2,)),
+                dma((2 * kchunks + nq + 2,)),
                 dma((5,)),
                 dma((8,)),
                 dma((8,)),
@@ -509,7 +513,7 @@
             compiler_params=pltpu.CompilerParams(dimension_semantics=("arbitrary",), vmem_limit_bytes=60 << 20),
         )(cq_all, kv_all, tab_all, wuq_t, wuq_t, wk2, wk2, wv2, wv2)
 
-        nc, bufs = 512, 6
+        nc, bufs = 512, 3
         span = mine * v_dim
         pieces = model // 2 // nc
         attn_out = pl.pallas_call(

time: 145 us -> 139 us (0.959)
  Pallas kernels: 138 us -> 132 us
    pallas_call x1, Pallas kernels: 37.9 us -> 33.2 us  [local_step(): pl.pallas_call(out_kernel, out_shape=jax.ShapeDtypeStruct((rows, model),...]
where the time goes in v4:
time: 139 us
  Pallas kernels  132 us (95%)
  local copies, waits for them, and re-layouts  4.6 us (3%)
  other arithmetic  2.16 us (2%)
    pallas_call x1, Pallas kernels, local_step(): pl.pallas_call(functools.partial(attn_kernel, attn_scale * math.log2(math...  74.8 us
    pallas_call x1, Pallas kernels, local_step(): pl.pallas_call(out_kernel, out_shape=jax.ShapeDtypeStruct((rows, model),...  33.2 us
    pallas_call x1, Pallas kernels, local_step(): pl.pallas_call(functools.partial(front_kernel, ranks, mine), out_shape=(j...  23.8 us
    unnamed x4, local copies, waits for them, and re-layouts  4.6 us

profile of v4, /device:TPU:119, one launch (start us, length us, event | category | flops | bytes accessed | tf_op | source)
XLA Modules:
  0.0 139.2 jit_solution(17013782627037209392)
XLA Ops:
  0.6 0.7 convert_element_type.3
  1.3 1.5 %multiply_sine_fusion = (f32[32,256]{1,0:T(8,128)}, f32[32,256]{1,0:T(8,128)}) fusion(f32[256]{0:T(256)S(1)} %convert_element_type.3, f32[32]{0:T(128)} %constant.2.clone), kind=kLoop, calls=%fused_computation | loop fusion | flops 8192 | bytes 66688 | tf_op jit(solution)/shard_map/sin | solution.py:436
  2.8 23.8 %shard_map.130 = (bf16[2048,640]{1,0:T(8,128)(2,1)}, bf16[512,1536]{1,0:T(8,128)(2,1)}, f32[2,64,256]{2,1,0:T(8,128)}, bf16[512,4096]{1,0:T(8,128)(2,1)}, bf16[512,4096]{1,0:T(8,128)(2,1)}) custom-call(bf16[256,6144]{1,0:T(8,128)(2,1)} %x_hbm.1, bf16[576,6144]{1,0:T(8,128)(2,1)} %bitcast.5, bf16[6144,1536]{1,0:T(8,128)(2,1)} %wq_hbm.1, ...), custom_call_target="tpu_custom_call" | custom-call | flops 6643777536 | bytes 25952256 | tf_op jit(solution)/shard_map/pallas_call | solution.py:443
  26.6 74.8 %shard_map.131 = (bf16[512,2048]{1,0:T(8,128)(2,1)}, bf16[512,2048]{1,0:T(8,128)(2,1)}, bf16[256,512]{1,0:T(8,128)(2,1)}, bf16[256,64]{1,0:T(8,128)(2,1)}) custom-call(bf16[512,1536]{1,0:T(8,128)(2,1)} %get-tuple-element.12.cq_ref, bf16[2048,640]{1,0:T(8,128)(2,1)} %get-tuple-element.13.kv_ref, f32[2,64,256]{2,1,0:T(8,128)} %get-tuple-element.14.tab_ref, ...), custom_call_target="tpu_custom_call" | custom-call | tf_op jit(solution)/shard_map/pallas_call | solution.py:495
  101.4 0.0 copy-start
  101.4 33.2 %shard_map.132 = bf16[256,6144]{1,0:T(8,128)(2,1)} custom-call(bf16[512,2048]{1,0:T(8,128)(2,1)} %get-tuple-element.17.oa_hbm, bf16[512,2048]{1,0:T(8,128)(2,1)} %get-tuple-element.18.ob_hbm, bf16[8192,6144]{1,0:T(8,128)(2,1)} %bitcast.2.wo_hbm), custom_call_target="tpu_custom_call" | custom-call | tf_op jit(solution)/shard_map/pallas_call | solution.py:519
  134.6 0.0 copy-done
  134.6 0.7 copy.14
  135.3 3.9 %copy.16 = bf16[256,6144]{1,0:T(8,128)(2,1)} copy(bf16[256,6144]{1,0:T(8,128)(2,1)} %shard_map.132) | data formatting | bytes 6291456
Async XLA Ops:
  101.4 33.2 %copy-start = (bf16[256,64]{1,0:T(8,128)(2,1)S(1)}, bf16[256,64]{1,0:T(8,128)(2,1)}, u32[]{:S(2)}) copy-start(bf16[256,64]{1,0:T(8,128)(2,1)} %get-tuple-element.23) | copy-start | bytes 98308

commit v5 on v4

--- a/solution.py
+++ b/solution.py
@@ -81,7 +81,6 @@
     barrier = pltpu.get_barrier_semaphore()
     for peer in (sib, right, left):
         pl.semaphore_signal(barrier, inc=1, device_id={"sp": peer}, device_id_type=MESH)
-    pl.semaphore_wait(barrier, 3)
 
     def block(idx, start=0, size=None):
         return kv_all.at[pl.ds(idx * rows + start, size or rows)]
@@ -108,6 +107,7 @@
     kv_v[:, :kv_rank] = ckv
     kv_v[:, kv_rank:] = jnp.concatenate([pe, jnp.zeros((rows, kv_v.shape[1] - kv_rank - 2 * half), BF16)], axis=-1)
 
+    pl.semaphore_wait(barrier, 3)
     to_sib = remote(kv_v, block(me), kv_send.at[0], kv_recv.at[0], sib)
     to_right = remote(kv_v, block(me), kv_send.at[1], kv_recv.at[1], right)
     to_left = remote(kv_v, block(me), kv_send.at[2], kv_recv.at[2], left)
@@ -325,14 +325,14 @@
         finish(l_b, o_b, ob_ref)
 
 
-def out_kernel(oa_hbm, ob_hbm, wo_hbm, out_hbm, own_v, sib_v, w_v, acc_v, out_v,
-               o_sem, w_sem, out_sem, swap_send, swap_recv, res_send, res_recv):
+def out_kernel(oa_hbm, ob_hbm, wo_hbm, res_v, own_v, sib_v, w_v, acc_v, out_v,
+               o_sem, w_sem, swap_send, swap_recv, res_send, res_recv):
     me = lax.axis_index("sp")
     core = lax.rem(me, 2)
     sib = me + 1 - 2 * core
     wide = oa_hbm.shape[1]
     span = own_v.shape[1]
-    rows = out_hbm.shape[0]
+    rows = res_v.shape[0]
     bufs, _, nc = w_v.shape
     steps = acc_v.shape[0]
 
@@ -374,18 +374,17 @@
     for c in swap:
         c.wait()
 
-    def store(n):
-        slot = lax.rem(n, 2)
-        cols = pl.ds(pl.multiple_of(core * (steps * nc) + n * nc, nc), nc)
-        keep = pltpu.make_async_copy(out_v.at[slot, pl.ds(pl.multiple_of(core * rows, rows), rows)],
-                                     out_hbm.at[:, cols], out_sem.at[slot])
-        give = pltpu.make_async_remote_copy(
-            src_ref=out_v.at[slot, pl.ds(pl.multiple_of((1 - core) * rows, rows), rows)], dst_ref=out_hbm.at[:, cols],
+    def cols(n):
+        return pl.ds(pl.multiple_of(core * (steps * nc) + n * nc, nc), nc)
+
+    def give(n):
+        return pltpu.make_async_remote_copy(
+            src_ref=out_v.at[lax.rem(n, 2), pl.ds(pl.multiple_of((1 - core) * rows, rows), rows)], dst_ref=res_v.at[:, cols(n)],
             send_sem=res_send.at[n], recv_sem=res_recv.at[n], device_id={"sp": sib}, device_id_type=MESH)
-        return keep, give
 
     def sib_half(n, carry):
         i = n + steps
+        slot = lax.rem(n, 2)
         fetch(i).wait()
 
         @pl.when(i + 2 < 2 * steps)
@@ -394,22 +393,18 @@
 
         @pl.when(n >= 2)
         def _():
-            keep, give = store(n - 2)
-            keep.wait()
-            give.wait_send()
-
-        out_v[lax.rem(n, 2)] = (acc_v[n] + jnp.dot(sib_v[...], w_v[lax.rem(i, bufs)], preferred_element_type=F32)).astype(BF16)
-        for c in store(n):
-            c.start()
+            give(n - 2).wait_send()
+
+        out_v[slot] = (acc_v[n] + jnp.dot(sib_v[...], w_v[lax.rem(i, bufs)], preferred_element_type=F32)).astype(BF16)
+        give(n).start()
+        res_v[:, cols(n)] = out_v[slot, pl.ds(pl.multiple_of(core * rows, rows), rows), :]
         return carry
 
     lax.fori_loop(0, steps, sib_half, 0)
     for n in range(steps - 2, steps):
-        keep, give = store(n)
-        keep.wait()
-        give.wait_send()
+        give(n).wait_send()
     for n in range(steps):
-        store(n)[1].wait_recv()
+        give(n).wait_recv()
 
 
 def solution(mesh):
@@ -520,7 +515,7 @@
             out_kernel,
             out_shape=jax.ShapeDtypeStruct((rows, model), BF16),
             in_specs=[any_spec] * 3,
-            out_specs=any_spec,
+            out_specs=vmem_spec,
             scratch_shapes=[
                 pltpu.VMEM((qn, span), BF16),
                 pltpu.VMEM((qn, span), BF16),
@@ -531,7 +526,6 @@
                 dma((bufs,)),
                 dma((2,)),
                 dma((2,)),
-                dma((2,)),
                 dma((pieces,)),
                 dma((pieces,)),
             ],

time: 139 us -> 141 us (1.014)
    pallas_call x1, Pallas kernels: 33.2 us -> 34.9 us  [local_step(): pl.pallas_call(out_kernel, out_shape=jax.ShapeDtypeStruct((rows, model),...]
where the time goes in v5:
time: 141 us
  Pallas kernels  133 us (94%)
  local copies, waits for them, and re-layouts  4.6 us (3%)
  other arithmetic  2.16 us (2%)
    pallas_call x1, Pallas kernels, local_step(): pl.pallas_call(functools.partial(attn_kernel, attn_scale * math.log2(math...  74.8 us
    pallas_call x1, Pallas kernels, local_step(): pl.pallas_call(out_kernel, out_shape=jax.ShapeDtypeStruct((rows, model),...  34.9 us
    pallas_call x1, Pallas kernels, local_step(): pl.pallas_call(functools.partial(front_kernel, ranks, mine), out_shape=(j...  23.8 us
    unnamed x4, local copies, waits for them, and re-layouts  4.6 us

profile of v5, /device:TPU:119, one launch (start us, length us, event | category | flops | bytes accessed | tf_op | source)
XLA Modules:
  0.0 140.9 jit_solution(10118314561723306020)
XLA Ops:
  0.6 0.7 convert_element_type.3
  1.3 1.5 %multiply_sine_fusion = (f32[32,256]{1,0:T(8,128)}, f32[32,256]{1,0:T(8,128)}) fusion(f32[256]{0:T(256)S(1)} %convert_element_type.3, f32[32]{0:T(128)} %constant.2.clone), kind=kLoop, calls=%fused_computation | loop fusion | flops 8192 | bytes 66688 | tf_op jit(solution)/shard_map/sin | solution.py:431
  2.8 23.8 %shard_map.130 = (bf16[2048,640]{1,0:T(8,128)(2,1)}, bf16[512,1536]{1,0:T(8,128)(2,1)}, f32[2,64,256]{2,1,0:T(8,128)}, bf16[512,4096]{1,0:T(8,128)(2,1)}, bf16[512,4096]{1,0:T(8,128)(2,1)}) custom-call(bf16[256,6144]{1,0:T(8,128)(2,1)} %x_hbm.1, bf16[576,6144]{1,0:T(8,128)(2,1)} %bitcast.5, bf16[6144,1536]{1,0:T(8,128)(2,1)} %wq_hbm.1, ...), custom_call_target="tpu_custom_call" | custom-call | flops 6643777536 | bytes 25952256 | tf_op jit(solution)/shard_map/pallas_call | solution.py:438
  26.6 74.8 %shard_map.131 = (bf16[512,2048]{1,0:T(8,128)(2,1)}, bf16[512,2048]{1,0:T(8,128)(2,1)}, bf16[256,512]{1,0:T(8,128)(2,1)}, bf16[256,64]{1,0:T(8,128)(2,1)}) custom-call(bf16[512,1536]{1,0:T(8,128)(2,1)} %get-tuple-element.12.cq_ref, bf16[2048,640]{1,0:T(8,128)(2,1)} %get-tuple-element.13.kv_ref, f32[2,64,256]{2,1,0:T(8,128)} %get-tuple-element.14.tab_ref, ...), custom_call_target="tpu_custom_call" | custom-call | tf_op jit(solution)/shard_map/pallas_call | solution.py:490
  101.4 0.0 copy-start
  101.4 34.9 %shard_map.132 = bf16[256,6144]{1,0:T(8,128)(2,1)} custom-call(bf16[512,2048]{1,0:T(8,128)(2,1)} %get-tuple-element.17.oa_hbm, bf16[512,2048]{1,0:T(8,128)(2,1)} %get-tuple-element.18.ob_hbm, bf16[8192,6144]{1,0:T(8,128)(2,1)} %bitcast.2.wo_hbm), custom_call_target="tpu_custom_call" | custom-call | tf_op jit(solution)/shard_map/pallas_call | solution.py:514
  136.3 0.0 copy-done
  136.3 0.7 copy.14
  137.0 3.9 %copy.16 = bf16[256,6144]{1,0:T(8,128)(2,1)} copy(bf16[256,6144]{1,0:T(8,128)(2,1)} %shard_map.132) | data formatting | bytes 6291456
Async XLA Ops:
  101.4 34.9 %copy-start = (bf16[256,64]{1,0:T(8,128)(2,1)S(1)}, bf16[256,64]{1,0:T(8,128)(2,1)}, u32[]{:S(2)}) copy-start(bf16[256,64]{1,0:T(8,128)(2,1)} %get-tuple-element.23) | copy-start | bytes 98308

commit v6 on v4

--- a/solution.py
+++ b/solution.py
@@ -81,7 +81,6 @@
     barrier = pltpu.get_barrier_semaphore()
     for peer in (sib, right, left):
         pl.semaphore_signal(barrier, inc=1, device_id={"sp": peer}, device_id_type=MESH)
-    pl.semaphore_wait(barrier, 3)
 
     def block(idx, start=0, size=None):
         return kv_all.at[pl.ds(idx * rows + start, size or rows)]
@@ -108,6 +107,7 @@
     kv_v[:, :kv_rank] = ckv
     kv_v[:, kv_rank:] = jnp.concatenate([pe, jnp.zeros((rows, kv_v.shape[1] - kv_rank - 2 * half), BF16)], axis=-1)
 
+    pl.semaphore_wait(barrier, 3)
     to_sib = remote(kv_v, block(me), kv_send.at[0], kv_recv.at[0], sib)
     to_right = remote(kv_v, block(me), kv_send.at[1], kv_recv.at[1], right)
     to_left = remote(kv_v, block(me), kv_send.at[2], kv_recv.at[2], left)
@@ -179,45 +179,148 @@
         c.wait()
 
 
-def attn_kernel(scale2, steps, cq_ref, kv_ref, tab_ref,
-                wqa_ref, wqb_ref, wka_ref, wkb_ref, wva_ref, wvb_ref, oa_ref, ob_ref, ckv_ref, cpe_ref,
-                k_v, v_a, v_b, q_v, s_a, s_b, m_a, m_b, l_a, l_b, o_a, o_b, cosq_ref, sinq_ref):
+def shares(me, ranks, steps):
+    chips = ranks // 2
+    chip = me // 2
+    give = jnp.maximum(chip - chips // 2 + 1, 0)
+    take = jnp.maximum(chips // 2 - chip, 0)
+    return chip, steps - give, take, give
+
+
+def weight_step(i, ranks, steps):
+    _, n_loc, n_rem, _ = shares(lax.axis_index("sp"), ranks, steps)
+    own = jnp.minimum(i, n_loc - 1)
+    far = steps - n_rem + jnp.minimum(i - n_loc - 1, n_rem - 1)
+    return jnp.where((i <= n_loc) | (n_rem == 0), own, far)
+
+
+def attn_kernel(scale2, ranks, steps, cq_hbm, kv_ref, tab_ref,
+                wqa_ref, wqb_ref, wka_ref, wkb_ref, wva_ref, wvb_ref, oa_hbm, ob_hbm, ckv_ref, cpe_ref,
+                cq_v, tab_v, k_v, v_a, v_b, q_v, s_a, s_b, m_a, m_b, l_a, l_b, o_a, o_b, cosq_ref, sinq_ref, oa_v, ob_v,
+                cq_sem, lat_send, lat_recv, fwd_send, fwd_recv, o_sem, o_send, oa_recv, ob_recv):
     step = pl.program_id(0)
+    final = pl.num_programs(0) - 1
     me = lax.axis_index("sp")
-    full = me // 2
+    core = lax.rem(me, 2)
+    sib = me + 1 - 2 * core
+    chip, n_loc, n_rem, n_give = shares(me, ranks, steps)
+    far_chip = ranks // 2 - 1 - chip
+    far = 2 * far_chip + core
+    most = oa_recv.shape[0]
+    is_far = step > n_loc
+    qset = jnp.where(is_far, 1, 0)
+    full = jnp.where(is_far, far_chip, chip)
     _, blocks, blk, kdim = k_v.shape
     kv_rank = wka_ref.shape[0]
     nope = wka_ref.shape[1] // 2
-    half = cosq_ref.shape[0]
+    half = cosq_ref.shape[1]
     rot = 2 * half
     sub = blk // 2
     everything = slice(None)
+    my_rows = pl.ds(pl.multiple_of(core * sub, sub), sub)
+
+    lat = [pltpu.make_async_remote_copy(src_ref=src, dst_ref=dst, send_sem=lat_send.at[k], recv_sem=lat_recv.at[k],
+                                        device_id={"sp": far}, device_id_type=MESH)
+           for k, (src, dst) in enumerate(((cq_hbm.at[my_rows], cq_v.at[1, my_rows]), (tab_ref.at[core], tab_v.at[core])))]
+    fwd = [pltpu.make_async_remote_copy(src_ref=ref, dst_ref=ref, send_sem=fwd_send.at[k], recv_sem=fwd_recv.at[k],
+                                        device_id={"sp": sib}, device_id_type=MESH)
+           for k, ref in enumerate((cq_v.at[1, my_rows], tab_v.at[core]))]
+
+    def o_cols(at):
+        return pl.ds(pl.multiple_of(at * 2 * nope, 2 * nope), 2 * nope)
+
+    def o_local(part, at):
+        src, dst = ((oa_v, oa_hbm), (ob_v, ob_hbm))[part]
+        return pltpu.make_async_copy(src, dst.at[:, o_cols(at)], o_sem.at[part])
+
+    def o_far(part, r):
+        src, dst, recv = ((oa_v, oa_hbm, oa_recv), (ob_v, ob_hbm, ob_recv))[part]
+        return pltpu.make_async_remote_copy(src_ref=src, dst_ref=dst.at[:, o_cols(steps - 1 - r)], send_sem=o_send.at[part], recv_sem=recv.at[r],
+                                            device_id={"sp": far}, device_id_type=MESH)
+
+    def left_own(s):
+        return (s >= 1) & (s <= n_loc)
+
+    def left_far(s):
+        return (s >= n_loc + 2) & (s <= n_loc + n_rem + 1)
+
+    def emit(part):
+        @pl.when(left_own(step))
+        def _():
+            o_local(part, step - 1).start()
+
+        @pl.when(left_far(step))
+        def _():
+            o_far(part, n_loc + n_rem + 1 - step).start()
+
+    def settle(part, s):
+        @pl.when(left_own(s))
+        def _():
+            o_local(part, s - 1).wait()
+
+        @pl.when(left_far(s))
+        def _():
+            o_far(part, n_loc + n_rem + 1 - s).wait_send()
 
     @pl.when(step == 0)
     def _():
+        own_cq = pltpu.make_async_copy(cq_hbm, cq_v.at[0], cq_sem.at[0])
+        own_cq.start()
+        barrier = pltpu.get_barrier_semaphore()
+        for peer in (sib, far):
+            pl.semaphore_signal(barrier, inc=1, device_id={"sp": peer}, device_id_type=MESH)
+        pl.semaphore_wait(barrier, 2)
+
+        @pl.when(n_give > 0)
+        def _():
+            for c in lat:
+                c.start()
+
         for kb in range(blocks):
             pe = kv_ref[kb * blk:(kb + 1) * blk, kv_rank:]
             k_v[0, kb, :, nope:] = pe
             k_v[1, kb, :, nope:] = pe
         q_v[:, nope + rot:, :] = jnp.zeros((2, kdim - nope - rot, blk), BF16)
         for c in range(2):
-            cosq_ref[:, c * sub:(c + 1) * sub] = tab_ref[c, :half, :]
-            sinq_ref[:, c * sub:(c + 1) * sub] = tab_ref[c, half:, :]
+            cosq_ref[0, :, c * sub:(c + 1) * sub] = tab_ref[c, :half, :]
+            sinq_ref[0, :, c * sub:(c + 1) * sub] = tab_ref[c, half:, :]
         rows = ckv_ref.shape[0]
         own = kv_ref[pl.ds(pl.multiple_of(me * rows, rows), rows), :]
         ckv_ref[...] = own[:, :kv_rank]
         cpe_ref[...] = own[:, kv_rank:kv_rank + rot]
+        own_cq.wait()
+
+    @pl.when(step > 0)
+    def _():
+        for part in range(2):
+            settle(part, step - 1)
+
+    @pl.when((step == n_loc - 1) & (n_rem > 0))
+    def _():
+        for c in lat:
+            c.wait_recv()
+        for c in fwd:
+            c.start()
+
+    @pl.when((step == n_loc + 1) & (n_rem > 0))
+    def _():
+        for c in fwd:
+            c.wait()
+        for c in range(2):
+            cosq_ref[1, :, c * sub:(c + 1) * sub] = tab_v[c, :half, :]
+            sinq_ref[1, :, c * sub:(c + 1) * sub] = tab_v[c, half:, :]
 
     def q_proj(w_ref):
         w = jnp.concatenate([w_ref[0], w_ref[1]], axis=0)
-        both = lax.dot_general(w, cq_ref[...], NT, preferred_element_type=F32)
+        both = lax.dot_general(w, cq_v[qset], NT, preferred_element_type=F32)
+        cos_t, sin_t = cosq_ref[qset], sinq_ref[qset]
         for h in range(2):
             u = both[h * (nope + rot):(h + 1) * (nope + rot)]
             q_v[h, :nope, :] = u[:nope].astype(BF16)
             z1 = u[nope:nope + half]
             z2 = u[nope + half:]
-            q_v[h, nope:nope + half, :] = (z1 * cosq_ref[...] - z2 * sinq_ref[...]).astype(BF16)
-            q_v[h, nope + half:nope + rot, :] = (z2 * cosq_ref[...] + z1 * sinq_ref[...]).astype(BF16)
+            q_v[h, nope:nope + half, :] = (z1 * cos_t - z2 * sin_t).astype(BF16)
+            q_v[h, nope + half:nope + rot, :] = (z2 * cos_t + z1 * sin_t).astype(BF16)
 
     def kv_proj(kb, wk, wv, v_ref):
         c = kv_ref[pl.ds(pl.multiple_of(kb * blk, blk), blk), :kv_rank]
@@ -279,12 +382,13 @@
         l_ref[...] = jnp.zeros_like(l_ref)
         o_ref[...] = jnp.zeros_like(o_ref)
 
-    def stage(wq_ref, wk_ref, wv_ref, new, old, done, done_out):
+    def stage(wq_ref, wk_ref, wv_ref, new, old, done, done_out, part):
         s_n, m_n, v_n = new
         s_o, m_o, v_o, l_o, out_o = old
         m = top(m_o)
         q_proj(wq_ref)
         finish(done[0], done[1], done_out)
+        emit(part)
         clear(l_o, out_o)
         m_n[...] = jnp.full_like(m_n, -jnp.inf)
         wk = wk_ref[...]
@@ -303,16 +407,17 @@
             pv_diag(h, full, v_o, s_o, m, l_o, out_o)
             qk_diag(h, full, s_n, m_n)
 
-    @pl.when(step < steps)
+    @pl.when((step < n_loc) | ((step > n_loc) & (step <= n_loc + n_rem)))
     def _():
-        stage(wqa_ref, wka_ref, wva_ref, (s_a, m_a, v_a), (s_b, m_b, v_b, l_b, o_b), (l_a, o_a), oa_ref)
-        stage(wqb_ref, wkb_ref, wvb_ref, (s_b, m_b, v_b), (s_a, m_a, v_a, l_a, o_a), (l_b, o_b), ob_ref)
-
-    @pl.when(step == steps)
+        stage(wqa_ref, wka_ref, wva_ref, (s_a, m_a, v_a), (s_b, m_b, v_b, l_b, o_b), (l_a, o_a), oa_v, 0)
+        stage(wqb_ref, wkb_ref, wvb_ref, (s_b, m_b, v_b), (s_a, m_a, v_a, l_a, o_a), (l_b, o_b), ob_v, 1)
+
+    @pl.when((step == n_loc) | ((step == n_loc + n_rem + 1) & (n_rem > 0)))
     def _():
         m = top(m_b)
         clear(l_b, o_b)
-        finish(l_a, o_a, oa_ref)
+        finish(l_a, o_a, oa_v)
+        emit(0)
 
         def body(kb, carry):
             for h in range(2):
@@ -322,7 +427,21 @@
         lax.fori_loop(0, full, body, 0)
         for h in range(2):
             pv_diag(h, full, v_b, s_b, m, l_b, o_b)
-        finish(l_b, o_b, ob_ref)
+        finish(l_b, o_b, ob_v)
+        emit(1)
+
+    @pl.when(step == final)
+    def _():
+        @pl.when(n_give > 0)
+        def _():
+            for c in lat:
+                c.wait_send()
+
+        for r in range(most):
+            @pl.when(n_give > r)
+            def _(r=r):
+                for part in range(2):
+                    o_far(part, r).wait_recv()
 
 
 def out_kernel(oa_hbm, ob_hbm, wo_hbm, out_hbm, own_v, sib_v, w_v, acc_v, out_v,
@@ -477,40 +596,42 @@
         qn = 2 * rows
         nblk = seq // qn
         steps = mine // 4
-        last = steps - 1
 
         def whole(shape):
             return pl.BlockSpec(shape, lambda i: (0,) * len(shape))
 
         def up_spec(part):
-            return pl.BlockSpec((2, qk_dim, q_rank), lambda i: (lax.rem(lax.axis_index("sp"), 2) * (mine // 2) + part * steps + jnp.minimum(i, last), 0, 0))
+            return pl.BlockSpec((2, qk_dim, q_rank), lambda i: (lax.rem(lax.axis_index("sp"), 2) * (mine // 2) + part * steps + weight_step(i, ranks, steps), 0, 0))
 
         def lat_spec(part):
-            return pl.BlockSpec((kv_rank, 2 * nope), lambda i: (0, part * steps + jnp.minimum(i, last)))
+            return pl.BlockSpec((kv_rank, 2 * nope), lambda i: (0, part * steps + weight_step(i, ranks, steps)))
 
         head_v = pltpu.VMEM((2, nblk, v_dim, qn), BF16)
         scores = pltpu.VMEM((2, nblk, qn, qn), F32)
         stat = pltpu.VMEM((2, 8, qn), F32)
         head_o = pltpu.VMEM((2, v_dim, qn), F32)
+        rope_v = pltpu.VMEM((2, half, qn), F32)
+        pair_o = pltpu.VMEM((qn, 2 * v_dim), BF16)
+        most = ranks // 4
         o_a, o_b, cache_kv, cache_pe = pl.pallas_call(
-            functools.partial(attn_kernel, attn_scale * math.log2(math.e), steps),
+            functools.partial(attn_kernel, attn_scale * math.log2(math.e), ranks, steps),
             out_shape=(jax.ShapeDtypeStruct((qn, 2 * steps * v_dim), BF16),) * 2 + (
                 jax.ShapeDtypeStruct((rows, kv_rank), BF16),
                 jax.ShapeDtypeStruct((rows, rot), BF16),
             ),
-            grid=(steps + 1,),
+            grid=(steps + most + 3,),
             in_specs=[
-                whole((qn, q_rank)),
+                any_spec,
                 whole((seq, kv_w)),
                 whole((2, rot, rows)),
                 up_spec(0), up_spec(1), lat_spec(0), lat_spec(1), lat_spec(0), lat_spec(1),
             ],
-            out_specs=(pl.BlockSpec((qn, 2 * v_dim), lambda i: (0, jnp.maximum(i - 1, 0))),) * 2 + (
-                whole((rows, kv_rank)), whole((rows, rot))),
-            scratch_shapes=[pltpu.VMEM((2, nblk, qn, nope + pe_w), BF16), head_v, head_v, pltpu.VMEM((2, nope + pe_w, qn), BF16),
-                            scores, scores, stat, stat, stat, stat, head_o, head_o,
-                            pltpu.VMEM((half, qn), F32), pltpu.VMEM((half, qn), F32)],
-            compiler_params=pltpu.CompilerParams(dimension_semantics=("arbitrary",), vmem_limit_bytes=60 << 20),
+            out_specs=(any_spec, any_spec, whole((rows, kv_rank)), whole((rows, rot))),
+            scratch_shapes=[pltpu.VMEM((2, qn, q_rank), BF16), pltpu.VMEM((2, rot, rows), F32),
+                            pltpu.VMEM((2, nblk, qn, nope + pe_w), BF16), head_v, head_v, pltpu.VMEM((2, nope + pe_w, qn), BF16),
+                            scores, scores, stat, stat, stat, stat, head_o, head_o, rope_v, rope_v, pair_o, pair_o,
+                            dma((1,)), dma((2,)), dma((2,)), dma((2,)), dma((2,)), dma((2,)), dma((2,)), dma((most,)), dma((most,))],
+            compiler_params=pltpu.CompilerParams(dimension_semantics=("arbitrary",), collective_id=2, has_side_effects=True, vmem_limit_bytes=62 << 20),
         )(cq_all, kv_all, tab_all, wuq_t, wuq_t, wk2, wk2, wv2, wv2)
 
         nc, bufs = 512, 3

time: 139 us -> 137 us (0.986)
  Pallas kernels: 132 us -> 128 us
    pallas_call x1, Pallas kernels: 74.8 us -> 70 us  [local_step(): pl.pallas_call(functools.partial(attn_kernel, attn_scale * math.log2(math...]
    unnamed x4 -> x7, local copies, waits for them, and re-layouts: 4.6 us -> 5.3 us
where the time goes in v6:
time: 137 us; the launch traced here: 136 us
  Pallas kernels  128 us (93%)
  local copies, waits for them, and re-layouts  5.3 us (4%)
  other arithmetic  2.16 us (2%)
    pallas_call x1, Pallas kernels, local_step(): pl.pallas_call(functools.partial(attn_kernel, attn_scale * math.log2(math...  70 us
    pallas_call x1, Pallas kernels, local_step(): pl.pallas_call(out_kernel, out_shape=jax.ShapeDtypeStruct((rows, model),...  34.4 us
    pallas_call x1, Pallas kernels, local_step(): pl.pallas_call(functools.partial(front_kernel, ranks, mine), out_shape=(j...  23.8 us
    unnamed x7, local copies, waits for them, and re-layouts  5.3 us

profile of v6, /device:TPU:119, one launch (start us, length us, event | category | flops | bytes accessed | tf_op | source)
XLA Modules:
  0.0 136.4 jit_solution(16280859639051380894)
XLA Ops:
  0.6 0.7 convert_element_type.3
  1.3 1.5 %multiply_sine_fusion = (f32[32,256]{1,0:T(8,128)}, f32[32,256]{1,0:T(8,128)}) fusion(f32[256]{0:T(256)S(1)} %convert_element_type.3, f32[32]{0:T(128)} %constant.2.clone), kind=kLoop, calls=%fused_computation | loop fusion | flops 8192 | bytes 66688 | tf_op jit(solution)/shard_map/sin | solution.py:555
  2.8 23.8 %shard_map.130 = (bf16[2048,640]{1,0:T(8,128)(2,1)}, bf16[512,1536]{1,0:T(8,128)(2,1)}, f32[2,64,256]{2,1,0:T(8,128)}, bf16[512,4096]{1,0:T(8,128)(2,1)}, bf16[512,4096]{1,0:T(8,128)(2,1)}) custom-call(bf16[256,6144]{1,0:T(8,128)(2,1)} %x_hbm.1, bf16[576,6144]{1,0:T(8,128)(2,1)} %bitcast.5, bf16[6144,1536]{1,0:T(8,128)(2,1)} %wq_hbm.1, ...), custom_call_target="tpu_custom_call" | custom-call | flops 6643777536 | bytes 25952256 | tf_op jit(solution)/shard_map/pallas_call | solution.py:562
  26.6 70.0 %shard_map.131 = (bf16[512,2048]{1,0:T(8,128)(2,1)}, bf16[512,2048]{1,0:T(8,128)(2,1)}, bf16[256,512]{1,0:T(8,128)(2,1)}, bf16[256,64]{1,0:T(8,128)(2,1)}) custom-call(bf16[512,1536]{1,0:T(8,128)(2,1)} %get-tuple-element.12.cq_hbm, bf16[2048,640]{1,0:T(8,128)(2,1)} %get-tuple-element.13.kv_ref, f32[2,64,256]{2,1,0:T(8,128)} %get-tuple-element.14.tab_ref, ...), custom_call_target="tpu_custom_call" | custom-call | tf_op jit(solution)/shard_map/pallas_call | solution.py:616
  96.6 0.0 copy-start.1
  96.6 34.4 %shard_map.132 = bf16[256,6144]{1,0:T(8,128)(2,1)} custom-call(bf16[512,2048]{1,0:T(8,128)(2,1)} %get-tuple-element.17.oa_hbm, bf16[512,2048]{1,0:T(8,128)(2,1)} %get-tuple-element.18.ob_hbm, bf16[8192,6144]{1,0:T(8,128)(2,1)} %bitcast.2.wo_hbm), custom_call_target="tpu_custom_call" | custom-call | tf_op jit(solution)/shard_map/pallas_call | solution.py:640
  131.1 0.0 copy-done.1
  131.1 0.0 copy-start
  131.1 0.7 copy.14
  131.8 3.9 %copy.17 = bf16[256,6144]{1,0:T(8,128)(2,1)} copy(bf16[256,6144]{1,0:T(8,128)(2,1)} %shard_map.132) | data formatting | bytes 6291456
  135.7 0.0 copy-done
  135.7 0.7 copy.18
Async XLA Ops:
  96.6 34.5 %copy-start.1 = (bf16[256,64]{1,0:T(8,128)(2,1)S(1)}, bf16[256,64]{1,0:T(8,128)(2,1)}, u32[]{:S(2)}) copy-start(bf16[256,64]{1,0:T(8,128)(2,1)} %get-tuple-element.23) | copy-start | bytes 98308
  131.1 4.6 %copy-start = (bf16[256,512]{1,0:T(8,128)(2,1)S(1)}, bf16[256,512]{1,0:T(8,128)(2,1)}, u32[]{:S(2)}) copy-start(bf16[256,512]{1,0:T(8,128)(2,1)} %get-tuple-element.30) | copy-start | bytes 786436

commit v7 on v6

--- a/solution.py
+++ b/solution.py
@@ -184,30 +184,32 @@
     chip = me // 2
     give = jnp.maximum(chip - chips // 2 + 1, 0)
     take = jnp.maximum(chips // 2 - chip, 0)
-    return chip, steps - give, take, give
+    lead = jnp.where(take > 0, steps // 2 + 2 * (take - 1), steps - give)
+    return chip, lead, take, give
 
 
 def weight_step(i, ranks, steps):
-    _, n_loc, n_rem, _ = shares(lax.axis_index("sp"), ranks, steps)
-    own = jnp.minimum(i, n_loc - 1)
-    far = steps - n_rem + jnp.minimum(i - n_loc - 1, n_rem - 1)
-    return jnp.where((i <= n_loc) | (n_rem == 0), own, far)
+    _, lead, take, _ = shares(lax.axis_index("sp"), ranks, steps)
+    far = steps - take + jnp.minimum(i - lead - 1, take - 1)
+    late = jnp.where(i <= lead + take + 1, far, jnp.minimum(i - take - 2, steps - 1))
+    return jnp.where((i <= lead) | (take == 0), jnp.minimum(i, lead - 1), late)
 
 
 def attn_kernel(scale2, ranks, steps, cq_hbm, kv_ref, tab_ref,
                 wqa_ref, wqb_ref, wka_ref, wkb_ref, wva_ref, wvb_ref, oa_hbm, ob_hbm, ckv_ref, cpe_ref,
                 cq_v, tab_v, k_v, v_a, v_b, q_v, s_a, s_b, m_a, m_b, l_a, l_b, o_a, o_b, cosq_ref, sinq_ref, oa_v, ob_v,
-                cq_sem, lat_send, lat_recv, fwd_send, fwd_recv, o_sem, o_send, oa_recv, ob_recv):
+                cq_sem, lat_send, lat_recv, fwd_send, fwd_recv, o_sem, oa_send, ob_send, oa_recv, ob_recv):
     step = pl.program_id(0)
     final = pl.num_programs(0) - 1
     me = lax.axis_index("sp")
     core = lax.rem(me, 2)
     sib = me + 1 - 2 * core
-    chip, n_loc, n_rem, n_give = shares(me, ranks, steps)
+    chip, lead, take, give = shares(me, ranks, steps)
+    taker = take > 0
     far_chip = ranks // 2 - 1 - chip
     far = 2 * far_chip + core
     most = oa_recv.shape[0]
-    is_far = step > n_loc
+    is_far = (step > lead) & (step <= lead + take + 1) & taker
     qset = jnp.where(is_far, 1, 0)
     full = jnp.where(is_far, far_chip, chip)
     _, blocks, blk, kdim = k_v.shape
@@ -229,38 +231,38 @@
     def o_cols(at):
         return pl.ds(pl.multiple_of(at * 2 * nope, 2 * nope), 2 * nope)
 
-    def o_local(part, at):
+    def o_local(part, s):
         src, dst = ((oa_v, oa_hbm), (ob_v, ob_hbm))[part]
-        return pltpu.make_async_copy(src, dst.at[:, o_cols(at)], o_sem.at[part])
+        at = jnp.where(s <= lead, s - 1, s - take - 3)
+        return pltpu.make_async_copy(src.at[most], dst.at[:, o_cols(at)], o_sem.at[part])
 
     def o_far(part, r):
-        src, dst, recv = ((oa_v, oa_hbm, oa_recv), (ob_v, ob_hbm, ob_recv))[part]
-        return pltpu.make_async_remote_copy(src_ref=src, dst_ref=dst.at[:, o_cols(steps - 1 - r)], send_sem=o_send.at[part], recv_sem=recv.at[r],
+        src, dst, send, recv = ((oa_v, oa_hbm, oa_send, oa_recv), (ob_v, ob_hbm, ob_send, ob_recv))[part]
+        return pltpu.make_async_remote_copy(src_ref=src.at[r], dst_ref=dst.at[:, o_cols(steps - 1 - r)], send_sem=send.at[r], recv_sem=recv.at[r],
                                             device_id={"sp": far}, device_id_type=MESH)
 
     def left_own(s):
-        return (s >= 1) & (s <= n_loc)
+        return ((s >= 1) & (s <= lead)) | (taker & (s >= lead + take + 3) & (s <= steps + take + 2))
 
     def left_far(s):
-        return (s >= n_loc + 2) & (s <= n_loc + n_rem + 1)
+        return taker & (s >= lead + 2) & (s <= lead + take + 1)
+
+    far_slot = lead + take + 1 - step
+    slot = jnp.where(left_far(step), far_slot, most)
 
     def emit(part):
         @pl.when(left_own(step))
         def _():
-            o_local(part, step - 1).start()
+            o_local(part, step).start()
 
         @pl.when(left_far(step))
         def _():
-            o_far(part, n_loc + n_rem + 1 - step).start()
+            o_far(part, far_slot).start()
 
     def settle(part, s):
         @pl.when(left_own(s))
         def _():
-            o_local(part, s - 1).wait()
-
-        @pl.when(left_far(s))
-        def _():
-            o_far(part, n_loc + n_rem + 1 - s).wait_send()
+            o_local(part, s).wait()
 
     @pl.when(step == 0)
     def _():
@@ -271,7 +273,7 @@
             pl.semaphore_signal(barrier, inc=1, device_id={"sp": peer}, device_id_type=MESH)
         pl.semaphore_wait(barrier, 2)
 
-        @pl.when(n_give > 0)
+        @pl.when(give > 0)
         def _():
             for c in lat:
                 c.start()
@@ -295,14 +297,14 @@
         for part in range(2):
             settle(part, step - 1)
 
-    @pl.when((step == n_loc - 1) & (n_rem > 0))
+    @pl.when((step == lead) & taker)
     def _():
         for c in lat:
             c.wait_recv()
         for c in fwd:
             c.start()
 
-    @pl.when((step == n_loc + 1) & (n_rem > 0))
+    @pl.when((step == lead + 1) & taker)
     def _():
         for c in fwd:
             c.wait()
@@ -376,7 +378,7 @@
     def finish(l_ref, o_ref, out_ref):
         for h in range(2):
             l = jnp.sum(l_ref[h], axis=0, keepdims=True)
-            out_ref[:, h * nope:(h + 1) * nope] = (o_ref[h] / l).T.astype(BF16)
+            out_ref[slot, :, h * nope:(h + 1) * nope] = (o_ref[h] / l).T.astype(BF16)
 
     def clear(l_ref, o_ref):
         l_ref[...] = jnp.zeros_like(l_ref)
@@ -407,12 +409,12 @@
             pv_diag(h, full, v_o, s_o, m, l_o, out_o)
             qk_diag(h, full, s_n, m_n)
 
-    @pl.when((step < n_loc) | ((step > n_loc) & (step <= n_loc + n_rem)))
+    @pl.when((step < lead) | (taker & (step > lead) & (step != lead + take + 1) & (step < steps + take + 2)))
     def _():
         stage(wqa_ref, wka_ref, wva_ref, (s_a, m_a, v_a), (s_b, m_b, v_b, l_b, o_b), (l_a, o_a), oa_v, 0)
         stage(wqb_ref, wkb_ref, wvb_ref, (s_b, m_b, v_b), (s_a, m_a, v_a, l_a, o_a), (l_b, o_b), ob_v, 1)
 
-    @pl.when((step == n_loc) | ((step == n_loc + n_rem + 1) & (n_rem > 0)))
+    @pl.when((step == lead) | (taker & ((step == lead + take + 1) | (step == steps + take + 2))))
     def _():
         m = top(m_b)
         clear(l_b, o_b)
@@ -432,16 +434,24 @@
 
     @pl.when(step == final)
     def _():
-        @pl.when(n_give > 0)
+        for part in range(2):
+            settle(part, step)
+
+        @pl.when(give > 0)
         def _():
             for c in lat:
                 c.wait_send()
 
         for r in range(most):
-            @pl.when(n_give > r)
+            @pl.when(give > r)
             def _(r=r):
                 for part in range(2):
                     o_far(part, r).wait_recv()
+
+            @pl.when(take > r)
+            def _(r=r):
+                for part in range(2):
+                    o_far(part, r).wait_send()
 
 
 def out_kernel(oa_hbm, ob_hbm, wo_hbm, out_hbm, own_v, sib_v, w_v, acc_v, out_v,
@@ -611,8 +621,8 @@
         stat = pltpu.VMEM((2, 8, qn), F32)
         head_o = pltpu.VMEM((2, v_dim, qn), F32)
         rope_v = pltpu.VMEM((2, half, qn), F32)
-        pair_o = pltpu.VMEM((qn, 2 * v_dim), BF16)
         most = ranks // 4
+        pair_o = pltpu.VMEM((most + 1, qn, 2 * v_dim), BF16)
         o_a, o_b, cache_kv, cache_pe = pl.pallas_call(
             functools.partial(attn_kernel, attn_scale * math.log2(math.e), ranks, steps),
             out_shape=(jax.ShapeDtypeStruct((qn, 2 * steps * v_dim), BF16),) * 2 + (
@@ -630,7 +640,7 @@
             scratch_shapes=[pltpu.VMEM((2, qn, q_rank), BF16), pltpu.VMEM((2, rot, rows), F32),
                             pltpu.VMEM((2, nblk, qn, nope + pe_w), BF16), head_v, head_v, pltpu.VMEM((2, nope + pe_w, qn), BF16),
                             scores, scores, stat, stat, stat, stat, head_o, head_o, rope_v, rope_v, pair_o, pair_o,
-                            dma((1,)), dma((2,)), dma((2,)), dma((2,)), dma((2,)), dma((2,)), dma((2,)), dma((most,)), dma((most,))],
+                            dma((1,)), dma((2,)), dma((2,)), dma((2,)), dma((2,)), dma((2,)), dma((most,)), dma((most,)), dma((most,)), dma((most,))],
             compiler_params=pltpu.CompilerParams(dimension_semantics=("arbitrary",), collective_id=2, has_side_effects=True, vmem_limit_bytes=62 << 20),
         )(cq_all, kv_all, tab_all, wuq_t, wuq_t, wk2, wk2, wv2, wv2)
 

time: 137 us -> 130 us (0.949)
  Pallas kernels: 128 us -> 122 us
    pallas_call x1, Pallas kernels: 70 us -> 64.3 us  [local_step(): pl.pallas_call(functools.partial(attn_kernel, attn_scale * math.log2(math...]
where the time goes in v7:
time: 130 us
  Pallas kernels  122 us (94%)
  local copies, waits for them, and re-layouts  5.3 us (4%)
  other arithmetic  2.16 us (2%)
    pallas_call x1, Pallas kernels, local_step(): pl.pallas_call(functools.partial(attn_kernel, attn_scale * math.log2(math...  64.3 us
    pallas_call x1, Pallas kernels, local_step(): pl.pallas_call(out_kernel, out_shape=jax.ShapeDtypeStruct((rows, model),...  33.6 us
    pallas_call x1, Pallas kernels, local_step(): pl.pallas_call(functools.partial(front_kernel, ranks, mine), out_shape=(j...  23.8 us
    unnamed x7, local copies, waits for them, and re-layouts  5.3 us

profile of v7, /device:TPU:119, one launch (start us, length us, event | category | flops | bytes accessed | tf_op | source)
XLA Modules:
  0.0 129.9 jit_solution(15255968837222248697)
XLA Ops:
  0.6 0.7 convert_element_type.3
  1.3 1.5 %multiply_sine_fusion = (f32[32,256]{1,0:T(8,128)}, f32[32,256]{1,0:T(8,128)}) fusion(f32[256]{0:T(256)S(1)} %convert_element_type.3, f32[32]{0:T(128)} %constant.2.clone), kind=kLoop, calls=%fused_computation | loop fusion | flops 8192 | bytes 66688 | tf_op jit(solution)/shard_map/sin | solution.py:565
  2.8 23.8 %shard_map.130 = (bf16[2048,640]{1,0:T(8,128)(2,1)}, bf16[512,1536]{1,0:T(8,128)(2,1)}, f32[2,64,256]{2,1,0:T(8,128)}, bf16[512,4096]{1,0:T(8,128)(2,1)}, bf16[512,4096]{1,0:T(8,128)(2,1)}) custom-call(bf16[256,6144]{1,0:T(8,128)(2,1)} %x_hbm.1, bf16[576,6144]{1,0:T(8,128)(2,1)} %bitcast.5, bf16[6144,1536]{1,0:T(8,128)(2,1)} %wq_hbm.1, ...), custom_call_target="tpu_custom_call" | custom-call | flops 6643777536 | bytes 25952256 | tf_op jit(solution)/shard_map/pallas_call | solution.py:572
  26.6 64.3 %shard_map.131 = (bf16[512,2048]{1,0:T(8,128)(2,1)}, bf16[512,2048]{1,0:T(8,128)(2,1)}, bf16[256,512]{1,0:T(8,128)(2,1)}, bf16[256,64]{1,0:T(8,128)(2,1)}) custom-call(bf16[512,1536]{1,0:T(8,128)(2,1)} %get-tuple-element.12.cq_hbm, bf16[2048,640]{1,0:T(8,128)(2,1)} %get-tuple-element.13.kv_ref, f32[2,64,256]{2,1,0:T(8,128)} %get-tuple-element.14.tab_ref, ...), custom_call_target="tpu_custom_call" | custom-call | tf_op jit(solution)/shard_map/pallas_call | solution.py:626
  91.0 0.0 copy-start.1
  91.0 33.6 %shard_map.132 = bf16[256,6144]{1,0:T(8,128)(2,1)} custom-call(bf16[512,2048]{1,0:T(8,128)(2,1)} %get-tuple-element.17.oa_hbm, bf16[512,2048]{1,0:T(8,128)(2,1)} %get-tuple-element.18.ob_hbm, bf16[8192,6144]{1,0:T(8,128)(2,1)} %bitcast.2.wo_hbm), custom_call_target="tpu_custom_call" | custom-call | tf_op jit(solution)/shard_map/pallas_call | solution.py:650
  124.6 0.0 copy-done.1
  124.6 0.0 copy-start
  124.6 0.7 copy.14
  125.3 3.9 %copy.17 = bf16[256,6144]{1,0:T(8,128)(2,1)} copy(bf16[256,6144]{1,0:T(8,128)(2,1)} %shard_map.132) | data formatting | bytes 6291456
  129.2 0.0 copy-done
  129.2 0.7 copy.18
Async XLA Ops:
  91.0 33.6 %copy-start.1 = (bf16[256,64]{1,0:T(8,128)(2,1)S(1)}, bf16[256,64]{1,0:T(8,128)(2,1)}, u32[]{:S(2)}) copy-start(bf16[256,64]{1,0:T(8,128)(2,1)} %get-tuple-element.23) | copy-start | bytes 98308
  124.6 4.6 %copy-start = (bf16[256,512]{1,0:T(8,128)(2,1)S(1)}, bf16[256,512]{1,0:T(8,128)(2,1)}, u32[]{:S(2)}) copy-start(bf16[256,512]{1,0:T(8,128)(2,1)} %get-tuple-element.30) | copy-start | bytes 786436

commit v8 on v7

--- a/solution.py
+++ b/solution.py
@@ -132,6 +132,28 @@
     own.append(pltpu.make_async_copy(cq_v, cq_all.at[pl.ds(core * rows, rows)], own_sem.at[2]))
     own[-1].start()
 
+    depth = wide_v.shape[1] // 8
+    groups = wide_v.shape[0]
+    width = wide_v.shape[2]
+
+    def up_relayout(t, out):
+        arrive(kchunks + nq + t)
+
+        def relayout(i, carry):
+            base = pl.multiple_of(i * depth, depth)
+            for g in range(groups):
+                wide_v[g] = wu_v[t, pl.ds(base, depth), g * 8:(g + 1) * 8, :].astype(F32).reshape(depth * 8, width)
+            for g in range(groups):
+                for h in range(8):
+                    col = (g * 8 + h) * width
+                    wo_v[t, pl.ds(base, depth), col:col + width] = wide_v[g, pl.ds(h, depth, stride=8), :].astype(BF16)
+            return carry
+
+        lax.fori_loop(0, wu_v.shape[1] // depth, relayout, 0)
+        own.append(pltpu.make_async_copy(wo_v.at[t], out, own_sem.at[3 + t]))
+        own[-1].start()
+
+    up_relayout(0, wk_out)
     mid = rows // 2
     to_right.wait_recv()
     half_right = remote(block(left, 0, mid), block(left, 0, mid), kv_send.at[3], kv_recv.at[3], right)
@@ -143,27 +165,7 @@
     half_left.start()
     sib_right = remote(block(right), block(right), kv_send.at[6], kv_recv.at[6], sib)
     sib_right.start()
-
-    depth = wide_v.shape[1] // 8
-    groups = wide_v.shape[0]
-    width = wide_v.shape[2]
-    for t, out in enumerate((wk_out, wv_out)):
-        arrive(kchunks + nq + t)
-
-        def relayout(i, _, t=t):
-            base = pl.multiple_of(i * depth, depth)
-            for g in range(groups):
-                wide_v[g] = wu_v[t, pl.ds(base, depth), g * 8:(g + 1) * 8, :].astype(F32).reshape(depth * 8, width)
-            for g in range(groups):
-                for h in range(8):
-                    col = (g * 8 + h) * width
-                    wo_v[t, pl.ds(base, depth), col:col + width] = wide_v[g, pl.ds(h, depth, stride=8), :].astype(BF16)
-            return _
-
-        lax.fori_loop(0, wu_v.shape[1] // depth, relayout, 0)
-        own.append(pltpu.make_async_copy(wo_v.at[t], out, own_sem.at[3 + t]))
-        own[-1].start()
-
+    up_relayout(1, wv_out)
     half_right.wait_recv()
     half_left.wait_recv()
     sib_across = remote(block(across), block(across), kv_send.at[7], kv_recv.at[7], sib)
@@ -184,7 +186,7 @@
     chip = me // 2
     give = jnp.maximum(chip - chips // 2 + 1, 0)
     take = jnp.maximum(chips // 2 - chip, 0)
-    lead = jnp.where(take > 0, steps // 2 + 2 * (take - 1), steps - give)
+    lead = jnp.where(take > 0, steps // 2 + take - 1, steps - give)
     return chip, lead, take, give
 
 

time: 130 us -> 129 us (level)
  no operation moved by 1% of the time
where the time goes in v8:
time: 129 us
  Pallas kernels  121 us (94%)
  local copies, waits for them, and re-layouts  5.3 us (4%)
  other arithmetic  2.16 us (2%)
    pallas_call x1, Pallas kernels, local_step(): pl.pallas_call(functools.partial(attn_kernel, attn_scale * math.log2(math...  63.6 us
    pallas_call x1, Pallas kernels, local_step(): pl.pallas_call(out_kernel, out_shape=jax.ShapeDtypeStruct((rows, model),...  33.2 us
    pallas_call x1, Pallas kernels, local_step(): pl.pallas_call(functools.partial(front_kernel, ranks, mine), out_shape=(j...  23.8 us
    unnamed x7, local copies, waits for them, and re-layouts  5.3 us

profile of v8, /device:TPU:119, one launch (start us, length us, event | category | flops | bytes accessed | tf_op | source)
XLA Modules:
  0.0 128.7 jit_solution(1297274315110612091)
XLA Ops:
  0.6 0.7 convert_element_type.3
  1.3 1.5 %multiply_sine_fusion = (f32[32,256]{1,0:T(8,128)}, f32[32,256]{1,0:T(8,128)}) fusion(f32[256]{0:T(256)S(1)} %convert_element_type.3, f32[32]{0:T(128)} %constant.2.clone), kind=kLoop, calls=%fused_computation | loop fusion | flops 8192 | bytes 66688 | tf_op jit(solution)/shard_map/sin | solution.py:567
  2.8 23.8 %shard_map.130 = (bf16[2048,640]{1,0:T(8,128)(2,1)}, bf16[512,1536]{1,0:T(8,128)(2,1)}, f32[2,64,256]{2,1,0:T(8,128)}, bf16[512,4096]{1,0:T(8,128)(2,1)}, bf16[512,4096]{1,0:T(8,128)(2,1)}) custom-call(bf16[256,6144]{1,0:T(8,128)(2,1)} %x_hbm.1, bf16[576,6144]{1,0:T(8,128)(2,1)} %bitcast.5, bf16[6144,1536]{1,0:T(8,128)(2,1)} %wq_hbm.1, ...), custom_call_target="tpu_custom_call" | custom-call | flops 6643777536 | bytes 25952256 | tf_op jit(solution)/shard_map/pallas_call | solution.py:574
  26.6 63.6 %shard_map.131 = (bf16[512,2048]{1,0:T(8,128)(2,1)}, bf16[512,2048]{1,0:T(8,128)(2,1)}, bf16[256,512]{1,0:T(8,128)(2,1)}, bf16[256,64]{1,0:T(8,128)(2,1)}) custom-call(bf16[512,1536]{1,0:T(8,128)(2,1)} %get-tuple-element.12.cq_hbm, bf16[2048,640]{1,0:T(8,128)(2,1)} %get-tuple-element.13.kv_ref, f32[2,64,256]{2,1,0:T(8,128)} %get-tuple-element.14.tab_ref, ...), custom_call_target="tpu_custom_call" | custom-call | tf_op jit(solution)/shard_map/pallas_call | solution.py:628
  90.2 0.0 copy-start.1
  90.3 33.2 %shard_map.132 = bf16[256,6144]{1,0:T(8,128)(2,1)} custom-call(bf16[512,2048]{1,0:T(8,128)(2,1)} %get-tuple-element.17.oa_hbm, bf16[512,2048]{1,0:T(8,128)(2,1)} %get-tuple-element.18.ob_hbm, bf16[8192,6144]{1,0:T(8,128)(2,1)} %bitcast.2.wo_hbm), custom_call_target="tpu_custom_call" | custom-call | tf_op jit(solution)/shard_map/pallas_call | solution.py:652
  123.4 0.0 copy-done.1
  123.4 0.0 copy-start
  123.4 0.7 copy.14
  124.1 3.9 %copy.17 = bf16[256,6144]{1,0:T(8,128)(2,1)} copy(bf16[256,6144]{1,0:T(8,128)(2,1)} %shard_map.132) | data formatting | bytes 6291456
  128.0 0.0 copy-done
  128.0 0.7 copy.18
Async XLA Ops:
  90.2 33.2 %copy-start.1 = (bf16[256,64]{1,0:T(8,128)(2,1)S(1)}, bf16[256,64]{1,0:T(8,128)(2,1)}, u32[]{:S(2)}) copy-start(bf16[256,64]{1,0:T(8,128)(2,1)} %get-tuple-element.23) | copy-start | bytes 98308
  123.4 4.6 %copy-start = (bf16[256,512]{1,0:T(8,128)(2,1)S(1)}, bf16[256,512]{1,0:T(8,128)(2,1)}, u32[]{:S(2)}) copy-start(bf16[256,512]{1,0:T(8,128)(2,1)} %get-tuple-element.30) | copy-start | bytes 786436

commit v9 on v8

--- a/solution.py
+++ b/solution.py
@@ -36,7 +36,7 @@
     return jnp.asarray(freq_list, dtype=jnp.float32)
 
 
-def front_kernel(ranks, heads, x_hbm, wkv_hbm, wq_hbm, wuk_hbm, wuv_hbm, gq_ref, gkv_ref, cos_ref, sin_ref,
+def front_kernel(ranks, heads, x_hbm, wkv_hbm, wq_hbm, wuk_hbm, wuv_hbm, gq_ref, gkv_ref, pos_ref, freq_ref,
                  kv_all, cq_all, tab_all, wk_out, wv_out,
                  x_v, wkv_v, wq_v, wu_v, wo_v, wide_v, cq_f, kv_v, cq_v, tab_v,
                  w_sem, own_sem, kv_send, kv_recv, pair_send, pair_recv):
@@ -44,7 +44,7 @@
     core = lax.rem(me, 2)
     sib = me + 1 - 2 * core
     rows = x_v.shape[0]
-    half = cos_ref.shape[0]
+    half = freq_ref.shape[0]
     kv_rank = gkv_ref.shape[0]
     right = lax.rem(me + 2, ranks)
     left = lax.rem(me + ranks - 2, ranks)
@@ -82,8 +82,8 @@
     for peer in (sib, right, left):
         pl.semaphore_signal(barrier, inc=1, device_id={"sp": peer}, device_id_type=MESH)
 
-    def block(idx, start=0, size=None):
-        return kv_all.at[pl.ds(idx * rows + start, size or rows)]
+    def block(idx):
+        return kv_all.at[pl.ds(idx * rows, rows)]
 
     def remote(src, dst, send, recv, dev):
         return pltpu.make_async_remote_copy(src_ref=src, dst_ref=dst, send_sem=send, recv_sem=recv,
@@ -97,8 +97,9 @@
     a = acc[:, :kv_rank]
     inv = lax.rsqrt(jnp.mean(a * a, axis=-1, keepdims=True) + NORM_EPS)
     ckv = (a * inv * gkv_ref[...][None, :]).astype(BF16)
-    tab_v[:half, :] = cos_ref[...]
-    tab_v[half:, :] = sin_ref[...]
+    angles = freq_ref[...] * pos_ref[...].astype(F32)[None, :]
+    tab_v[:half, :] = jnp.cos(angles)
+    tab_v[half:, :] = jnp.sin(angles)
     tab = tab_v[...].T
     cos_t, sin_t = tab[:, :half], tab[:, half:]
     z1 = acc[:, kv_rank:kv_rank + half]
@@ -108,11 +109,19 @@
     kv_v[:, kv_rank:] = jnp.concatenate([pe, jnp.zeros((rows, kv_v.shape[1] - kv_rank - 2 * half), BF16)], axis=-1)
 
     pl.semaphore_wait(barrier, 3)
+    mid = rows // 2
+
+    def piece(h):
+        return pl.ds(h * mid, mid)
+
+    def part(idx, h):
+        return kv_all.at[pl.ds(idx * rows + h * mid, mid)]
+
     to_sib = remote(kv_v, block(me), kv_send.at[0], kv_recv.at[0], sib)
-    to_right = remote(kv_v, block(me), kv_send.at[1], kv_recv.at[1], right)
-    to_left = remote(kv_v, block(me), kv_send.at[2], kv_recv.at[2], left)
+    to_right = [remote(kv_v.at[piece(h)], part(me, h), kv_send.at[1 + h], kv_recv.at[1 + h], right) for h in range(2)]
+    to_left = [remote(kv_v.at[piece(h)], part(me, h), kv_send.at[3 + h], kv_recv.at[3 + h], left) for h in range(2)]
     tab_copy = remote(tab_v, tab_all.at[core], pair_send.at[0], pair_recv.at[0], sib)
-    for c in (to_right, to_left, to_sib, tab_copy):
+    for c in (to_right[0], to_left[1], to_right[1], to_left[0], to_sib, tab_copy):
         c.start()
     own = [pltpu.make_async_copy(kv_v, block(me), own_sem.at[0]),
            pltpu.make_async_copy(tab_v, tab_all.at[core], own_sem.at[1])]
@@ -132,6 +141,13 @@
     own.append(pltpu.make_async_copy(cq_v, cq_all.at[pl.ds(core * rows, rows)], own_sem.at[2]))
     own[-1].start()
 
+    to_right[0].wait_recv()
+    half_right = remote(part(left, 0), part(left, 0), kv_send.at[5], kv_recv.at[5], right)
+    half_right.start()
+    to_left[1].wait_recv()
+    half_left = remote(part(right, 1), part(right, 1), kv_send.at[6], kv_recv.at[6], left)
+    half_left.start()
+
     depth = wide_v.shape[1] // 8
     groups = wide_v.shape[0]
     width = wide_v.shape[2]
@@ -154,28 +170,23 @@
         own[-1].start()
 
     up_relayout(0, wk_out)
-    mid = rows // 2
-    to_right.wait_recv()
-    half_right = remote(block(left, 0, mid), block(left, 0, mid), kv_send.at[3], kv_recv.at[3], right)
-    half_right.start()
-    sib_left = remote(block(left), block(left), kv_send.at[5], kv_recv.at[5], sib)
+    to_right[1].wait_recv()
+    sib_left = remote(block(left), block(left), kv_send.at[7], kv_recv.at[7], sib)
     sib_left.start()
-    to_left.wait_recv()
-    half_left = remote(block(right, mid, mid), block(right, mid, mid), kv_send.at[4], kv_recv.at[4], left)
-    half_left.start()
-    sib_right = remote(block(right), block(right), kv_send.at[6], kv_recv.at[6], sib)
+    to_left[0].wait_recv()
+    sib_right = remote(block(right), block(right), kv_send.at[8], kv_recv.at[8], sib)
     sib_right.start()
     up_relayout(1, wv_out)
     half_right.wait_recv()
+    sib_across0 = remote(part(across, 0), part(across, 0), kv_send.at[9], kv_recv.at[9], sib)
+    sib_across0.start()
     half_left.wait_recv()
-    sib_across = remote(block(across), block(across), kv_send.at[7], kv_recv.at[7], sib)
-    sib_across.start()
+    sib_across1 = remote(part(across, 1), part(across, 1), kv_send.at[10], kv_recv.at[10], sib)
+    sib_across1.start()
     to_sib.wait()
-    to_right.wait_send()
-    to_left.wait_send()
-    half_right.wait_send()
-    half_left.wait_send()
-    for c in (sib_left, sib_right, sib_across, tab_copy, cq_copy):
+    for c in to_right + to_left + [half_right, half_left]:
+        c.wait_send()
+    for c in (sib_left, sib_right, sib_across0, sib_across1, tab_copy, cq_copy):
         c.wait()
     for c in own:
         c.wait()
@@ -457,7 +468,7 @@
 
 
 def out_kernel(oa_hbm, ob_hbm, wo_hbm, out_hbm, own_v, sib_v, w_v, acc_v, out_v,
-               o_sem, w_sem, out_sem, swap_send, swap_recv, res_send, res_recv):
+               o_sem, lead_sem, w_sem, out_sem, swap_send, swap_recv, res_send, res_recv):
     me = lax.axis_index("sp")
     core = lax.rem(me, 2)
     sib = me + 1 - 2 * core
@@ -478,22 +489,30 @@
 
     own = [pltpu.make_async_copy(h, own_v.at[:, pl.ds(k * wide, wide)], o_sem.at[k])
            for k, h in enumerate((oa_hbm, ob_hbm))]
-    fetch(0).start()
-    for c in own:
-        c.start()
-    fetch(1).start()
+    lead = [pltpu.make_async_copy(
+        wo_hbm.at[pl.ds(pl.multiple_of(core * span + k * wide, wide), wide), pl.ds(pl.multiple_of(core * (steps * nc), nc), nc)],
+        w_v.at[0, pl.ds(k * wide, wide)], lead_sem.at[k]) for k in range(2)]
+    for k in range(2):
+        own[k].start()
+        lead[k].start()
 
     barrier = pltpu.get_barrier_semaphore()
     pl.semaphore_signal(barrier, inc=1, device_id={"sp": sib}, device_id_type=MESH)
-    pl.semaphore_wait(barrier, 1)
     swap = [pltpu.make_async_remote_copy(
         src_ref=h, dst_ref=sib_v.at[:, pl.ds(k * wide, wide)],
         send_sem=swap_send.at[k], recv_sem=swap_recv.at[k], device_id={"sp": sib}, device_id_type=MESH)
         for k, h in enumerate((oa_hbm, ob_hbm))]
-    for c in own:
-        c.wait()
+    own[0].wait()
+    lead[0].wait()
+    fetch(1).start()
+    acc_v[0] = jnp.dot(own_v[:, :wide], w_v[0, :wide, :], preferred_element_type=F32)
+    own[1].wait()
+    lead[1].wait()
+    fetch(2).start()
+    pl.semaphore_wait(barrier, 1)
     for c in swap:
         c.start()
+    acc_v[0] += jnp.dot(own_v[:, wide:], w_v[0, wide:, :], preferred_element_type=F32)
 
     def own_half(i, carry):
         fetch(i).wait()
@@ -501,7 +520,7 @@
         acc_v[i] = jnp.dot(own_v[...], w_v[lax.rem(i, bufs)], preferred_element_type=F32)
         return carry
 
-    lax.fori_loop(0, steps, own_half, 0)
+    lax.fori_loop(1, steps, own_half, 0)
     for c in swap:
         c.wait()
 
@@ -563,9 +582,6 @@
         mine = num_heads // 2
         pe_w = 128
         attn_scale = (0.1 * math.log(YARN_FACTOR) + 1.0) ** 2 / math.sqrt(qk_dim)
-        angles = rope_freqs(rot)[:, None] * tok_pos.astype(F32)[None, :]
-        cos_t, sin_t = jnp.cos(angles), jnp.sin(angles)
-
         kchunks, nq, depth = 4, 3, 64
         kv_w = kv_rank + pe_w
         any_spec = pl.BlockSpec(memory_space=pl.ANY)
@@ -595,14 +611,14 @@
                 pltpu.VMEM((rot, rows), F32),
                 dma((2 * kchunks + nq + 2,)),
                 dma((5,)),
-                dma((8,)),
-                dma((8,)),
+                dma((11,)),
+                dma((11,)),
                 dma((2,)),
                 dma((2,)),
             ],
             compiler_params=pltpu.CompilerParams(collective_id=0, has_side_effects=True, vmem_limit_bytes=60 << 20),
             cost_estimate=pl.CostEstimate(flops=2 * rows * model * (q_rank + kv_rank + rot), bytes_accessed=2 * model * (q_rank + kv_rank + rot), transcendentals=0),
-        )(tok_in, w_dkv.T, w_dq, w_uk, w_uv, g_q, g_kv, cos_t, sin_t)
+        )(tok_in, w_dkv.T, w_dq, w_uk, w_uv, g_q, g_kv, tok_pos, rope_freqs(rot)[:, None])
 
         wuq_t = jnp.transpose(w_uq, (1, 2, 0))
         qn = 2 * rows
@@ -661,6 +677,7 @@
                 pltpu.VMEM((pieces, qn, nc), F32),
                 pltpu.VMEM((2, qn, nc), BF16),
                 dma((2,)),
+                dma((2,)),
                 dma((bufs,)),
                 dma((2,)),
                 dma((2,)),

time: 129 us -> 124 us (0.961)
  Pallas kernels: 121 us -> 118 us
  other arithmetic: 2.16 us -> 0 us
    pallas_call x1, Pallas kernels: 23.8 us -> 21.1 us  [local_step(): pl.pallas_call(functools.partial(front_kernel, ranks, mine), out_shape=(j...]
    sin x1 -> x0, other arithmetic: 1.48 us -> none  [local_step(): cos_t, sin_t = (jnp.cos(angles), jnp.sin(angles))]
where the time goes in v9:
time: 124 us
  Pallas kernels  118 us (95%)
  local copies, waits for them, and re-layouts  5.3 us (4%)
    pallas_call x1, Pallas kernels, local_step(): pl.pallas_call(functools.partial(attn_kernel, attn_scale * math.log2(math...  64.4 us
    pallas_call x1, Pallas kernels, local_step(): pl.pallas_call(out_kernel, out_shape=jax.ShapeDtypeStruct((rows, model),...  32.6 us
    pallas_call x1, Pallas kernels, local_step(): pl.pallas_call(functools.partial(front_kernel, ranks, mine), out_shape=(j...  21.1 us
    unnamed x7, local copies, waits for them, and re-layouts  5.3 us

profile of v9, /device:TPU:119, one launch (start us, length us, event | category | flops | bytes accessed | tf_op | source)
XLA Modules:
  0.0 124.1 jit_solution(3097731688664341892)
XLA Ops:
  0.6 21.1 %shard_map.130 = (bf16[2048,640]{1,0:T(8,128)(2,1)}, bf16[512,1536]{1,0:T(8,128)(2,1)}, f32[2,64,256]{2,1,0:T(8,128)}, bf16[512,4096]{1,0:T(8,128)(2,1)}, bf16[512,4096]{1,0:T(8,128)(2,1)}) custom-call(bf16[256,6144]{1,0:T(8,128)(2,1)} %x_hbm.1, bf16[576,6144]{1,0:T(8,128)(2,1)} %bitcast.5, bf16[6144,1536]{1,0:T(8,128)(2,1)} %wq_hbm.1, ...), custom_call_target="tpu_custom_call" | custom-call | flops 6643777536 | bytes 25952256 | tf_op jit(solution)/shard_map/pallas_call | solution.py:590
  21.7 64.4 %shard_map.131 = (bf16[512,2048]{1,0:T(8,128)(2,1)}, bf16[512,2048]{1,0:T(8,128)(2,1)}, bf16[256,512]{1,0:T(8,128)(2,1)}, bf16[256,64]{1,0:T(8,128)(2,1)}) custom-call(bf16[512,1536]{1,0:T(8,128)(2,1)} %get-tuple-element.12.cq_hbm, bf16[2048,640]{1,0:T(8,128)(2,1)} %get-tuple-element.13.kv_ref, f32[2,64,256]{2,1,0:T(8,128)} %get-tuple-element.14.tab_ref, ...), custom_call_target="tpu_custom_call" | custom-call | tf_op jit(solution)/shard_map/pallas_call | solution.py:644
  86.2 0.0 copy-start.1
  86.2 32.6 %shard_map.132 = bf16[256,6144]{1,0:T(8,128)(2,1)} custom-call(bf16[512,2048]{1,0:T(8,128)(2,1)} %get-tuple-element.17.oa_hbm, bf16[512,2048]{1,0:T(8,128)(2,1)} %get-tuple-element.18.ob_hbm, bf16[8192,6144]{1,0:T(8,128)(2,1)} %bitcast.2.wo_hbm), custom_call_target="tpu_custom_call" | custom-call | tf_op jit(solution)/shard_map/pallas_call | solution.py:668
  118.8 0.0 copy-done.1
  118.8 0.0 copy-start
  118.8 0.7 copy.14
  119.5 3.9 %copy.17 = bf16[256,6144]{1,0:T(8,128)(2,1)} copy(bf16[256,6144]{1,0:T(8,128)(2,1)} %shard_map.132) | data formatting | bytes 6291456
  123.4 0.0 copy-done
  123.4 0.7 copy.18
Async XLA Ops:
  86.2 32.7 %copy-start.1 = (bf16[256,64]{1,0:T(8,128)(2,1)S(1)}, bf16[256,64]{1,0:T(8,128)(2,1)}, u32[]{:S(2)}) copy-start(bf16[256,64]{1,0:T(8,128)(2,1)} %get-tuple-element.23) | copy-start | bytes 98308
  118.8 4.6 %copy-start = (bf16[256,512]{1,0:T(8,128)(2,1)S(1)}, bf16[256,512]{1,0:T(8,128)(2,1)}, u32[]{:S(2)}) copy-start(bf16[256,512]{1,0:T(8,128)(2,1)} %get-tuple-element.28) | copy-start | bytes 786436

commit v10 on v9

--- a/solution.py
+++ b/solution.py
@@ -208,10 +208,10 @@
     return jnp.where((i <= lead) | (take == 0), jnp.minimum(i, lead - 1), late)
 
 
-def attn_kernel(scale2, ranks, steps, cq_hbm, kv_ref, tab_ref,
-                wqa_ref, wqb_ref, wka_ref, wkb_ref, wva_ref, wvb_ref, oa_hbm, ob_hbm, ckv_ref, cpe_ref,
+def attn_kernel(scale2, ranks, steps, cq_ref, kv_ref, tab_ref,
+                wqa_ref, wqb_ref, wka_ref, wkb_ref, wva_ref, wvb_ref, oa_hbm, ob_hbm,
                 cq_v, tab_v, k_v, v_a, v_b, q_v, s_a, s_b, m_a, m_b, l_a, l_b, o_a, o_b, cosq_ref, sinq_ref, oa_v, ob_v,
-                cq_sem, lat_send, lat_recv, fwd_send, fwd_recv, o_sem, oa_send, ob_send, oa_recv, ob_recv):
+                lat_send, lat_recv, fwd_send, fwd_recv, o_sem, oa_send, ob_send, oa_recv, ob_recv):
     step = pl.program_id(0)
     final = pl.num_programs(0) - 1
     me = lax.axis_index("sp")
@@ -236,7 +236,7 @@
 
     lat = [pltpu.make_async_remote_copy(src_ref=src, dst_ref=dst, send_sem=lat_send.at[k], recv_sem=lat_recv.at[k],
                                         device_id={"sp": far}, device_id_type=MESH)
-           for k, (src, dst) in enumerate(((cq_hbm.at[my_rows], cq_v.at[1, my_rows]), (tab_ref.at[core], tab_v.at[core])))]
+           for k, (src, dst) in enumerate(((cq_ref.at[my_rows], cq_v.at[1, my_rows]), (tab_ref.at[core], tab_v.at[core])))]
     fwd = [pltpu.make_async_remote_copy(src_ref=ref, dst_ref=ref, send_sem=fwd_send.at[k], recv_sem=fwd_recv.at[k],
                                         device_id={"sp": sib}, device_id_type=MESH)
            for k, ref in enumerate((cq_v.at[1, my_rows], tab_v.at[core]))]
@@ -279,8 +279,6 @@
 
     @pl.when(step == 0)
     def _():
-        own_cq = pltpu.make_async_copy(cq_hbm, cq_v.at[0], cq_sem.at[0])
-        own_cq.start()
         barrier = pltpu.get_barrier_semaphore()
         for peer in (sib, far):
             pl.semaphore_signal(barrier, inc=1, device_id={"sp": peer}, device_id_type=MESH)
@@ -299,11 +297,7 @@
         for c in range(2):
             cosq_ref[0, :, c * sub:(c + 1) * sub] = tab_ref[c, :half, :]
             sinq_ref[0, :, c * sub:(c + 1) * sub] = tab_ref[c, half:, :]
-        rows = ckv_ref.shape[0]
-        own = kv_ref[pl.ds(pl.multiple_of(me * rows, rows), rows), :]
-        ckv_ref[...] = own[:, :kv_rank]
-        cpe_ref[...] = own[:, kv_rank:kv_rank + rot]
-        own_cq.wait()
+        cq_v[0] = cq_ref[...]
 
     @pl.when(step > 0)
     def _():
@@ -560,6 +554,29 @@
         give.wait_send()
     for n in range(steps):
         store(n)[1].wait_recv()
+
+
+def result_kernel(res_hbm, kv_hbm, out_hbm, ckv_hbm, pe_hbm, res_v, kv_v, pe_v, in_sem, out_sem):
+    me = lax.axis_index("sp")
+    chunks, rows, width = res_v.shape
+    kv_rank = ckv_hbm.shape[1]
+    rot = pe_hbm.shape[0]
+    take = [pltpu.make_async_copy(kv_hbm.at[pl.ds(pl.multiple_of(me * rows, rows), rows)], kv_v, in_sem.at[chunks])]
+    take += [pltpu.make_async_copy(res_hbm.at[:, pl.ds(c * width, width)], res_v.at[c], in_sem.at[c]) for c in range(chunks)]
+    for c in take:
+        c.start()
+    take[0].wait()
+    pe_v[...] = kv_v[:, kv_rank:].astype(F32).T[:rot].astype(BF16)
+    give = [pltpu.make_async_copy(kv_v.at[:, pl.ds(0, kv_rank)], ckv_hbm, out_sem.at[chunks]),
+            pltpu.make_async_copy(pe_v, pe_hbm, out_sem.at[chunks + 1])]
+    for c in give:
+        c.start()
+    for c in range(chunks):
+        take[1 + c].wait()
+        give.append(pltpu.make_async_copy(res_v.at[c], out_hbm.at[:, pl.ds(c * width, width)], out_sem.at[c]))
+        give[-1].start()
+    for c in give:
+        c.wait()
 
 
 def solution(mesh):
@@ -641,31 +658,28 @@
         rope_v = pltpu.VMEM((2, half, qn), F32)
         most = ranks // 4
         pair_o = pltpu.VMEM((most + 1, qn, 2 * v_dim), BF16)
-        o_a, o_b, cache_kv, cache_pe = pl.pallas_call(
+        o_a, o_b = pl.pallas_call(
             functools.partial(attn_kernel, attn_scale * math.log2(math.e), ranks, steps),
-            out_shape=(jax.ShapeDtypeStruct((qn, 2 * steps * v_dim), BF16),) * 2 + (
-                jax.ShapeDtypeStruct((rows, kv_rank), BF16),
-                jax.ShapeDtypeStruct((rows, rot), BF16),
-            ),
+            out_shape=(jax.ShapeDtypeStruct((qn, 2 * steps * v_dim), BF16),) * 2,
             grid=(steps + most + 3,),
             in_specs=[
-                any_spec,
+                whole((qn, q_rank)),
                 whole((seq, kv_w)),
                 whole((2, rot, rows)),
                 up_spec(0), up_spec(1), lat_spec(0), lat_spec(1), lat_spec(0), lat_spec(1),
             ],
-            out_specs=(any_spec, any_spec, whole((rows, kv_rank)), whole((rows, rot))),
+            out_specs=(any_spec, any_spec),
             scratch_shapes=[pltpu.VMEM((2, qn, q_rank), BF16), pltpu.VMEM((2, rot, rows), F32),
                             pltpu.VMEM((2, nblk, qn, nope + pe_w), BF16), head_v, head_v, pltpu.VMEM((2, nope + pe_w, qn), BF16),
                             scores, scores, stat, stat, stat, stat, head_o, head_o, rope_v, rope_v, pair_o, pair_o,
-                            dma((1,)), dma((2,)), dma((2,)), dma((2,)), dma((2,)), dma((2,)), dma((most,)), dma((most,)), dma((most,)), dma((most,))],
+                            dma((2,)), dma((2,)), dma((2,)), dma((2,)), dma((2,)), dma((most,)), dma((most,)), dma((most,)), dma((most,))],
             compiler_params=pltpu.CompilerParams(dimension_semantics=("arbitrary",), collective_id=2, has_side_effects=True, vmem_limit_bytes=62 << 20),
         )(cq_all, kv_all, tab_all, wuq_t, wuq_t, wk2, wk2, wv2, wv2)
 
         nc, bufs = 512, 3
         span = mine * v_dim
         pieces = model // 2 // nc
-        attn_out = pl.pallas_call(
+        res = pl.pallas_call(
             out_kernel,
             out_shape=jax.ShapeDtypeStruct((rows, model), BF16),
             in_specs=[any_spec] * 3,
@@ -687,7 +701,26 @@
             ],
             compiler_params=pltpu.CompilerParams(collective_id=1, has_side_effects=True, vmem_limit_bytes=60 << 20),
         )(o_a, o_b, w_o.reshape(num_heads * v_dim, model))
-        return attn_out, cache_kv, cache_pe
+        chunks = 8
+        attn_out, cache_kv, pe_t = pl.pallas_call(
+            result_kernel,
+            out_shape=(
+                jax.ShapeDtypeStruct((rows, model), BF16),
+                jax.ShapeDtypeStruct((rows, kv_rank), BF16),
+                jax.ShapeDtypeStruct((rot, rows), BF16),
+            ),
+            in_specs=[any_spec] * 2,
+            out_specs=(any_spec,) * 3,
+            scratch_shapes=[
+                pltpu.VMEM((chunks, rows, model // chunks), BF16),
+                pltpu.VMEM((rows, kv_w), BF16),
+                pltpu.VMEM((rot, rows), BF16),
+                dma((chunks + 1,)),
+                dma((chunks + 2,)),
+            ],
+            compiler_params=pltpu.CompilerParams(vmem_limit_bytes=62 << 20),
+        )(res, kv_all)
+        return attn_out, cache_kv, pe_t.T
 
     return jax.shard_map(local_step, mesh=mesh,
                          in_specs=(rows_spec, tok_spec) + (replicated,) * 8,

time: 124 us -> 122 us (0.984)
  local copies, waits for them, and re-layouts: 5.3 us -> 0 us
  Pallas kernels: 118 us -> 121 us
    unnamed x7 -> x0, local copies, waits for them, and re-layouts: 5.3 us -> none
    pallas_call x0 -> x1, Pallas kernels: none -> 3.03 us  [local_step(): pl.pallas_call(result_kernel, out_shape=(jax.ShapeDtypeStruct((rows, mode...]
where the time goes in v10:
time: 122 us
  Pallas kernels  121 us (99%)
    pallas_call x1, Pallas kernels, local_step(): pl.pallas_call(functools.partial(attn_kernel, attn_scale * math.log2(math...  64.3 us
    pallas_call x1, Pallas kernels, local_step(): pl.pallas_call(out_kernel, out_shape=jax.ShapeDtypeStruct((rows, model),...  32.6 us
    pallas_call x1, Pallas kernels, local_step(): pl.pallas_call(functools.partial(front_kernel, ranks, mine), out_shape=(j...  21.1 us
    pallas_call x1, Pallas kernels, local_step(): pl.pallas_call(result_kernel, out_shape=(jax.ShapeDtypeStruct((rows, mode...  3.03 us

profile of v10, /device:TPU:119, one launch (start us, length us, event | category | flops | bytes accessed | tf_op | source)
XLA Modules:
  0.0 121.7 jit_solution(5027092413214345317)
XLA Ops:
  0.6 21.1 %shard_map.130 = (bf16[2048,640]{1,0:T(8,128)(2,1)}, bf16[512,1536]{1,0:T(8,128)(2,1)}, f32[2,64,256]{2,1,0:T(8,128)}, bf16[512,4096]{1,0:T(8,128)(2,1)}, bf16[512,4096]{1,0:T(8,128)(2,1)}) custom-call(bf16[256,6144]{1,0:T(8,128)(2,1)} %x_hbm.1, bf16[576,6144]{1,0:T(8,128)(2,1)} %bitcast.6, bf16[6144,1536]{1,0:T(8,128)(2,1)} %wq_hbm.1, ...), custom_call_target="tpu_custom_call" | custom-call | flops 6643777536 | bytes 25952256 | tf_op jit(solution)/shard_map/pallas_call | solution.py:607
  21.7 64.3 %shard_map.131 = (bf16[512,2048]{1,0:T(8,128)(2,1)}, bf16[512,2048]{1,0:T(8,128)(2,1)}) custom-call(bf16[512,1536]{1,0:T(8,128)(2,1)} %get-tuple-element.13.cq_ref, bf16[2048,640]{1,0:T(8,128)(2,1)} %get-tuple-element.14.kv_ref.kv_hbm, f32[2,64,256]{2,1,0:T(8,128)} %get-tuple-element.15.tab_ref, bf16[64,192,1536]{2,1,0:T(8,128)(2,1)} %bitcast.4, ...), custom_call_target="tpu_custom_call" | custom-call | tf_op jit(solution)/shard_map/pallas_call | solution.py:661
  86.0 32.6 %shard_map.132.res_hbm = bf16[256,6144]{1,0:T(8,128)(2,1)} custom-call(bf16[512,2048]{1,0:T(8,128)(2,1)} %get-tuple-element.18.oa_hbm, bf16[512,2048]{1,0:T(8,128)(2,1)} %get-tuple-element.19.ob_hbm, bf16[8192,6144]{1,0:T(8,128)(2,1)} %bitcast.2.wo_hbm), custom_call_target="tpu_custom_call" | custom-call | tf_op jit(solution)/shard_map/pallas_call | solution.py:682
  118.6 3.0 %shard_map.133 = (bf16[256,6144]{1,0:T(8,128)(2,1)}, bf16[256,512]{1,0:T(8,128)(2,1)}, bf16[64,256]{1,0:T(8,128)(2,1)}) custom-call(bf16[256,6144]{1,0:T(8,128)(2,1)} %shard_map.132.res_hbm, bf16[2048,640]{1,0:T(8,128)(2,1)} %get-tuple-element.14.kv_ref.kv_hbm), custom_call_target="tpu_custom_call" | custom-call | tf_op jit(solution)/shard_map/pallas_call | solution.py:705

commit v11 on v10

--- a/solution.py
+++ b/solution.py
@@ -282,13 +282,6 @@
         barrier = pltpu.get_barrier_semaphore()
         for peer in (sib, far):
             pl.semaphore_signal(barrier, inc=1, device_id={"sp": peer}, device_id_type=MESH)
-        pl.semaphore_wait(barrier, 2)
-
-        @pl.when(give > 0)
-        def _():
-            for c in lat:
-                c.start()
-
         for kb in range(blocks):
             pe = kv_ref[kb * blk:(kb + 1) * blk, kv_rank:]
             k_v[0, kb, :, nope:] = pe
@@ -298,6 +291,12 @@
             cosq_ref[0, :, c * sub:(c + 1) * sub] = tab_ref[c, :half, :]
             sinq_ref[0, :, c * sub:(c + 1) * sub] = tab_ref[c, half:, :]
         cq_v[0] = cq_ref[...]
+        pl.semaphore_wait(barrier, 2)
+
+        @pl.when(give > 0)
+        def _():
+            for c in lat:
+                c.start()
 
     @pl.when(step > 0)
     def _():

time: 122 us -> 122 us (level)
  no operation moved by 1% of the time
where the time goes in v11:
time: 122 us; the launch traced here: 121 us
  Pallas kernels  121 us (99%)
    pallas_call x1, Pallas kernels, local_step(): pl.pallas_call(functools.partial(attn_kernel, attn_scale * math.log2(math...  64 us
    pallas_call x1, Pallas kernels, local_step(): pl.pallas_call(out_kernel, out_shape=jax.ShapeDtypeStruct((rows, model),...  32.6 us
    pallas_call x1, Pallas kernels, local_step(): pl.pallas_call(functools.partial(front_kernel, ranks, mine), out_shape=(j...  21.1 us
    pallas_call x1, Pallas kernels, local_step(): pl.pallas_call(result_kernel, out_shape=(jax.ShapeDtypeStruct((rows, mode...  3.03 us

profile of v11, /device:TPU:119, one launch (start us, length us, event | category | flops | bytes accessed | tf_op | source)
XLA Modules:
  0.0 121.5 jit_solution(3569521533090036193)
XLA Ops:
  0.6 21.1 %shard_map.130 = (bf16[2048,640]{1,0:T(8,128)(2,1)}, bf16[512,1536]{1,0:T(8,128)(2,1)}, f32[2,64,256]{2,1,0:T(8,128)}, bf16[512,4096]{1,0:T(8,128)(2,1)}, bf16[512,4096]{1,0:T(8,128)(2,1)}) custom-call(bf16[256,6144]{1,0:T(8,128)(2,1)} %x_hbm.1, bf16[576,6144]{1,0:T(8,128)(2,1)} %bitcast.6, bf16[6144,1536]{1,0:T(8,128)(2,1)} %wq_hbm.1, ...), custom_call_target="tpu_custom_call" | custom-call | flops 6643777536 | bytes 25952256 | tf_op jit(solution)/shard_map/pallas_call | solution.py:606
  21.7 64.0 %shard_map.131 = (bf16[512,2048]{1,0:T(8,128)(2,1)}, bf16[512,2048]{1,0:T(8,128)(2,1)}) custom-call(bf16[512,1536]{1,0:T(8,128)(2,1)} %get-tuple-element.13.cq_ref, bf16[2048,640]{1,0:T(8,128)(2,1)} %get-tuple-element.14.kv_ref.kv_hbm, f32[2,64,256]{2,1,0:T(8,128)} %get-tuple-element.15.tab_ref, bf16[64,192,1536]{2,1,0:T(8,128)(2,1)} %bitcast.4, ...), custom_call_target="tpu_custom_call" | custom-call | tf_op jit(solution)/shard_map/pallas_call | solution.py:660
  85.7 32.6 %shard_map.132.res_hbm = bf16[256,6144]{1,0:T(8,128)(2,1)} custom-call(bf16[512,2048]{1,0:T(8,128)(2,1)} %get-tuple-element.18.oa_hbm, bf16[512,2048]{1,0:T(8,128)(2,1)} %get-tuple-element.19.ob_hbm, bf16[8192,6144]{1,0:T(8,128)(2,1)} %bitcast.2.wo_hbm), custom_call_target="tpu_custom_call" | custom-call | tf_op jit(solution)/shard_map/pallas_call | solution.py:681
  118.3 3.0 %shard_map.133 = (bf16[256,6144]{1,0:T(8,128)(2,1)}, bf16[256,512]{1,0:T(8,128)(2,1)}, bf16[64,256]{1,0:T(8,128)(2,1)}) custom-call(bf16[256,6144]{1,0:T(8,128)(2,1)} %shard_map.132.res_hbm, bf16[2048,640]{1,0:T(8,128)(2,1)} %get-tuple-element.14.kv_ref.kv_hbm), custom_call_target="tpu_custom_call" | custom-call | tf_op jit(solution)/shard_map/pallas_call | solution.py:704
